TPU v7x, 8 devices: a whole 2x2x1 slice. The times are simulated.
8 devices in a mesh: data: 1 (over z), hid: 2 (over y), vocab: 4 (over x, core).
Axes of the slice: x: 2, y: 2, z: 1, core: 2. Of those that a mesh axis runs over, the one named last changes fastest.
Arguments:
- h_states: bfloat16 [1024, 5120], P('data', 'hid')
- w_head: bfloat16 [5120, 100352], P('hid', 'vocab')
- inv_temp: float32 [1024], P('data')
- tgt_ids: int32 [1024], P('data')
Outputs:
- output 1: float32 [1024, 100352], P('data', ('vocab', 'hid'))
- output 2: float32 [1024], P('data')
All inputs are finite; a program needn't handle non-finite values.
Results may differ from a plain program's by a relative error of at most 0.001.
Values are sent between devices in bfloat16 or wider.
A program may use at most 1 GiB of HBM per device.

v0:
```python
import functools

import jax
import jax.numpy as jnp
from jax import lax
from jax.experimental import pallas as pl
from jax.experimental.pallas import tpu as pltpu
from jax.sharding import PartitionSpec as P


CT = 256
SUB = 32
LAST_VMEM = 32 * 1024 * 1024
ALL_VMEM = 67043328


def mm_kernel(sel_ref, h_ref, w_ref, *refs, splits):
    out_refs = refs[len(refs) - len(splits):]
    res = jnp.dot(h_ref[...], w_ref[...], preferred_element_type=jnp.float32)
    at = 0
    for ref, rows in zip(out_refs, splits):
        ref[...] = res[at:at + rows]
        at += rows


def partial_products(h, w, half, row0, splits, tile0, ntiles, tn, half_tiles, deps=()):
    rows = sum(splits)
    depth = h.shape[1]
    cols = ntiles * tn
    return pl.pallas_call(
        functools.partial(mm_kernel, splits=splits),
        out_shape=[jax.ShapeDtypeStruct((r, cols), jnp.float32) for r in splits],
        grid_spec=pltpu.PrefetchScalarGridSpec(
            num_scalar_prefetch=1,
            grid=(ntiles,),
            in_specs=[
                pl.BlockSpec((rows, depth), lambda j, s: (row0 // rows, 0)),
                pl.BlockSpec((depth, tn), lambda j, s: (0, s[0] * half_tiles + tile0 + j)),
            ] + [pl.BlockSpec(memory_space=pl.ANY)] * len(deps),
            out_specs=[pl.BlockSpec((r, tn), lambda j, s: (0, j)) for r in splits],
        ),
        cost_estimate=pl.CostEstimate(
            flops=2 * rows * depth * cols, bytes_accessed=depth * cols * 2 + rows * cols * 4, transcendentals=0),
        compiler_params=pltpu.CompilerParams(dimension_semantics=("arbitrary",), vmem_limit_bytes=ALL_VMEM),
    )(half, h, w, *deps)


def local_kernel(temp_ref, tgt_ref, tri_ref, own_ref, *refs, npieces, ndeps):
    recv_refs = refs[:npieces]
    pre_ref, st_ref, z_s, hi_s, mid_s, lo_s = refs[npieces + ndeps:]
    rows = own_ref.shape[0]
    nt = own_ref.shape[1] // CT
    temp = jnp.broadcast_to(temp_ref[...], (rows, CT))
    mx = jnp.full((rows, CT), -jnp.inf, jnp.float32)
    t0 = 0
    for ref in recv_refs:
        n = ref.shape[1] // CT

        def max_step(j, mx, ref=ref, t0=t0):
            src = pl.ds(pl.multiple_of(j * CT, CT), CT)
            dst = pl.ds(pl.multiple_of((t0 + j) * CT, CT), CT)
            z = (own_ref[:, dst] + ref[:, src]) * temp
            z_s[t0 + j] = z
            return jnp.maximum(mx, z)

        mx = lax.fori_loop(0, n, max_step, mx, unroll=7)
        t0 += n
    m = jnp.max(mx, axis=1, keepdims=True)
    mb = jnp.broadcast_to(m, (rows, CT))
    tgt = jnp.broadcast_to(tgt_ref[...], (rows, CT))
    col = lax.broadcasted_iota(jnp.int32, (rows, CT), 1)
    rel = tgt - col

    def exp_step(j, carry):
        sacc, cacc = carry
        e = jnp.exp(z_s[j] - mb)
        hi = e.astype(jnp.bfloat16)
        r1 = e - hi.astype(jnp.float32)
        mid = r1.astype(jnp.bfloat16)
        lo = (r1 - mid.astype(jnp.float32)).astype(jnp.bfloat16)
        hi_s[j] = hi
        mid_s[j] = mid
        lo_s[j] = lo
        return sacc + e, cacc + jnp.where(rel >= j * CT, e, 0.0)

    zero = jnp.zeros((rows, CT), jnp.float32)
    sacc, cacc = lax.fori_loop(0, nt, exp_step, (zero, zero), unroll=7)
    s = jnp.sum(sacc, axis=1, keepdims=True)
    c = jnp.sum(cacc, axis=1, keepdims=True)
    lane = lax.broadcasted_iota(jnp.int32, (rows, 128), 1)
    st_ref[...] = jnp.where(lane == 0, m, jnp.where(lane == 1, s, jnp.where(lane == 2, c, 0.0)))

    tri = tri_ref[...]
    group = 7

    def prefix_step(g, carry):
        at = pl.ds(g * group, group)
        pre = jnp.dot(hi_s[at].reshape(group * rows, CT), tri, preferred_element_type=jnp.float32)
        pre += jnp.dot(mid_s[at].reshape(group * rows, CT), tri, preferred_element_type=jnp.float32)
        pre += jnp.dot(lo_s[at].reshape(group * rows, CT), tri, preferred_element_type=jnp.float32)
        for k in range(group):
            blk = pre[k * rows:(k + 1) * rows]
            dst = pl.ds(pl.multiple_of((g * group + k) * CT, CT), CT)
            pre_ref[:, dst] = blk + carry
            carry = carry + jnp.broadcast_to(blk[:, CT - 1:CT], (rows, CT))
        return carry

    lax.fori_loop(0, nt // group, prefix_step, zero)


def local_prefix(temp, tgt, tri, own, own_row0, recvs, rows, row0, deps=(), vmem=ALL_VMEM):
    cols = own.shape[1]
    nt = cols // CT
    sub = min(SUB, rows)
    return pl.pallas_call(
        functools.partial(local_kernel, npieces=len(recvs), ndeps=len(deps)),
        grid=(rows // sub,),
        out_shape=[jax.ShapeDtypeStruct((rows, cols), jnp.float32), jax.ShapeDtypeStruct((rows, 128), jnp.float32)],
        in_specs=[
            pl.BlockSpec((sub, 1), lambda i: (row0 // sub + i, 0)),
            pl.BlockSpec((sub, 1), lambda i: (row0 // sub + i, 0)),
            pl.BlockSpec((CT, CT), lambda i: (0, 0)),
            pl.BlockSpec((sub, cols), lambda i: (own_row0 // sub + i, 0)),
        ] + [pl.BlockSpec((sub, r.shape[1]), lambda i: (i, 0)) for r in recvs]
        + [pl.BlockSpec(memory_space=pl.ANY)] * len(deps),
        out_specs=[pl.BlockSpec((sub, cols), lambda i: (i, 0)), pl.BlockSpec((sub, 128), lambda i: (i, 0))],
        scratch_shapes=[
            pltpu.VMEM((nt, sub, CT), jnp.float32),
            pltpu.VMEM((nt, sub, CT), jnp.bfloat16),
            pltpu.VMEM((nt, sub, CT), jnp.bfloat16),
            pltpu.VMEM((nt, sub, CT), jnp.bfloat16),
        ],
        cost_estimate=pl.CostEstimate(
            flops=6 * rows * cols * CT, bytes_accessed=rows * cols * 12, transcendentals=rows * cols),
        compiler_params=pltpu.CompilerParams(dimension_semantics=("arbitrary",), vmem_limit_bytes=vmem),
    )(temp, tgt, tri, own, *recvs, *deps)


def final_kernel(pos_ref, pre_ref, mine_ref, other_ref, *refs):
    out_ref, ct_ref = refs[-2:]
    voc, hid = pos_ref[0], pos_ref[1]
    nv = mine_ref.shape[0]
    stats = [(v, mine_ref[v], True) for v in range(nv)] + [(v, other_ref[v], False) for v in range(nv)]
    top = functools.reduce(jnp.maximum, [st[:, 0:1] for _, st, _ in stats])
    total = below = at_tgt = scale = jnp.zeros_like(top)
    for v, st, same in stats:
        f = jnp.exp(st[:, 0:1] - top)
        s = st[:, 1:2] * f
        total += s
        at_tgt += st[:, 2:3] * f
        lower = (v < voc) if same else ((v < voc) | ((v == voc) & (hid == 1)))
        below += jnp.where(lower, s, 0.0)
        if same:
            scale = jnp.where(v == voc, f, scale)
    inv = 1.0 / total
    ct_ref[...] = jnp.broadcast_to(at_tgt * inv, ct_ref.shape)
    out_ref[...] = pre_ref[...] * (scale * inv) + below * inv


def last_kernel(pre_ref, ab_ref, *refs):
    out_ref = refs[-1]
    out_ref[...] = pre_ref[...] * ab_ref[:, 0:1] + ab_ref[:, 1:2]


def exchange_kernel(st_ref, ab_ref, slots, send_sem, recv_sem):
    voc = lax.axis_index("vocab")
    hid = lax.axis_index("hid")
    steps = [(dv, dh) for dv in range(4) for dh in range(2)][1:]
    barrier = pltpu.get_barrier_semaphore()
    for dv, dh in steps:
        pl.semaphore_signal(
            barrier, inc=1, device_id={"vocab": lax.rem(voc + dv, 4), "hid": lax.rem(hid + dh, 2)},
            device_id_type=pl.DeviceIdType.MESH)
    pl.semaphore_wait(barrier, len(steps))
    copies = []
    for i, (dv, dh) in enumerate(steps):
        copy = pltpu.make_async_remote_copy(
            src_ref=st_ref,
            dst_ref=slots.at[i],
            send_sem=send_sem.at[i],
            recv_sem=recv_sem.at[i],
            device_id={"vocab": lax.rem(voc + dv, 4), "hid": lax.rem(hid + dh, 2)},
            device_id_type=pl.DeviceIdType.MESH,
        )
        copy.start()
        copies.append(copy)
    for copy in copies:
        copy.wait()
    own = st_ref[...]
    top = own[:, 0:1]
    for i in range(len(steps)):
        top = jnp.maximum(top, slots[i][:, 0:1])
    scale = jnp.exp(own[:, 0:1] - top)
    total = own[:, 1:2] * scale
    at_tgt = own[:, 2:3] * scale
    below = jnp.zeros_like(top)
    for i, (dv, dh) in enumerate(steps):
        st = slots[i]
        f = jnp.exp(st[:, 0:1] - top)
        s = st[:, 1:2] * f
        total += s
        at_tgt += st[:, 2:3] * f
        first = lax.rem(voc + 4 - dv, 4) * 2 + lax.rem(hid + 2 - dh, 2)
        below += jnp.where(first < voc * 2 + hid, s, 0.0)
    inv = 1.0 / total
    lane = lax.broadcasted_iota(jnp.int32, ab_ref.shape, 1)
    ab_ref[...] = jnp.where(lane == 0, scale * inv, jnp.where(lane == 1, below * inv, at_tgt * inv))


def exchange(st):
    rows = st.shape[0]
    return pl.pallas_call(
        exchange_kernel,
        out_shape=jax.ShapeDtypeStruct((rows, 128), jnp.float32),
        in_specs=[pl.BlockSpec(memory_space=pltpu.VMEM)],
        out_specs=pl.BlockSpec(memory_space=pltpu.VMEM),
        scratch_shapes=[
            pltpu.VMEM((7, rows, 128), jnp.float32),
            pltpu.SemaphoreType.DMA((7,)),
            pltpu.SemaphoreType.DMA((7,)),
        ],
        compiler_params=pltpu.CompilerParams(collective_id=0, has_side_effects=True, vmem_limit_bytes=8 * 1024 * 1024),
        name="exchange",
    )(st)


def finish(pos, pre, stats, out, all_rows, row0, name, deps=(), vmem=ALL_VMEM):
    rows, cols = pre.shape
    sub = min(SUB, rows)
    common = dict(
        cost_estimate=pl.CostEstimate(flops=64 * rows * cols, bytes_accessed=rows * cols * 8, transcendentals=0),
        compiler_params=pltpu.CompilerParams(dimension_semantics=("arbitrary",), vmem_limit_bytes=vmem),
        name=name,
    )
    any_spec = pl.BlockSpec(memory_space=pl.ANY)
    tail = ([] if out is None else [out]) + list(deps)
    full = jax.ShapeDtypeStruct((all_rows, cols), jnp.float32)
    if pos is None:
        return pl.pallas_call(
            last_kernel,
            grid=(rows // sub,),
            out_shape=full,
            in_specs=[pl.BlockSpec((sub, cols), lambda i: (i, 0)), pl.BlockSpec((sub, 128), lambda i: (i, 0))]
            + [any_spec] * len(tail),
            out_specs=pl.BlockSpec((sub, cols), lambda i: (row0 // sub + i, 0)),
            input_output_aliases={2: 0},
            **common,
        )(pre, stats, *tail)
    mine, other = stats
    nv = mine.shape[0]
    return pl.pallas_call(
        final_kernel,
        out_shape=[full, jax.ShapeDtypeStruct((rows, 128), jnp.float32)],
        grid_spec=pltpu.PrefetchScalarGridSpec(
            num_scalar_prefetch=1,
            grid=(rows // sub,),
            in_specs=[
                pl.BlockSpec((sub, cols), lambda i, s: (i, 0)),
                pl.BlockSpec((nv, sub, 128), lambda i, s: (0, i, 0)),
                pl.BlockSpec((nv, sub, 128), lambda i, s: (0, i, 0)),
            ] + [any_spec] * len(tail),
            out_specs=[pl.BlockSpec((sub, cols), lambda i, s: (row0 // sub + i, 0)),
                       pl.BlockSpec((sub, 128), lambda i, s: (i, 0))],
        ),
        input_output_aliases={} if out is None else {4: 0},
        **common,
    )(pos, pre, mine, other, *tail)


def solution(mesh):
    def pipeline(h, w, temp, tgt):
        rows_all = h.shape[0]
        cols = w.shape[1] // 2
        hid = lax.axis_index("hid")
        voc = lax.axis_index("vocab")
        own_half = hid.astype(jnp.int32).reshape(1)
        peer_half = (1 - hid).astype(jnp.int32).reshape(1)
        pos = jnp.stack([voc, hid]).astype(jnp.int32)
        temp2 = temp[:, None]
        tgt2 = (tgt - (voc * 2 + hid) * cols)[:, None]
        tri = (lax.broadcasted_iota(jnp.int32, (CT, CT), 0) <= lax.broadcasted_iota(jnp.int32, (CT, CT), 1)).astype(jnp.bfloat16)
        swap = [(0, 1), (1, 0)]

        blk = 128
        nblk = rows_all // blk
        last = (64, 32, 16, 16)
        tn = 7 * CT
        ht = cols // tn

        units = [(b, 0, blk) for b in range(nblk - 1)]
        units += [(nblk - 1, sum(last[:i]), r) for i, r in enumerate(last)]
        nu = len(units)
        parts = {}
        owns = {}
        tok = None

        def peer(b):
            nonlocal tok
            if b >= nblk:
                return
            splits = last if b == nblk - 1 else (blk,)
            outs = partial_products(h, w, peer_half, b * blk, splits, 0, ht, tn, ht, (tok,))
            tok = outs[0]
            for i, o in enumerate(outs):
                parts[b + i] = [o]

        def mine_half(b):
            nonlocal tok
            if b >= nblk:
                return
            tok = owns[b] = partial_products(h, w, own_half, b * blk, (blk,), 0, ht, tn, ht, (tok,))[0]

        tok = partial_products(h, w, peer_half, 0, (blk,), 0, 2, tn // 2, 2 * ht)[0]
        parts[0] = [tok]
        tok = partial_products(h, w, peer_half, 0, (blk,), 1, ht - 1, tn, ht, (tok,))[0]
        parts[0].append(tok)
        peer(1)
        peer(2)
        mine_half(0)
        mine_half(1)

        def send(arrays):
            return [lax.ppermute(a, "hid", swap) for a in arrays]

        recvs = {0: send(parts[0][:1]) + send(parts[0][1:]), 1: send(parts[1])}
        pres, stats, at_tgt = {}, {}, []
        out = None

        def close(k):
            nonlocal out, tok
            b, at, _ = units[k]
            out, ct = finish(pos, pres[k], stats[k], out, rows_all, b * blk + at, f"finish{k}", (tok,))
            at_tgt.append(ct[:, 0])
            tok = ct

        for k, (b, at, rows) in enumerate(units):
            pres[k], st = local_prefix(temp2, tgt2, tri, owns[b], at, recvs[k], rows, b * blk + at, (tok,),
                                        LAST_VMEM if k == nu - 1 else ALL_VMEM)
            if k == nu - 1:
                tok = st
                close(k - 1)
                ab = exchange(st)
                out = finish(None, pres[k], ab, out, rows_all, b * blk + at, f"finish{k}", (tok,), LAST_VMEM)
                at_tgt.append(ab[:, 2])
                break
            mine = lax.all_gather(st, "vocab")
            if k + 2 < nu:
                *sent, mine = lax.optimization_barrier((*parts[k + 2], mine))
                stats[k] = (mine, send([mine])[0])
                recvs[k + 2] = send(sent)
            else:
                stats[k] = (mine, send([mine])[0])
            tok = mine
            if k >= 1:
                close(k - 1)
            peer(k + 3)
            mine_half(k + 2)
        return out, jnp.concatenate(at_tgt)

    return jax.shard_map(
        pipeline,
        mesh=mesh,
        in_specs=(P("data", "hid"), P("hid", "vocab"), P("data"), P("data")),
        out_specs=(P("data", ("vocab", "hid")), P("data")),
        check_vma=False,
    )
```

profile of v0, /device:TPU:0, one launch (start us, length us, event | category | flops | bytes accessed | tf_op | source)
XLA Modules:
  0.0 1480.6 jit_solution(6235146713385985619)
XLA Ops:
  6.2 20.8 %shard_map.60.refs_0_ = f32[128,10752]{1,0:T(8,128)} custom-call(s32[1]{0:T(128)} %bitcast.4.sel_ref, bf16[1024,2560]{1,0:T(8,128)(2,1)} %h_ref.33, bf16[2560,25088]{1,0:T(8,128)(2,1)} %w_ref.33, f32[128,1792]{1,0:T(8,128)} %shard_map.59.refs_0_), custom_call_target="tpu_custom_call" | custom-call | flops 7046430720 | bytes 60555264 | tf_op jit(solution)/shard_map/pallas_call | solution.py:30
  30.4 24.1 %shard_map.61.refs_0_ = f32[128,12544]{1,0:T(8,128)} custom-call(s32[1]{0:T(128)} %bitcast.4.sel_ref, bf16[1024,2560]{1,0:T(8,128)(2,1)} %h_ref.33, bf16[2560,25088]{1,0:T(8,128)(2,1)} %w_ref.33, f32[128,10752]{1,0:T(8,128)} %shard_map.60.refs_0_), custom_call_target="tpu_custom_call" | custom-call | flops 8220835840 | bytes 70647808 | tf_op jit(solution)/shard_map/pallas_call | solution.py:30
  56.5 24.1 %shard_map.62.refs_0_ = f32[128,12544]{1,0:T(8,128)} custom-call(s32[1]{0:T(128)} %bitcast.4.sel_ref, bf16[1024,2560]{1,0:T(8,128)(2,1)} %h_ref.33, bf16[2560,25088]{1,0:T(8,128)(2,1)} %w_ref.33, f32[128,12544]{1,0:T(8,128)} %shard_map.61.refs_0_), custom_call_target="tpu_custom_call" | custom-call | flops 8220835840 | bytes 70647808 | tf_op jit(solution)/shard_map/pallas_call | solution.py:30
  80.6 24.1 %shard_map.63.refs_0_.own_ref = f32[128,12544]{1,0:T(8,128)} custom-call(s32[1]{0:T(128)} %bitcast.2.sel_ref, bf16[1024,2560]{1,0:T(8,128)(2,1)} %h_ref.33, bf16[2560,25088]{1,0:T(8,128)(2,1)} %w_ref.33, f32[128,12544]{1,0:T(8,128)} %shard_map.62.refs_0_), custom_call_target="tpu_custom_call" | custom-call | flops 8220835840 | bytes 70647808 | tf_op jit(solution)/shard_map/pallas_call | solution.py:30
  108.8 24.1 %shard_map.64.refs_2_.own_ref = f32[128,12544]{1,0:T(8,128)} custom-call(s32[1]{0:T(128)} %bitcast.2.sel_ref, bf16[1024,2560]{1,0:T(8,128)(2,1)} %h_ref.33, bf16[2560,25088]{1,0:T(8,128)(2,1)} %w_ref.33, f32[128,12544]{1,0:T(8,128)} %shard_map.63.refs_0_.own_ref), custom_call_target="tpu_custom_call" | custom-call | flops 8220835840 | bytes 70647808 | tf_op jit(solution)/shard_map/pallas_call | solution.py:30
  132.9 37.0 %collective-permute-done.1.refs_0_ = f32[128,1792]{1,0:T(8,128)} collective-permute-done((f32[128,1792]{1,0:T(8,128)}, f32[128,1792]{1,0:T(8,128)}, u32[]{:S(2)}, u32[]{:S(2)}) %collective-permute-start.1) | collective-permute-done | bytes 917536 | tf_op jit(solution)/shard_map/ppermute | solution.py:323
  169.9 17.6 %shard_map.65 = (f32[128,12544]{1,0:T(8,128)}, f32[128,128]{1,0:T(8,128)}) custom-call(f32[1024,1]{1,0:T(8,128)} %copy.36.temp_ref, s32[1024,1]{1,0:T(8,128)} %copy.37.tgt_ref, bf16[256,256]{1,0:T(8,128)(2,1)} %fusion.tri_ref, f32[128,12544]{1,0:T(8,128)} %shard_map.63.refs_0_.own_ref, f32[128,1792]{1,0:T(8,128)} %collective-permute-done.1.refs_0_, ...), custom_call_target="tpu_custom_call" | custom-call | flops 2466250752 | bytes 19267584 | tf_op jit(solution)/shard_map/pallas_call | solution.py:115
  199.7 24.1 %shard_map.66.refs_0_ = f32[128,12544]{1,0:T(8,128)} custom-call(s32[1]{0:T(128)} %bitcast.4.sel_ref, bf16[1024,2560]{1,0:T(8,128)(2,1)} %h_ref.33, bf16[2560,25088]{1,0:T(8,128)(2,1)} %w_ref.33, f32[4,128,128]{2,1,0:T(8,128)} %bitcast.5.refs_0_.mine_ref), custom_call_target="tpu_custom_call" | custom-call | flops 8220835840 | bytes 70647808 | tf_op jit(solution)/shard_map/pallas_call | solution.py:30
  223.7 24.1 %shard_map.67.refs_1_.own_ref = f32[128,12544]{1,0:T(8,128)} custom-call(s32[1]{0:T(128)} %bitcast.2.sel_ref, bf16[1024,2560]{1,0:T(8,128)(2,1)} %h_ref.33, bf16[2560,25088]{1,0:T(8,128)(2,1)} %w_ref.33, f32[128,12544]{1,0:T(8,128)} %shard_map.66.refs_0_), custom_call_target="tpu_custom_call" | custom-call | flops 8220835840 | bytes 70647808 | tf_op jit(solution)/shard_map/pallas_call | solution.py:30
  247.9 59.7 %collective-permute-done.refs_0_ = f32[128,12544]{1,0:T(8,128)} collective-permute-done((f32[128,12544]{1,0:T(8,128)}, f32[128,12544]{1,0:T(8,128)}, u32[]{:S(2)}, u32[]{:S(2)}) %collective-permute-start) | collective-permute-done | bytes 6422560 | tf_op jit(solution)/shard_map/ppermute | solution.py:323
  337.4 113.4 %collective-permute-done.4.other_ref = f32[4,128,128]{2,1,0:T(8,128)} collective-permute-done((f32[4,128,128]{2,1,0:T(8,128)}, f32[4,128,128]{2,1,0:T(8,128)}, u32[]{:S(2)}, u32[]{:S(2)}) %collective-permute-start.4) | collective-permute-done | bytes 262176 | tf_op jit(solution)/shard_map/ppermute | solution.py:323
  458.0 24.1 %shard_map.69.refs_0_ = f32[128,12544]{1,0:T(8,128)} custom-call(s32[1]{0:T(128)} %bitcast.4.sel_ref, bf16[1024,2560]{1,0:T(8,128)(2,1)} %h_ref.33, bf16[2560,25088]{1,0:T(8,128)(2,1)} %w_ref.33, f32[128,128]{1,0:T(8,128)} %get-tuple-element.73.refs_0_), custom_call_target="tpu_custom_call" | custom-call | flops 8220835840 | bytes 70647808 | tf_op jit(solution)/shard_map/pallas_call | solution.py:30
  482.1 24.1 %shard_map.70.refs_1_.own_ref = f32[128,12544]{1,0:T(8,128)} custom-call(s32[1]{0:T(128)} %bitcast.2.sel_ref, bf16[1024,2560]{1,0:T(8,128)(2,1)} %h_ref.33, bf16[2560,25088]{1,0:T(8,128)(2,1)} %w_ref.33, f32[128,12544]{1,0:T(8,128)} %shard_map.69.refs_0_), custom_call_target="tpu_custom_call" | custom-call | flops 8220835840 | bytes 70647808 | tf_op jit(solution)/shard_map/pallas_call | solution.py:30
  537.4 194.3 %collective-permute-done.3.other_ref = f32[4,128,128]{2,1,0:T(8,128)} collective-permute-done((f32[4,128,128]{2,1,0:T(8,128)}, f32[4,128,128]{2,1,0:T(8,128)}, u32[]{:S(2)}, u32[]{:S(2)}) %collective-permute-start.3) | collective-permute-done | bytes 262176 | tf_op jit(solution)/shard_map/ppermute | solution.py:323
  738.9 24.1 %shard_map.72.refs_0_ = f32[128,12544]{1,0:T(8,128)} custom-call(s32[1]{0:T(128)} %bitcast.4.sel_ref, bf16[1024,2560]{1,0:T(8,128)(2,1)} %h_ref.33, bf16[2560,25088]{1,0:T(8,128)(2,1)} %w_ref.33, f32[128,128]{1,0:T(8,128)} %get-tuple-element.77.refs_0_), custom_call_target="tpu_custom_call" | custom-call | flops 8220835840 | bytes 70647808 | tf_op jit(solution)/shard_map/pallas_call | solution.py:30
  763.0 24.1 %shard_map.73.refs_1_.own_ref = f32[128,12544]{1,0:T(8,128)} custom-call(s32[1]{0:T(128)} %bitcast.2.sel_ref, bf16[1024,2560]{1,0:T(8,128)(2,1)} %h_ref.33, bf16[2560,25088]{1,0:T(8,128)(2,1)} %w_ref.33, f32[128,12544]{1,0:T(8,128)} %shard_map.72.refs_0_), custom_call_target="tpu_custom_call" | custom-call | flops 8220835840 | bytes 70647808 | tf_op jit(solution)/shard_map/pallas_call | solution.py:30
  823.5 24.1 %shard_map.75.refs_0_ = f32[128,12544]{1,0:T(8,128)} custom-call(s32[1]{0:T(128)} %bitcast.4.sel_ref, bf16[1024,2560]{1,0:T(8,128)(2,1)} %h_ref.33, bf16[2560,25088]{1,0:T(8,128)(2,1)} %w_ref.33, f32[128,128]{1,0:T(8,128)} %get-tuple-element.84.refs_0_), custom_call_target="tpu_custom_call" | custom-call | flops 8220835840 | bytes 70647808 | tf_op jit(solution)/shard_map/pallas_call | solution.py:30
  847.6 24.1 %shard_map.76.refs_1_.own_ref = f32[128,12544]{1,0:T(8,128)} custom-call(s32[1]{0:T(128)} %bitcast.2.sel_ref, bf16[1024,2560]{1,0:T(8,128)(2,1)} %h_ref.33, bf16[2560,25088]{1,0:T(8,128)(2,1)} %w_ref.33, f32[128,12544]{1,0:T(8,128)} %shard_map.75.refs_0_), custom_call_target="tpu_custom_call" | custom-call | flops 8220835840 | bytes 70647808 | tf_op jit(solution)/shard_map/pallas_call | solution.py:30
  901.0 196.0 %collective-permute-done.10.other_ref = f32[4,128,128]{2,1,0:T(8,128)} collective-permute-done((f32[4,128,128]{2,1,0:T(8,128)}, f32[4,128,128]{2,1,0:T(8,128)}, u32[]{:S(2)}, u32[]{:S(2)}) %collective-permute-start.10) | collective-permute-done | bytes 262176 | tf_op jit(solution)/shard_map/ppermute | solution.py:323
  1104.2 24.1 %shard_map.78 = (f32[64,12544]{1,0:T(8,128)}, f32[32,12544]{1,0:T(8,128)}, f32[16,12544]{1,0:T(8,128)}, f32[16,12544]{1,0:T(8,128)}) custom-call(s32[1]{0:T(128)} %bitcast.4.sel_ref, bf16[1024,2560]{1,0:T(8,128)(2,1)} %h_ref.33, bf16[2560,25088]{1,0:T(8,128)(2,1)} %w_ref.33, f32[128,128]{1,0:T(8,128)} %get-tuple-element.91.refs_0_), custom_call_target="tpu_custom_call" | custom-call | flops 8220835840 | bytes 70647808 | tf_op jit(solution)/shard_map/pallas_call | solution.py:30
  1128.4 24.1 %shard_map.79.refs_1_.own_ref = f32[128,12544]{1,0:T(8,128)} custom-call(s32[1]{0:T(128)} %bitcast.2.sel_ref, bf16[1024,2560]{1,0:T(8,128)(2,1)} %h_ref.33, bf16[2560,25088]{1,0:T(8,128)(2,1)} %w_ref.33, f32[64,12544]{1,0:T(8,128)} %get-tuple-element.108.refs_0_), custom_call_target="tpu_custom_call" | custom-call | flops 8220835840 | bytes 70647808 | tf_op jit(solution)/shard_map/pallas_call | solution.py:30
  1181.5 72.9 %collective-permute-done.9.other_ref = f32[4,128,128]{2,1,0:T(8,128)} collective-permute-done((f32[4,128,128]{2,1,0:T(8,128)}, f32[4,128,128]{2,1,0:T(8,128)}, u32[]{:S(2)}, u32[]{:S(2)}) %collective-permute-start.9) | collective-permute-done | bytes 262176 | tf_op jit(solution)/shard_map/ppermute | solution.py:323
  1261.7 24.1 %shard_map.81.refs_1_.own_ref = f32[128,12544]{1,0:T(8,128)} custom-call(s32[1]{0:T(128)} %bitcast.2.sel_ref, bf16[1024,2560]{1,0:T(8,128)(2,1)} %h_ref.33, bf16[2560,25088]{1,0:T(8,128)(2,1)} %w_ref.33, f32[128,128]{1,0:T(8,128)} %get-tuple-element.96.refs_0_), custom_call_target="tpu_custom_call" | custom-call | flops 8220835840 | bytes 70647808 | tf_op jit(solution)/shard_map/pallas_call | solution.py:30
  1316.5 40.4 %collective-permute-done.15.other_ref = f32[4,128,128]{2,1,0:T(8,128)} collective-permute-done((f32[4,128,128]{2,1,0:T(8,128)}, f32[4,128,128]{2,1,0:T(8,128)}, u32[]{:S(2)}, u32[]{:S(2)}) %collective-permute-start.15) | collective-permute-done | bytes 262176 | tf_op jit(solution)/shard_map/ppermute | solution.py:323
  (125 shorter events, 366.2 us)
Async XLA Ops:
  27.1 142.8 %collective-permute-start.2 = (f32[128,10752]{1,0:T(8,128)}, f32[128,10752]{1,0:T(8,128)}, u32[]{:S(2)}, u32[]{:S(2)}) collective-permute-start(f32[128,10752]{1,0:T(8,128)} %shard_map.60.refs_0_), channel_id=1, source_target_pairs={{0,4},{4,0},{1,5},{5,1},{2,6},{6,2},{3,7},{7,3}} | collective-permute-start | bytes 16515080 | tf_op jit(solution)/shard_map/ppermute | solution.py:323
  30.4 139.5 %collective-permute-start.1 = (f32[128,1792]{1,0:T(8,128)}, f32[128,1792]{1,0:T(8,128)}, u32[]{:S(2)}, u32[]{:S(2)}) collective-permute-start(f32[128,1792]{1,0:T(8,128)} %shard_map.59.refs_0_), channel_id=1, source_target_pairs={{0,4},{4,0},{1,5},{5,1},{2,6},{6,2},{3,7},{7,3}} | collective-permute-start | bytes 2752520 | tf_op jit(solution)/shard_map/ppermute | solution.py:323
  54.5 253.0 %collective-permute-start = (f32[128,12544]{1,0:T(8,128)}, f32[128,12544]{1,0:T(8,128)}, u32[]{:S(2)}, u32[]{:S(2)}) collective-permute-start(f32[128,12544]{1,0:T(8,128)} %shard_map.61.refs_0_), channel_id=1, source_target_pairs={{0,4},{4,0},{1,5},{5,1},{2,6},{6,2},{3,7},{7,3}} | collective-permute-start | bytes 19267592 | tf_op jit(solution)/shard_map/ppermute | solution.py:323
  197.6 308.6 %collective-permute-start.5 = (f32[128,12544]{1,0:T(8,128)}, f32[128,12544]{1,0:T(8,128)}, u32[]{:S(2)}, u32[]{:S(2)}) collective-permute-start(f32[128,12544]{1,0:T(8,128)} %shard_map.62.refs_0_), channel_id=1, source_target_pairs={{0,4},{4,0},{1,5},{5,1},{2,6},{6,2},{3,7},{7,3}} | collective-permute-start | bytes 19267592 | tf_op jit(solution)/shard_map/ppermute | solution.py:323
  199.1 251.6 %collective-permute-start.4 = (f32[4,128,128]{2,1,0:T(8,128)}, f32[4,128,128]{2,1,0:T(8,128)}, u32[]{:S(2)}, u32[]{:S(2)}) collective-permute-start(f32[4,128,128]{2,1,0:T(8,128)} %bitcast.5.refs_0_.mine_ref), channel_id=1, source_target_pairs={{0,4},{4,0},{1,5},{5,1},{2,6},{6,2},{3,7},{7,3}} | collective-permute-start | bytes 786440 | tf_op jit(solution)/shard_map/ppermute | solution.py:323
  335.3 451.8 %collective-permute-start.8 = (f32[128,12544]{1,0:T(8,128)}, f32[128,12544]{1,0:T(8,128)}, u32[]{:S(2)}, u32[]{:S(2)}) collective-permute-start(f32[128,12544]{1,0:T(8,128)} %shard_map.66.refs_0_), channel_id=1, source_target_pairs={{0,4},{4,0},{1,5},{5,1},{2,6},{6,2},{3,7},{7,3}} | collective-permute-start | bytes 19267592 | tf_op jit(solution)/shard_map/ppermute | solution.py:323
  533.8 337.8 %collective-permute-start.6 = (f32[128,12544]{1,0:T(8,128)}, f32[128,12544]{1,0:T(8,128)}, u32[]{:S(2)}, u32[]{:S(2)}) collective-permute-start(f32[128,12544]{1,0:T(8,128)} %shard_map.69.refs_0_), channel_id=1, source_target_pairs={{0,4},{4,0},{1,5},{5,1},{2,6},{6,2},{3,7},{7,3}} | collective-permute-start | bytes 19267592 | tf_op jit(solution)/shard_map/ppermute | solution.py:323
  535.4 196.3 %collective-permute-start.3 = (f32[4,128,128]{2,1,0:T(8,128)}, f32[4,128,128]{2,1,0:T(8,128)}, u32[]{:S(2)}, u32[]{:S(2)}) collective-permute-start(f32[4,128,128]{2,1,0:T(8,128)} %bitcast.25), channel_id=1, source_target_pairs={{0,4},{4,0},{1,5},{5,1},{2,6},{6,2},{3,7},{7,3}} | collective-permute-start | bytes 786440 | tf_op jit(solution)/shard_map/ppermute | solution.py:323
  535.9 280.4 %collective-permute-start.7 = (f32[4,128,128]{2,1,0:T(8,128)}, f32[4,128,128]{2,1,0:T(8,128)}, u32[]{:S(2)}, u32[]{:S(2)}) collective-permute-start(f32[4,128,128]{2,1,0:T(8,128)} %bitcast.7.refs_1_.mine_ref), channel_id=1, source_target_pairs={{0,4},{4,0},{1,5},{5,1},{2,6},{6,2},{3,7},{7,3}} | collective-permute-start | bytes 786440 | tf_op jit(solution)/shard_map/ppermute | solution.py:323
  814.7 337.8 %collective-permute-start.11 = (f32[128,12544]{1,0:T(8,128)}, f32[128,12544]{1,0:T(8,128)}, u32[]{:S(2)}, u32[]{:S(2)}) collective-permute-start(f32[128,12544]{1,0:T(8,128)} %shard_map.72.refs_0_), channel_id=1, source_target_pairs={{0,4},{4,0},{1,5},{5,1},{2,6},{6,2},{3,7},{7,3}} | collective-permute-start | bytes 19267592 | tf_op jit(solution)/shard_map/ppermute | solution.py:323
  898.9 386.9 %collective-permute-start.12 = (f32[128,12544]{1,0:T(8,128)}, f32[128,12544]{1,0:T(8,128)}, u32[]{:S(2)}, u32[]{:S(2)}) collective-permute-start(f32[128,12544]{1,0:T(8,128)} %shard_map.75.refs_0_), channel_id=1, source_target_pairs={{0,4},{4,0},{1,5},{5,1},{2,6},{6,2},{3,7},{7,3}} | collective-permute-start | bytes 19267592 | tf_op jit(solution)/shard_map/ppermute | solution.py:323
  899.5 197.5 %collective-permute-start.10 = (f32[4,128,128]{2,1,0:T(8,128)}, f32[4,128,128]{2,1,0:T(8,128)}, u32[]{:S(2)}, u32[]{:S(2)}) collective-permute-start(f32[4,128,128]{2,1,0:T(8,128)} %bitcast.22), channel_id=1, source_target_pairs={{0,4},{4,0},{1,5},{5,1},{2,6},{6,2},{3,7},{7,3}} | collective-permute-start | bytes 786440 | tf_op jit(solution)/shard_map/ppermute | solution.py:323
  1179.5 184.6 %collective-permute-start.16 = (f32[64,12544]{1,0:T(8,128)}, f32[64,12544]{1,0:T(8,128)}, u32[]{:S(2)}, u32[]{:S(2)}) collective-permute-start(f32[64,12544]{1,0:T(8,128)} %get-tuple-element.108.refs_0_), channel_id=1, source_target_pairs={{0,4},{4,0},{1,5},{5,1},{2,6},{6,2},{3,7},{7,3}} | collective-permute-start | bytes 9633800 | tf_op jit(solution)/shard_map/ppermute | solution.py:323
  1181.0 73.4 %collective-permute-start.9 = (f32[4,128,128]{2,1,0:T(8,128)}, f32[4,128,128]{2,1,0:T(8,128)}, u32[]{:S(2)}, u32[]{:S(2)}) collective-permute-start(f32[4,128,128]{2,1,0:T(8,128)} %bitcast.16), channel_id=1, source_target_pairs={{0,4},{4,0},{1,5},{5,1},{2,6},{6,2},{3,7},{7,3}} | collective-permute-start | bytes 786440 | tf_op jit(solution)/shard_map/ppermute | solution.py:323
  1313.0 79.2 %collective-permute-start.13 = (f32[32,12544]{1,0:T(8,128)}, f32[32,12544]{1,0:T(8,128)}, u32[]{:S(2)}, u32[]{:S(2)}) collective-permute-start(f32[32,12544]{1,0:T(8,128)} %get-tuple-element.101), channel_id=1, source_target_pairs={{0,4},{4,0},{1,5},{5,1},{2,6},{6,2},{3,7},{7,3}} | collective-permute-start | bytes 4816904 | tf_op jit(solution)/shard_map/ppermute | solution.py:323
  1314.5 42.4 %collective-permute-start.15 = (f32[4,128,128]{2,1,0:T(8,128)}, f32[4,128,128]{2,1,0:T(8,128)}, u32[]{:S(2)}, u32[]{:S(2)}) collective-permute-start(f32[4,128,128]{2,1,0:T(8,128)} %bitcast.19), channel_id=1, source_target_pairs={{0,4},{4,0},{1,5},{5,1},{2,6},{6,2},{3,7},{7,3}} | collective-permute-start | bytes 786440 | tf_op jit(solution)/shard_map/ppermute | solution.py:323
  1315.0 69.9 %collective-permute-start.14 = (f32[4,128,128]{2,1,0:T(8,128)}, f32[4,128,128]{2,1,0:T(8,128)}, u32[]{:S(2)}, u32[]{:S(2)}) collective-permute-start(f32[4,128,128]{2,1,0:T(8,128)} %bitcast.11.refs_1_.mine_ref), channel_id=1, source_target_pairs={{0,4},{4,0},{1,5},{5,1},{2,6},{6,2},{3,7},{7,3}} | collective-permute-start | bytes 786440 | tf_op jit(solution)/shard_map/ppermute | solution.py:323
  1383.4 50.4 %collective-permute-start.20 = (f32[16,12544]{1,0:T(8,128)}, f32[16,12544]{1,0:T(8,128)}, u32[]{:S(2)}, u32[]{:S(2)}) collective-permute-start(f32[16,12544]{1,0:T(8,128)} %get-tuple-element.120), channel_id=1, source_target_pairs={{0,4},{4,0},{1,5},{5,1},{2,6},{6,2},{3,7},{7,3}} | collective-permute-start | bytes 2408456 | tf_op jit(solution)/shard_map/ppermute | solution.py:323
  1407.5 47.0 %collective-permute-start.17 = (f32[16,12544]{1,0:T(8,128)}, f32[16,12544]{1,0:T(8,128)}, u32[]{:S(2)}, u32[]{:S(2)}) collective-permute-start(f32[16,12544]{1,0:T(8,128)} %get-tuple-element.114), channel_id=1, source_target_pairs={{0,4},{4,0},{1,5},{5,1},{2,6},{6,2},{3,7},{7,3}} | collective-permute-start | bytes 2408456 | tf_op jit(solution)/shard_map/ppermute | solution.py:323
  1412.6 17.0 %collective-permute-start.19 = (f32[4,64,128]{2,1,0:T(8,128)}, f32[4,64,128]{2,1,0:T(8,128)}, u32[]{:S(2)}, u32[]{:S(2)}) collective-permute-start(f32[4,64,128]{2,1,0:T(8,128)} %bitcast.28), channel_id=1, source_target_pairs={{0,4},{4,0},{1,5},{5,1},{2,6},{6,2},{3,7},{7,3}} | collective-permute-start | bytes 393224 | tf_op jit(solution)/shard_map/ppermute | solution.py:323
  1417.1 32.4 %collective-permute-start.18 = (f32[4,32,128]{2,1,0:T(8,128)}, f32[4,32,128]{2,1,0:T(8,128)}, u32[]{:S(2)}, u32[]{:S(2)}) collective-permute-start(f32[4,32,128]{2,1,0:T(8,128)} %bitcast.13.refs_1_.mine_ref), channel_id=1, source_target_pairs={{0,4},{4,0},{1,5},{5,1},{2,6},{6,2},{3,7},{7,3}} | collective-permute-start | bytes 196616 | tf_op jit(solution)/shard_map/ppermute | solution.py:323
  1447.4 24.1 %collective-permute-start.21 = (f32[4,16,128]{2,1,0:T(8,128)}, f32[4,16,128]{2,1,0:T(8,128)}, u32[]{:S(2)}, u32[]{:S(2)}) collective-permute-start(f32[4,16,128]{2,1,0:T(8,128)} %bitcast.14.refs_1_.mine_ref), channel_id=1, source_target_pairs={{0,4},{4,0},{1,5},{5,1},{2,6},{6,2},{3,7},{7,3}} | collective-permute-start | bytes 98312 | tf_op jit(solution)/shard_map/ppermute | solution.py:323
  1454.5 2.8 copy-start
  1465.8 5.1 copy-start.10
  (18 other events, 17.8 us)
where the time goes:
time: 1480 us
  waiting for transfers between devices  726 us (49%)
  Pallas kernels  605 us (41%)
  blocking collectives  95.5 us (6%)
  starting transfers between devices  26.1 us (2%)
  local copies, waits for them, and re-layouts  26 us (2%)
    ppermute x22, waiting for transfers between devices, send(): return [lax.ppermute(a, 'hid', swap) for a in arrays]  726 us
    pallas_call x17, Pallas kernels, partial_products(): pl.pallas_call(functools.partial(mm_kernel, splits=splits), out_shape=[ja...  388 us
    pallas_call x11, Pallas kernels, local_prefix(): pl.pallas_call(functools.partial(local_kernel, npieces=len(recvs), ndeps=...  149 us
    all_gather x10, blocking collectives, pipeline(): mine = lax.all_gather(st, 'vocab')  95.5 us
    pallas_call x10, Pallas kernels, finish(): pl.pallas_call(final_kernel, out_shape=[full, jax.ShapeDtypeStruct((rows,...  61.7 us
  transfers between devices with their start and end apart: 22, of which 8 were waited for; matrix products, arithmetic and copies ran while one was open for 1% of the time, Pallas kernels for 39%

commit v1 on v0

v1 whole, which is shorter than its diff:
```python
import functools

import jax
import jax.numpy as jnp
from jax import lax
from jax.experimental import pallas as pl
from jax.experimental.pallas import tpu as pltpu
from jax.sharding import PartitionSpec as P


CT = 256
SUB = 32
ALL_VMEM = 67043328


def mm_kernel(sel_ref, h_ref, w_ref, *refs, splits):
    out_refs = refs[len(refs) - len(splits):]
    res = jnp.dot(h_ref[...], w_ref[...], preferred_element_type=jnp.float32)
    at = 0
    for ref, rows in zip(out_refs, splits):
        ref[...] = res[at:at + rows]
        at += rows


def partial_products(h, w, half, row0, splits, tile0, ntiles, tn, half_tiles, deps=()):
    rows = sum(splits)
    depth = h.shape[1]
    cols = ntiles * tn
    return pl.pallas_call(
        functools.partial(mm_kernel, splits=splits),
        out_shape=[jax.ShapeDtypeStruct((r, cols), jnp.float32) for r in splits],
        grid_spec=pltpu.PrefetchScalarGridSpec(
            num_scalar_prefetch=1,
            grid=(ntiles,),
            in_specs=[
                pl.BlockSpec((rows, depth), lambda j, s: (row0 // rows, 0)),
                pl.BlockSpec((depth, tn), lambda j, s: (0, s[0] * half_tiles + tile0 + j)),
            ] + [pl.BlockSpec(memory_space=pl.ANY)] * len(deps),
            out_specs=[pl.BlockSpec((r, tn), lambda j, s: (0, j)) for r in splits],
        ),
        cost_estimate=pl.CostEstimate(
            flops=2 * rows * depth * cols, bytes_accessed=depth * cols * 2 + rows * cols * 4, transcendentals=0),
        compiler_params=pltpu.CompilerParams(dimension_semantics=("arbitrary",), vmem_limit_bytes=ALL_VMEM),
    )(half, h, w, *deps)


def local_kernel(temp_ref, tgt_ref, tri_ref, own_ref, *refs, npieces, has_prev, skip, at, group):
    recv_refs = refs[:npieces]
    prev_ref = refs[npieces] if has_prev else None
    pre_ref, st_ref, z_s, hi_s, mid_s, lo_s, st_s = refs[npieces + has_prev + skip:]
    step, nsteps = pl.program_id(0), pl.num_programs(0)
    rows = own_ref.shape[0]
    nt = own_ref.shape[1] // CT
    temp = jnp.broadcast_to(temp_ref[...], (rows, CT))
    mx = jnp.full((rows, CT), -jnp.inf, jnp.float32)
    t0 = 0
    for ref in recv_refs:
        n = ref.shape[1] // CT

        def max_step(j, mx, ref=ref, t0=t0):
            src = pl.ds(pl.multiple_of(j * CT, CT), CT)
            dst = pl.ds(pl.multiple_of((t0 + j) * CT, CT), CT)
            z = (own_ref[:, dst] + ref[:, src]) * temp
            z_s[t0 + j] = z
            return jnp.maximum(mx, z)

        mx = lax.fori_loop(0, n, max_step, mx, unroll=7)
        t0 += n
    m = jnp.max(mx, axis=1, keepdims=True)
    mb = jnp.broadcast_to(m, (rows, CT))
    tgt = jnp.broadcast_to(tgt_ref[...], (rows, CT))
    col = lax.broadcasted_iota(jnp.int32, (rows, CT), 1)
    rel = tgt - col

    def exp_step(j, carry):
        sacc, cacc = carry
        e = jnp.exp(z_s[j] - mb)
        hi = e.astype(jnp.bfloat16)
        r1 = e - hi.astype(jnp.float32)
        mid = r1.astype(jnp.bfloat16)
        lo = (r1 - mid.astype(jnp.float32)).astype(jnp.bfloat16)
        hi_s[j] = hi
        mid_s[j] = mid
        lo_s[j] = lo
        return sacc + e, cacc + jnp.where(rel >= j * CT, e, 0.0)

    zero = jnp.zeros((rows, CT), jnp.float32)
    sacc, cacc = lax.fori_loop(0, nt, exp_step, (zero, zero), unroll=7)
    s = jnp.sum(sacc, axis=1, keepdims=True)
    c = jnp.sum(cacc, axis=1, keepdims=True)
    lane = lax.broadcasted_iota(jnp.int32, (rows, 128), 1)

    @pl.when(step == 0)
    def _():
        st_s[...] = jnp.zeros_like(st_s)

    st_s[pl.ds(pl.multiple_of(at + step * rows, rows), rows), :] = jnp.where(
        lane == 0, m, jnp.where(lane == 1, s, jnp.where(lane == 2, c, 0.0)))

    @pl.when(step == nsteps - 1)
    def _():
        st = st_s[...].T[0:8]
        st_ref[...] = st + prev_ref[...] if has_prev else st

    tri = tri_ref[...]

    def prefix_step(g, carry):
        span = pl.ds(g * group, group)
        pre = jnp.dot(hi_s[span].reshape(group * rows, CT), tri, preferred_element_type=jnp.float32)
        pre += jnp.dot(mid_s[span].reshape(group * rows, CT), tri, preferred_element_type=jnp.float32)
        pre += jnp.dot(lo_s[span].reshape(group * rows, CT), tri, preferred_element_type=jnp.float32)
        for k in range(group):
            blk = pre[k * rows:(k + 1) * rows]
            dst = pl.ds(pl.multiple_of((g * group + k) * CT, CT), CT)
            pre_ref[:, dst] = blk + carry
            carry = carry + jnp.broadcast_to(blk[:, CT - 1:CT], (rows, CT))
        return carry

    lax.fori_loop(0, nt // group, prefix_step, zero)


def local_prefix(temp, tgt, tri, own, at, recvs, rows, row0, prev, deps):
    cols = own.shape[1]
    nt = cols // CT
    sub = min(SUB, rows)
    extra = ([] if prev is None else [prev]) + list(deps)
    extra_specs = ([] if prev is None else [pl.BlockSpec((8, 128), lambda i: (0, 0))])
    extra_specs += [pl.BlockSpec(memory_space=pl.ANY)] * len(deps)
    return pl.pallas_call(
        functools.partial(
            local_kernel, npieces=len(recvs), has_prev=int(prev is not None), skip=len(deps), at=at, group=7),
        grid=(rows // sub,),
        out_shape=[jax.ShapeDtypeStruct((rows, cols), jnp.float32), jax.ShapeDtypeStruct((8, 128), jnp.float32)],
        in_specs=[
            pl.BlockSpec((sub, 1), lambda i: (row0 // sub + i, 0)),
            pl.BlockSpec((sub, 1), lambda i: (row0 // sub + i, 0)),
            pl.BlockSpec((CT, CT), lambda i: (0, 0)),
            pl.BlockSpec((sub, cols), lambda i: (at // sub + i, 0)),
        ] + [pl.BlockSpec((sub, r.shape[1]), lambda i: (i, 0)) for r in recvs] + extra_specs,
        out_specs=[pl.BlockSpec((sub, cols), lambda i: (i, 0)), pl.BlockSpec((8, 128), lambda i: (0, 0))],
        scratch_shapes=[
            pltpu.VMEM((nt, sub, CT), jnp.float32),
            pltpu.VMEM((nt, sub, CT), jnp.bfloat16),
            pltpu.VMEM((nt, sub, CT), jnp.bfloat16),
            pltpu.VMEM((nt, sub, CT), jnp.bfloat16),
            pltpu.VMEM((128, 128), jnp.float32),
        ],
        cost_estimate=pl.CostEstimate(
            flops=6 * rows * cols * CT, bytes_accessed=rows * cols * 12, transcendentals=rows * cols),
        compiler_params=pltpu.CompilerParams(dimension_semantics=("arbitrary",), vmem_limit_bytes=ALL_VMEM),
    )(temp, tgt, tri, own, *recvs, *extra)


def combine(stats, me):
    top = functools.reduce(jnp.maximum, [st[0:1] for _, st in stats])
    total = below = at_tgt = jnp.zeros_like(top)
    scale = jnp.exp(stats[0][1][0:1] - top)
    for index, st in stats:
        f = jnp.exp(st[0:1] - top)
        s = st[1:2] * f
        total += s
        at_tgt += st[2:3] * f
        below += jnp.where(index < me, s, 0.0)
    inv = 1.0 / total
    first = lax.broadcasted_iota(jnp.int32, (128, 128), 0) == 0
    return jnp.where(first, scale * inv, below * inv).T, at_tgt * inv


def merged(ct, at_tgt, blk, at, rows):
    row = lax.broadcasted_iota(jnp.int32, ct.shape, 0)
    lane = lax.broadcasted_iota(jnp.int32, ct.shape, 1)
    return jnp.where((row == blk) & (lane >= at) & (lane < at + rows), at_tgt, ct)


def final_kernel(pos_ref, pre_ref, st_ref, mine_ref, other_ref, ctin_ref, *refs, blk, at, rows):
    out_ref, ct_ref, ab_s = refs[-3:]
    step = pl.program_id(0)
    sub = pre_ref.shape[0]

    @pl.when(step == 0)
    def _():
        voc, hid = pos_ref[0], pos_ref[1]
        nv = mine_ref.shape[0]
        me = voc * 2 + hid
        own = st_ref[...]
        stats = [(me, own)]
        real = lax.broadcasted_iota(jnp.int32, own.shape, 0) == 0
        for v in range(nv):
            stats.append((v * 2 + hid, jnp.where(real | (v != voc), mine_ref[v], 0.0)))
            stats.append((v * 2 + 1 - hid, other_ref[v]))
        ab, at_tgt = combine(stats, me)
        ab_s[...] = ab
        ct_ref[...] = merged(ctin_ref[...], at_tgt, blk, at, rows)

    ab = ab_s[pl.ds(pl.multiple_of(at + step * sub, sub), sub), :]
    out_ref[...] = pre_ref[...] * ab[:, 0:1] + ab[:, 1:2]


def finish(pos, pre, st, mine, other, out, ct, all_rows, blk, at, row0, deps):
    rows, cols = pre.shape
    sub = min(SUB, rows)
    tail = ([] if out is None else [out]) + list(deps)
    small = pl.BlockSpec((8, 128), lambda i, s: (0, 0))
    wide = pl.BlockSpec(mine.shape, lambda i, s: (0, 0, 0))
    return pl.pallas_call(
        functools.partial(final_kernel, blk=blk, at=at, rows=rows),
        out_shape=[jax.ShapeDtypeStruct((all_rows, cols), jnp.float32), jax.ShapeDtypeStruct((8, 128), jnp.float32)],
        grid_spec=pltpu.PrefetchScalarGridSpec(
            num_scalar_prefetch=1,
            grid=(rows // sub,),
            in_specs=[pl.BlockSpec((sub, cols), lambda i, s: (i, 0)), small, wide, wide, small]
            + [pl.BlockSpec(memory_space=pl.ANY)] * len(tail),
            out_specs=[pl.BlockSpec((sub, cols), lambda i, s: (row0 // sub + i, 0)), small],
            scratch_shapes=[pltpu.VMEM((128, 128), jnp.float32)],
        ),
        input_output_aliases={} if out is None else {6: 0},
        cost_estimate=pl.CostEstimate(flops=64 * rows * cols, bytes_accessed=rows * cols * 8, transcendentals=0),
        compiler_params=pltpu.CompilerParams(dimension_semantics=("arbitrary",), vmem_limit_bytes=ALL_VMEM),
    )(pos, pre, st, mine, other, ct, *tail)


def exchange_kernel(st_ref, ab_ref, at_tgt_ref, slots, send_sem, recv_sem):
    voc = lax.axis_index("vocab")
    hid = lax.axis_index("hid")
    steps = [(dv, dh) for dv in range(4) for dh in range(2)][1:]
    barrier = pltpu.get_barrier_semaphore()
    for dv, dh in steps:
        pl.semaphore_signal(
            barrier, inc=1, device_id={"vocab": lax.rem(voc + dv, 4), "hid": lax.rem(hid + dh, 2)},
            device_id_type=pl.DeviceIdType.MESH)
    pl.semaphore_wait(barrier, len(steps))
    copies = []
    for i, (dv, dh) in enumerate(steps):
        copy = pltpu.make_async_remote_copy(
            src_ref=st_ref,
            dst_ref=slots.at[i],
            send_sem=send_sem.at[i],
            recv_sem=recv_sem.at[i],
            device_id={"vocab": lax.rem(voc + dv, 4), "hid": lax.rem(hid + dh, 2)},
            device_id_type=pl.DeviceIdType.MESH,
        )
        copy.start()
        copies.append(copy)
    for copy in copies:
        copy.wait()
    me = voc * 2 + hid
    stats = [(me, st_ref[...])]
    for i, (dv, dh) in enumerate(steps):
        stats.append((lax.rem(voc + 4 - dv, 4) * 2 + lax.rem(hid + 2 - dh, 2), slots[i]))
    ab, at_tgt = combine(stats, me)
    ab_ref[...] = ab
    at_tgt_ref[...] = jnp.broadcast_to(at_tgt, at_tgt_ref.shape)


def exchange(st):
    return pl.pallas_call(
        exchange_kernel,
        out_shape=[jax.ShapeDtypeStruct((128, 128), jnp.float32), jax.ShapeDtypeStruct((8, 128), jnp.float32)],
        in_specs=[pl.BlockSpec(memory_space=pltpu.VMEM)],
        out_specs=[pl.BlockSpec(memory_space=pltpu.VMEM)] * 2,
        scratch_shapes=[
            pltpu.VMEM((7, 8, 128), jnp.float32),
            pltpu.SemaphoreType.DMA((7,)),
            pltpu.SemaphoreType.DMA((7,)),
        ],
        compiler_params=pltpu.CompilerParams(collective_id=0, has_side_effects=True, vmem_limit_bytes=ALL_VMEM),
        name="exchange",
    )(st)


def last_kernel(ab_ref, at_tgt_ref, ctin_ref, *refs, blk, at, rows, nparts):
    out_ref, ct_ref = refs[-2:]
    step = pl.program_id(0)
    sub = out_ref.shape[0]
    ab = ab_ref[pl.ds(pl.multiple_of(at + step * sub, sub), sub), :]
    ct_ref[...] = merged(ctin_ref[...], at_tgt_ref[...], blk, at, rows)
    for i in range(nparts):
        @pl.when(step == i)
        def _(pre_ref=refs[i]):
            out_ref[...] = pre_ref[...] * ab[:, 0:1] + ab[:, 1:2]


def finish_last(ab, at_tgt, ct, pres, out, blk, at, row0, deps):
    sub, cols = pres[0].shape
    n = len(pres)
    small = pl.BlockSpec((8, 128), lambda i: (0, 0))
    return pl.pallas_call(
        functools.partial(last_kernel, blk=blk, at=at, rows=sub * n, nparts=n),
        grid=(n,),
        out_shape=[jax.ShapeDtypeStruct(out.shape, jnp.float32), jax.ShapeDtypeStruct((8, 128), jnp.float32)],
        in_specs=[pl.BlockSpec((128, 128), lambda i: (0, 0)), small, small]
        + [pl.BlockSpec((sub, cols), lambda i: (0, 0))] * n
        + [pl.BlockSpec(memory_space=pl.ANY)] * (1 + len(deps)),
        out_specs=[pl.BlockSpec((sub, cols), lambda i: (row0 // sub + i, 0)), small],
        input_output_aliases={3 + n: 0},
        compiler_params=pltpu.CompilerParams(dimension_semantics=("arbitrary",), vmem_limit_bytes=ALL_VMEM),
        name="finish_last",
    )(ab, at_tgt, ct, *pres, out, *deps)


def solution(mesh):
    def pipeline(h, w, temp, tgt):
        rows_all = h.shape[0]
        cols = w.shape[1] // 2
        hid = lax.axis_index("hid")
        voc = lax.axis_index("vocab")
        own_half = hid.astype(jnp.int32).reshape(1)
        peer_half = (1 - hid).astype(jnp.int32).reshape(1)
        pos = jnp.stack([voc, hid]).astype(jnp.int32)
        temp2 = temp[:, None]
        tgt2 = (tgt - (voc * 2 + hid) * cols)[:, None]
        tri = (lax.broadcasted_iota(jnp.int32, (CT, CT), 0) <= lax.broadcasted_iota(jnp.int32, (CT, CT), 1)).astype(jnp.bfloat16)
        swap = [(0, 1), (1, 0)]

        blk = 128
        nblk = rows_all // blk
        last = (64, 32, 16, 16)
        tn = 7 * CT
        ht = cols // tn

        units = [(b, 0, blk) for b in range(nblk - 1)]
        units += [(nblk - 1, sum(last[:i]), r) for i, r in enumerate(last)]
        nu = len(units)
        parts = {}
        owns = {}
        tok = None

        def peer(b):
            nonlocal tok
            if b >= nblk:
                return
            splits = last if b == nblk - 1 else (blk,)
            outs = partial_products(h, w, peer_half, b * blk, splits, 0, ht, tn, ht, (tok,))
            tok = outs[0]
            for i, o in enumerate(outs):
                parts[b + i] = [o]

        def mine_half(b):
            nonlocal tok
            if b >= nblk:
                return
            tok = owns[b] = partial_products(h, w, own_half, b * blk, (blk,), 0, ht, tn, ht, (tok,))[0]

        tok = partial_products(h, w, peer_half, 0, (blk,), 0, 2, tn // 2, 2 * ht)[0]
        parts[0] = [tok]
        tok = partial_products(h, w, peer_half, 0, (blk,), 1, ht - 1, tn, ht, (tok,))[0]
        parts[0].append(tok)
        peer(1)
        peer(2)
        mine_half(0)
        mine_half(1)

        def send(arrays):
            return [lax.ppermute(a, "hid", swap) for a in arrays]

        recvs = {0: send(parts[0][:1]) + send(parts[0][1:]), 1: send(parts[1])}
        pres, stats = {}, {}
        out = None
        ct = jnp.zeros((nblk, blk), jnp.float32)

        def close(k):
            nonlocal out, ct, tok
            b, at, _ = units[k]
            out, ct = finish(pos, pres[k], *stats[k], out, ct, rows_all, b, at, b * blk + at, (tok,))
            tok = ct

        prev = None
        for k, (b, at, rows) in enumerate(units):
            pres[k], st = local_prefix(
                temp2, tgt2, tri, owns[b], at, recvs[k], rows, b * blk + at, prev, (tok,))
            tok = st
            if k == nu - 2:
                prev = st
                close(k - 1)
                continue
            if k == nu - 1:
                ab, at_tgt = exchange(st)
                at = units[k - 1][1]
                out, ct = finish_last(ab, at_tgt, ct, [pres[k - 1], pres[k]], out, b, at, b * blk + at, (tok,))
                break
            mine = lax.all_gather(st, "vocab")
            if k + 2 < nu:
                *sent, mine = lax.optimization_barrier((*parts[k + 2], mine))
                stats[k] = (st, mine, send([mine])[0])
                recvs[k + 2] = send(sent)
            tok = mine
            if k >= 1:
                close(k - 1)
            peer(k + 3)
            mine_half(k + 2)
        return out, ct.reshape(rows_all)

    return jax.shard_map(
        pipeline,
        mesh=mesh,
        in_specs=(P("data", "hid"), P("hid", "vocab"), P("data"), P("data")),
        out_specs=(P("data", ("vocab", "hid")), P("data")),
        check_vma=False,
    )
```

time: 1480 us -> 1420 us (0.959)
  blocking collectives: 95.5 us -> 64.7 us
  local copies, waits for them, and re-layouts: 26 us -> 3.36 us
    all_gather x10 -> x9, blocking collectives: 95.5 us -> 64.7 us  [pipeline(): mine = lax.all_gather(st, 'vocab')]
    ppermute x22 -> x21, waiting for transfers between devices: 726 us -> 718 us  [send(): return [lax.ppermute(a, 'hid', swap) for a in arrays]]
    pallas_call x23 -> x22, Pallas kernels: 217 us -> 217 us  [the longest x11 151 us: local_prefix(): pl.pallas_call(functools.partial(local_kernel, npieces=len(recvs), has_pr...]
  transfers between devices with their start and end apart: 22 -> 21, of which waited for: 8 -> 8; matrix products, arithmetic and copies ran while one was open for 1% -> 0% of each run, Pallas kernels for 39% -> 40%
where the time goes in v1:
time: 1420 us
  waiting for transfers between devices  718 us (51%)
  Pallas kernels  605 us (43%)
  blocking collectives  64.7 us (5%)
  starting transfers between devices  25.6 us (2%)
    ppermute x21, waiting for transfers between devices, send(): return [lax.ppermute(a, 'hid', swap) for a in arrays]  718 us
    pallas_call x17, Pallas kernels, partial_products(): pl.pallas_call(functools.partial(mm_kernel, splits=splits), out_shape=[ja...  388 us
    pallas_call x11, Pallas kernels, local_prefix(): pl.pallas_call(functools.partial(local_kernel, npieces=len(recvs), has_pr...  151 us
    all_gather x9, blocking collectives, pipeline(): mine = lax.all_gather(st, 'vocab')  64.7 us
    pallas_call x9, Pallas kernels, finish(): pl.pallas_call(functools.partial(final_kernel, blk=blk, at=at, rows=rows)...  57.5 us
  transfers between devices with their start and end apart: 21, of which 8 were waited for; matrix products, arithmetic and copies ran while one was open for 0% of the time, Pallas kernels for 40%

profile of v1, /device:TPU:0, one launch (start us, length us, event | category | flops | bytes accessed | tf_op | source)
XLA Modules:
  0.0 1420.0 jit_solution(6848038421714176320)
XLA Ops:
  6.2 20.9 %shard_map.60.refs_0_ = f32[128,10752]{1,0:T(8,128)} custom-call(s32[1]{0:T(128)} %bitcast.4.sel_ref, bf16[1024,2560]{1,0:T(8,128)(2,1)} %h_ref.33, bf16[2560,25088]{1,0:T(8,128)(2,1)} %w_ref.33, f32[128,1792]{1,0:T(8,128)} %shard_map.59.refs_0_), custom_call_target="tpu_custom_call" | custom-call | flops 7046430720 | bytes 60555264 | tf_op jit(solution)/shard_map/pallas_call | solution.py:29
  30.5 24.1 %shard_map.61.refs_0_ = f32[128,12544]{1,0:T(8,128)} custom-call(s32[1]{0:T(128)} %bitcast.4.sel_ref, bf16[1024,2560]{1,0:T(8,128)(2,1)} %h_ref.33, bf16[2560,25088]{1,0:T(8,128)(2,1)} %w_ref.33, f32[128,10752]{1,0:T(8,128)} %shard_map.60.refs_0_), custom_call_target="tpu_custom_call" | custom-call | flops 8220835840 | bytes 70647808 | tf_op jit(solution)/shard_map/pallas_call | solution.py:29
  56.5 24.1 %shard_map.62.refs_0_ = f32[128,12544]{1,0:T(8,128)} custom-call(s32[1]{0:T(128)} %bitcast.4.sel_ref, bf16[1024,2560]{1,0:T(8,128)(2,1)} %h_ref.33, bf16[2560,25088]{1,0:T(8,128)(2,1)} %w_ref.33, f32[128,12544]{1,0:T(8,128)} %shard_map.61.refs_0_), custom_call_target="tpu_custom_call" | custom-call | flops 8220835840 | bytes 70647808 | tf_op jit(solution)/shard_map/pallas_call | solution.py:29
  80.6 24.1 %shard_map.63.refs_0_.own_ref = f32[128,12544]{1,0:T(8,128)} custom-call(s32[1]{0:T(128)} %bitcast.2.sel_ref, bf16[1024,2560]{1,0:T(8,128)(2,1)} %h_ref.33, bf16[2560,25088]{1,0:T(8,128)(2,1)} %w_ref.33, f32[128,12544]{1,0:T(8,128)} %shard_map.62.refs_0_), custom_call_target="tpu_custom_call" | custom-call | flops 8220835840 | bytes 70647808 | tf_op jit(solution)/shard_map/pallas_call | solution.py:29
  108.9 24.2 %shard_map.64.refs_2_.own_ref = f32[128,12544]{1,0:T(8,128)} custom-call(s32[1]{0:T(128)} %bitcast.2.sel_ref, bf16[1024,2560]{1,0:T(8,128)(2,1)} %h_ref.33, bf16[2560,25088]{1,0:T(8,128)(2,1)} %w_ref.33, f32[128,12544]{1,0:T(8,128)} %shard_map.63.refs_0_.own_ref), custom_call_target="tpu_custom_call" | custom-call | flops 8220835840 | bytes 70647808 | tf_op jit(solution)/shard_map/pallas_call | solution.py:29
  133.0 36.9 %collective-permute-done.1.refs_0_ = f32[128,1792]{1,0:T(8,128)} collective-permute-done((f32[128,1792]{1,0:T(8,128)}, f32[128,1792]{1,0:T(8,128)}, u32[]{:S(2)}, u32[]{:S(2)}) %collective-permute-start.1) | collective-permute-done | bytes 917536 | tf_op jit(solution)/shard_map/ppermute | solution.py:354
  198.2 24.1 %shard_map.66.refs_0_ = f32[128,12544]{1,0:T(8,128)} custom-call(s32[1]{0:T(128)} %bitcast.4.sel_ref, bf16[1024,2560]{1,0:T(8,128)(2,1)} %h_ref.33, bf16[2560,25088]{1,0:T(8,128)(2,1)} %w_ref.33, f32[4,8,128]{2,1,0:T(8,128)} %bitcast.5.refs_0_.mine_ref), custom_call_target="tpu_custom_call" | custom-call | flops 8220835840 | bytes 70647808 | tf_op jit(solution)/shard_map/pallas_call | solution.py:29
  222.3 24.1 %shard_map.67.refs_1_.own_ref = f32[128,12544]{1,0:T(8,128)} custom-call(s32[1]{0:T(128)} %bitcast.2.sel_ref, bf16[1024,2560]{1,0:T(8,128)(2,1)} %h_ref.33, bf16[2560,25088]{1,0:T(8,128)(2,1)} %w_ref.33, f32[128,12544]{1,0:T(8,128)} %shard_map.66.refs_0_), custom_call_target="tpu_custom_call" | custom-call | flops 8220835840 | bytes 70647808 | tf_op jit(solution)/shard_map/pallas_call | solution.py:29
  246.4 61.2 %collective-permute-done.refs_0_ = f32[128,12544]{1,0:T(8,128)} collective-permute-done((f32[128,12544]{1,0:T(8,128)}, f32[128,12544]{1,0:T(8,128)}, u32[]{:S(2)}, u32[]{:S(2)}) %collective-permute-start) | collective-permute-done | bytes 6422560 | tf_op jit(solution)/shard_map/ppermute | solution.py:354
  334.6 111.0 %collective-permute-done.4.other_ref = f32[4,8,128]{2,1,0:T(8,128)} collective-permute-done((f32[4,8,128]{2,1,0:T(8,128)}, f32[4,8,128]{2,1,0:T(8,128)}, u32[]{:S(2)}, u32[]{:S(2)}) %collective-permute-start.4) | collective-permute-done | bytes 16416 | tf_op jit(solution)/shard_map/ppermute | solution.py:354
  453.2 24.1 %shard_map.70.refs_0_ = f32[128,12544]{1,0:T(8,128)} custom-call(s32[1]{0:T(128)} %bitcast.4.sel_ref, bf16[1024,2560]{1,0:T(8,128)(2,1)} %h_ref.33, bf16[2560,25088]{1,0:T(8,128)(2,1)} %w_ref.33, f32[8,128]{1,0:T(8,128)} %get-tuple-element.74.refs_0_.ctin_ref), custom_call_target="tpu_custom_call" | custom-call | flops 8220835840 | bytes 70647808 | tf_op jit(solution)/shard_map/pallas_call | solution.py:29
  477.3 24.1 %shard_map.71.refs_1_.own_ref = f32[128,12544]{1,0:T(8,128)} custom-call(s32[1]{0:T(128)} %bitcast.2.sel_ref, bf16[1024,2560]{1,0:T(8,128)(2,1)} %h_ref.33, bf16[2560,25088]{1,0:T(8,128)(2,1)} %w_ref.33, f32[128,12544]{1,0:T(8,128)} %shard_map.70.refs_0_), custom_call_target="tpu_custom_call" | custom-call | flops 8220835840 | bytes 70647808 | tf_op jit(solution)/shard_map/pallas_call | solution.py:29
  530.2 190.2 %collective-permute-done.3.other_ref = f32[4,8,128]{2,1,0:T(8,128)} collective-permute-done((f32[4,8,128]{2,1,0:T(8,128)}, f32[4,8,128]{2,1,0:T(8,128)}, u32[]{:S(2)}, u32[]{:S(2)}) %collective-permute-start.3) | collective-permute-done | bytes 16416 | tf_op jit(solution)/shard_map/ppermute | solution.py:354
  727.6 24.1 %shard_map.74.refs_0_ = f32[128,12544]{1,0:T(8,128)} custom-call(s32[1]{0:T(128)} %bitcast.4.sel_ref, bf16[1024,2560]{1,0:T(8,128)(2,1)} %h_ref.33, bf16[2560,25088]{1,0:T(8,128)(2,1)} %w_ref.33, f32[8,128]{1,0:T(8,128)} %get-tuple-element.79.refs_0_.ctin_ref), custom_call_target="tpu_custom_call" | custom-call | flops 8220835840 | bytes 70647808 | tf_op jit(solution)/shard_map/pallas_call | solution.py:29
  751.7 24.1 %shard_map.75.refs_1_.own_ref = f32[128,12544]{1,0:T(8,128)} custom-call(s32[1]{0:T(128)} %bitcast.2.sel_ref, bf16[1024,2560]{1,0:T(8,128)(2,1)} %h_ref.33, bf16[2560,25088]{1,0:T(8,128)(2,1)} %w_ref.33, f32[128,12544]{1,0:T(8,128)} %shard_map.74.refs_0_), custom_call_target="tpu_custom_call" | custom-call | flops 8220835840 | bytes 70647808 | tf_op jit(solution)/shard_map/pallas_call | solution.py:29
  809.4 24.1 %shard_map.78.refs_0_ = f32[128,12544]{1,0:T(8,128)} custom-call(s32[1]{0:T(128)} %bitcast.4.sel_ref, bf16[1024,2560]{1,0:T(8,128)(2,1)} %h_ref.33, bf16[2560,25088]{1,0:T(8,128)(2,1)} %w_ref.33, f32[8,128]{1,0:T(8,128)} %get-tuple-element.86.refs_0_.ctin_ref), custom_call_target="tpu_custom_call" | custom-call | flops 8220835840 | bytes 70647808 | tf_op jit(solution)/shard_map/pallas_call | solution.py:29
  833.5 24.1 %shard_map.79.refs_1_.own_ref = f32[128,12544]{1,0:T(8,128)} custom-call(s32[1]{0:T(128)} %bitcast.2.sel_ref, bf16[1024,2560]{1,0:T(8,128)(2,1)} %h_ref.33, bf16[2560,25088]{1,0:T(8,128)(2,1)} %w_ref.33, f32[128,12544]{1,0:T(8,128)} %shard_map.78.refs_0_), custom_call_target="tpu_custom_call" | custom-call | flops 8220835840 | bytes 70647808 | tf_op jit(solution)/shard_map/pallas_call | solution.py:29
  884.1 195.6 %collective-permute-done.10.other_ref = f32[4,8,128]{2,1,0:T(8,128)} collective-permute-done((f32[4,8,128]{2,1,0:T(8,128)}, f32[4,8,128]{2,1,0:T(8,128)}, u32[]{:S(2)}, u32[]{:S(2)}) %collective-permute-start.10) | collective-permute-done | bytes 16416 | tf_op jit(solution)/shard_map/ppermute | solution.py:354
  1086.8 24.1 %shard_map.82 = (f32[64,12544]{1,0:T(8,128)}, f32[32,12544]{1,0:T(8,128)}, f32[16,12544]{1,0:T(8,128)}, f32[16,12544]{1,0:T(8,128)}) custom-call(s32[1]{0:T(128)} %bitcast.4.sel_ref, bf16[1024,2560]{1,0:T(8,128)(2,1)} %h_ref.33, bf16[2560,25088]{1,0:T(8,128)(2,1)} %w_ref.33, f32[8,128]{1,0:T(8,128)} %get-tuple-element.92.refs_0_.ctin_ref), custom_call_target="tpu_custom_call" | custom-call | flops 8220835840 | bytes 70647808 | tf_op jit(solution)/shard_map/pallas_call | solution.py:29
  1110.9 24.1 %shard_map.83.refs_1_.own_ref = f32[128,12544]{1,0:T(8,128)} custom-call(s32[1]{0:T(128)} %bitcast.2.sel_ref, bf16[1024,2560]{1,0:T(8,128)(2,1)} %h_ref.33, bf16[2560,25088]{1,0:T(8,128)(2,1)} %w_ref.33, f32[64,12544]{1,0:T(8,128)} %get-tuple-element.111.refs_0_), custom_call_target="tpu_custom_call" | custom-call | flops 8220835840 | bytes 70647808 | tf_op jit(solution)/shard_map/pallas_call | solution.py:29
  1161.3 70.2 %collective-permute-done.9.other_ref = f32[4,8,128]{2,1,0:T(8,128)} collective-permute-done((f32[4,8,128]{2,1,0:T(8,128)}, f32[4,8,128]{2,1,0:T(8,128)}, u32[]{:S(2)}, u32[]{:S(2)}) %collective-permute-start.9) | collective-permute-done | bytes 16416 | tf_op jit(solution)/shard_map/ppermute | solution.py:354
  1238.6 24.1 %shard_map.86.refs_1_.own_ref = f32[128,12544]{1,0:T(8,128)} custom-call(s32[1]{0:T(128)} %bitcast.2.sel_ref, bf16[1024,2560]{1,0:T(8,128)(2,1)} %h_ref.33, bf16[2560,25088]{1,0:T(8,128)(2,1)} %w_ref.33, f32[8,128]{1,0:T(8,128)} %get-tuple-element.98.refs_0_.ctin_ref), custom_call_target="tpu_custom_call" | custom-call | flops 8220835840 | bytes 70647808 | tf_op jit(solution)/shard_map/pallas_call | solution.py:29
  1290.9 34.7 %collective-permute-done.15.other_ref = f32[4,8,128]{2,1,0:T(8,128)} collective-permute-done((f32[4,8,128]{2,1,0:T(8,128)}, f32[4,8,128]{2,1,0:T(8,128)}, u32[]{:S(2)}, u32[]{:S(2)}) %collective-permute-start.15) | collective-permute-done | bytes 16416 | tf_op jit(solution)/shard_map/ppermute | solution.py:354
  1374.4 18.5 %collective-permute-done.19.other_ref = f32[4,8,128]{2,1,0:T(8,128)} collective-permute-done((f32[4,8,128]{2,1,0:T(8,128)}, f32[4,8,128]{2,1,0:T(8,128)}, u32[]{:S(2)}, u32[]{:S(2)}) %collective-permute-start.19) | collective-permute-done | bytes 16416 | tf_op jit(solution)/shard_map/ppermute | solution.py:354
  (72 shorter events, 318.6 us)
Async XLA Ops:
  27.1 142.8 %collective-permute-start.2 = (f32[128,10752]{1,0:T(8,128)}, f32[128,10752]{1,0:T(8,128)}, u32[]{:S(2)}, u32[]{:S(2)}) collective-permute-start(f32[128,10752]{1,0:T(8,128)} %shard_map.60.refs_0_), channel_id=1, source_target_pairs={{0,4},{4,0},{1,5},{5,1},{2,6},{6,2},{3,7},{7,3}} | collective-permute-start | bytes 16515080 | tf_op jit(solution)/shard_map/ppermute | solution.py:354
  30.5 139.5 %collective-permute-start.1 = (f32[128,1792]{1,0:T(8,128)}, f32[128,1792]{1,0:T(8,128)}, u32[]{:S(2)}, u32[]{:S(2)}) collective-permute-start(f32[128,1792]{1,0:T(8,128)} %shard_map.59.refs_0_), channel_id=1, source_target_pairs={{0,4},{4,0},{1,5},{5,1},{2,6},{6,2},{3,7},{7,3}} | collective-permute-start | bytes 2752520 | tf_op jit(solution)/shard_map/ppermute | solution.py:354
  54.5 253.0 %collective-permute-start = (f32[128,12544]{1,0:T(8,128)}, f32[128,12544]{1,0:T(8,128)}, u32[]{:S(2)}, u32[]{:S(2)}) collective-permute-start(f32[128,12544]{1,0:T(8,128)} %shard_map.61.refs_0_), channel_id=1, source_target_pairs={{0,4},{4,0},{1,5},{5,1},{2,6},{6,2},{3,7},{7,3}} | collective-permute-start | bytes 19267592 | tf_op jit(solution)/shard_map/ppermute | solution.py:354
  195.5 306.0 %collective-permute-start.5 = (f32[128,12544]{1,0:T(8,128)}, f32[128,12544]{1,0:T(8,128)}, u32[]{:S(2)}, u32[]{:S(2)}) collective-permute-start(f32[128,12544]{1,0:T(8,128)} %shard_map.62.refs_0_), channel_id=1, source_target_pairs={{0,4},{4,0},{1,5},{5,1},{2,6},{6,2},{3,7},{7,3}} | collective-permute-start | bytes 19267592 | tf_op jit(solution)/shard_map/ppermute | solution.py:354
  197.6 247.9 %collective-permute-start.4 = (f32[4,8,128]{2,1,0:T(8,128)}, f32[4,8,128]{2,1,0:T(8,128)}, u32[]{:S(2)}, u32[]{:S(2)}) collective-permute-start(f32[4,8,128]{2,1,0:T(8,128)} %bitcast.5.refs_0_.mine_ref), channel_id=1, source_target_pairs={{0,4},{4,0},{1,5},{5,1},{2,6},{6,2},{3,7},{7,3}} | collective-permute-start | bytes 49160 | tf_op jit(solution)/shard_map/ppermute | solution.py:354
  333.0 442.7 %collective-permute-start.8 = (f32[128,12544]{1,0:T(8,128)}, f32[128,12544]{1,0:T(8,128)}, u32[]{:S(2)}, u32[]{:S(2)}) collective-permute-start(f32[128,12544]{1,0:T(8,128)} %shard_map.66.refs_0_), channel_id=1, source_target_pairs={{0,4},{4,0},{1,5},{5,1},{2,6},{6,2},{3,7},{7,3}} | collective-permute-start | bytes 19267592 | tf_op jit(solution)/shard_map/ppermute | solution.py:354
  526.7 330.9 %collective-permute-start.6 = (f32[128,12544]{1,0:T(8,128)}, f32[128,12544]{1,0:T(8,128)}, u32[]{:S(2)}, u32[]{:S(2)}) collective-permute-start(f32[128,12544]{1,0:T(8,128)} %shard_map.70.refs_0_), channel_id=1, source_target_pairs={{0,4},{4,0},{1,5},{5,1},{2,6},{6,2},{3,7},{7,3}} | collective-permute-start | bytes 19267592 | tf_op jit(solution)/shard_map/ppermute | solution.py:354
  528.2 192.3 %collective-permute-start.3 = (f32[4,8,128]{2,1,0:T(8,128)}, f32[4,8,128]{2,1,0:T(8,128)}, u32[]{:S(2)}, u32[]{:S(2)}) collective-permute-start(f32[4,8,128]{2,1,0:T(8,128)} %bitcast.25), channel_id=1, source_target_pairs={{0,4},{4,0},{1,5},{5,1},{2,6},{6,2},{3,7},{7,3}} | collective-permute-start | bytes 49160 | tf_op jit(solution)/shard_map/ppermute | solution.py:354
  528.7 273.6 %collective-permute-start.7 = (f32[4,8,128]{2,1,0:T(8,128)}, f32[4,8,128]{2,1,0:T(8,128)}, u32[]{:S(2)}, u32[]{:S(2)}) collective-permute-start(f32[4,8,128]{2,1,0:T(8,128)} %bitcast.7.refs_1_.mine_ref), channel_id=1, source_target_pairs={{0,4},{4,0},{1,5},{5,1},{2,6},{6,2},{3,7},{7,3}} | collective-permute-start | bytes 49160 | tf_op jit(solution)/shard_map/ppermute | solution.py:354
  800.8 334.2 %collective-permute-start.11 = (f32[128,12544]{1,0:T(8,128)}, f32[128,12544]{1,0:T(8,128)}, u32[]{:S(2)}, u32[]{:S(2)}) collective-permute-start(f32[128,12544]{1,0:T(8,128)} %shard_map.74.refs_0_), channel_id=1, source_target_pairs={{0,4},{4,0},{1,5},{5,1},{2,6},{6,2},{3,7},{7,3}} | collective-permute-start | bytes 19267592 | tf_op jit(solution)/shard_map/ppermute | solution.py:354
  882.1 380.6 %collective-permute-start.12 = (f32[128,12544]{1,0:T(8,128)}, f32[128,12544]{1,0:T(8,128)}, u32[]{:S(2)}, u32[]{:S(2)}) collective-permute-start(f32[128,12544]{1,0:T(8,128)} %shard_map.78.refs_0_), channel_id=1, source_target_pairs={{0,4},{4,0},{1,5},{5,1},{2,6},{6,2},{3,7},{7,3}} | collective-permute-start | bytes 19267592 | tf_op jit(solution)/shard_map/ppermute | solution.py:354
  882.6 197.1 %collective-permute-start.10 = (f32[4,8,128]{2,1,0:T(8,128)}, f32[4,8,128]{2,1,0:T(8,128)}, u32[]{:S(2)}, u32[]{:S(2)}) collective-permute-start(f32[4,8,128]{2,1,0:T(8,128)} %bitcast.28), channel_id=1, source_target_pairs={{0,4},{4,0},{1,5},{5,1},{2,6},{6,2},{3,7},{7,3}} | collective-permute-start | bytes 49160 | tf_op jit(solution)/shard_map/ppermute | solution.py:354
  1159.3 173.4 %collective-permute-start.16 = (f32[64,12544]{1,0:T(8,128)}, f32[64,12544]{1,0:T(8,128)}, u32[]{:S(2)}, u32[]{:S(2)}) collective-permute-start(f32[64,12544]{1,0:T(8,128)} %get-tuple-element.111.refs_0_), channel_id=1, source_target_pairs={{0,4},{4,0},{1,5},{5,1},{2,6},{6,2},{3,7},{7,3}} | collective-permute-start | bytes 9633800 | tf_op jit(solution)/shard_map/ppermute | solution.py:354
  1160.8 70.7 %collective-permute-start.9 = (f32[4,8,128]{2,1,0:T(8,128)}, f32[4,8,128]{2,1,0:T(8,128)}, u32[]{:S(2)}, u32[]{:S(2)}) collective-permute-start(f32[4,8,128]{2,1,0:T(8,128)} %bitcast.19), channel_id=1, source_target_pairs={{0,4},{4,0},{1,5},{5,1},{2,6},{6,2},{3,7},{7,3}} | collective-permute-start | bytes 49160 | tf_op jit(solution)/shard_map/ppermute | solution.py:354
  1287.3 71.0 %collective-permute-start.13 = (f32[32,12544]{1,0:T(8,128)}, f32[32,12544]{1,0:T(8,128)}, u32[]{:S(2)}, u32[]{:S(2)}) collective-permute-start(f32[32,12544]{1,0:T(8,128)} %get-tuple-element.103), channel_id=1, source_target_pairs={{0,4},{4,0},{1,5},{5,1},{2,6},{6,2},{3,7},{7,3}} | collective-permute-start | bytes 4816904 | tf_op jit(solution)/shard_map/ppermute | solution.py:354
  1288.8 36.7 %collective-permute-start.15 = (f32[4,8,128]{2,1,0:T(8,128)}, f32[4,8,128]{2,1,0:T(8,128)}, u32[]{:S(2)}, u32[]{:S(2)}) collective-permute-start(f32[4,8,128]{2,1,0:T(8,128)} %bitcast.22), channel_id=1, source_target_pairs={{0,4},{4,0},{1,5},{5,1},{2,6},{6,2},{3,7},{7,3}} | collective-permute-start | bytes 49160 | tf_op jit(solution)/shard_map/ppermute | solution.py:354
  1289.3 61.8 %collective-permute-start.14 = (f32[4,8,128]{2,1,0:T(8,128)}, f32[4,8,128]{2,1,0:T(8,128)}, u32[]{:S(2)}, u32[]{:S(2)}) collective-permute-start(f32[4,8,128]{2,1,0:T(8,128)} %bitcast.11.refs_1_.mine_ref), channel_id=1, source_target_pairs={{0,4},{4,0},{1,5},{5,1},{2,6},{6,2},{3,7},{7,3}} | collective-permute-start | bytes 49160 | tf_op jit(solution)/shard_map/ppermute | solution.py:354
  1349.7 47.4 %collective-permute-start.18 = (f32[16,12544]{1,0:T(8,128)}, f32[16,12544]{1,0:T(8,128)}, u32[]{:S(2)}, u32[]{:S(2)}) collective-permute-start(f32[16,12544]{1,0:T(8,128)} %get-tuple-element.117), channel_id=1, source_target_pairs={{0,4},{4,0},{1,5},{5,1},{2,6},{6,2},{3,7},{7,3}} | collective-permute-start | bytes 2408456 | tf_op jit(solution)/shard_map/ppermute | solution.py:354
  1371.9 34.0 %collective-permute-start.17 = (f32[16,12544]{1,0:T(8,128)}, f32[16,12544]{1,0:T(8,128)}, u32[]{:S(2)}, u32[]{:S(2)}) collective-permute-start(f32[16,12544]{1,0:T(8,128)} %get-tuple-element.116), channel_id=1, source_target_pairs={{0,4},{4,0},{1,5},{5,1},{2,6},{6,2},{3,7},{7,3}} | collective-permute-start | bytes 2408456 | tf_op jit(solution)/shard_map/ppermute | solution.py:354
  1372.4 20.5 %collective-permute-start.19 = (f32[4,8,128]{2,1,0:T(8,128)}, f32[4,8,128]{2,1,0:T(8,128)}, u32[]{:S(2)}, u32[]{:S(2)}) collective-permute-start(f32[4,8,128]{2,1,0:T(8,128)} %bitcast.16), channel_id=1, source_target_pairs={{0,4},{4,0},{1,5},{5,1},{2,6},{6,2},{3,7},{7,3}} | collective-permute-start | bytes 49160 | tf_op jit(solution)/shard_map/ppermute | solution.py:354
  1373.9 28.4 %collective-permute-start.20 = (f32[4,8,128]{2,1,0:T(8,128)}, f32[4,8,128]{2,1,0:T(8,128)}, u32[]{:S(2)}, u32[]{:S(2)}) collective-permute-start(f32[4,8,128]{2,1,0:T(8,128)} %bitcast.13.refs_1_.mine_ref), channel_id=1, source_target_pairs={{0,4},{4,0},{1,5},{5,1},{2,6},{6,2},{3,7},{7,3}} | collective-permute-start | bytes 49160 | tf_op jit(solution)/shard_map/ppermute | solution.py:354

commit v2 on v1

--- a/solution.py
+++ b/solution.py
@@ -44,28 +44,39 @@
     )(half, h, w, *deps)
 
 
-def local_kernel(temp_ref, tgt_ref, tri_ref, own_ref, *refs, npieces, has_prev, skip, at, group):
+def local_kernel(temp_ref, tgt_ref, tri_ref, own_ref, *refs, npieces, has_prev, skip, at, group, share):
     recv_refs = refs[:npieces]
     prev_ref = refs[npieces] if has_prev else None
-    pre_ref, st_ref, z_s, hi_s, mid_s, lo_s, st_s = refs[npieces + has_prev + skip:]
+    if share:
+        pre_ref, ab_ref, at_tgt_ref, z_s, hi_s, mid_s, lo_s, st_s, st_ref, slots, send_sem, recv_sem = refs[npieces + has_prev + skip:]
+        announce()
+    else:
+        pre_ref, st_ref, z_s, hi_s, mid_s, lo_s, st_s = refs[npieces + has_prev + skip:]
     step, nsteps = pl.program_id(0), pl.num_programs(0)
     rows = own_ref.shape[0]
     nt = own_ref.shape[1] // CT
     temp = jnp.broadcast_to(temp_ref[...], (rows, CT))
     mx = jnp.full((rows, CT), -jnp.inf, jnp.float32)
-    t0 = 0
-    for ref in recv_refs:
-        n = ref.shape[1] // CT
-
-        def max_step(j, mx, ref=ref, t0=t0):
-            src = pl.ds(pl.multiple_of(j * CT, CT), CT)
-            dst = pl.ds(pl.multiple_of((t0 + j) * CT, CT), CT)
-            z = (own_ref[:, dst] + ref[:, src]) * temp
-            z_s[t0 + j] = z
-            return jnp.maximum(mx, z)
-
-        mx = lax.fori_loop(0, n, max_step, mx, unroll=7)
-        t0 += n
+
+    def add_tile(t, part, mx):
+        z = (own_ref[:, pl.ds(pl.multiple_of(t * CT, CT), CT)] + part) * temp
+        z_s[t] = z
+        return jnp.maximum(mx, z)
+
+    t0 = off = 0
+    for i, ref in enumerate(recv_refs):
+        n, rest = divmod(ref.shape[1] - off, CT)
+
+        def max_step(j, mx, ref=ref, t0=t0, off=off):
+            return add_tile(t0 + j, ref[:, pl.ds(pl.multiple_of(off + j * CT, 128), CT)], mx)
+
+        mx = lax.fori_loop(0, n, max_step, mx, unroll=max(u for u in range(1, 8) if n % u == 0))
+        t0, off = t0 + n, 0
+        if rest:
+            off = CT - rest
+            both = jnp.concatenate([ref[:, ref.shape[1] - rest:], recv_refs[i + 1][:, :off]], axis=1)
+            mx = add_tile(t0, both, mx)
+            t0 += 1
     m = jnp.max(mx, axis=1, keepdims=True)
     mb = jnp.broadcast_to(m, (rows, CT))
     tgt = jnp.broadcast_to(tgt_ref[...], (rows, CT))
@@ -102,6 +113,8 @@
         st = st_s[...].T[0:8]
         st_ref[...] = st + prev_ref[...] if has_prev else st
 
+    if share:
+        copies = spread(st_ref, slots, send_sem, recv_sem)
     tri = tri_ref[...]
 
     def prefix_step(g, carry):
@@ -117,53 +130,142 @@
         return carry
 
     lax.fori_loop(0, nt // group, prefix_step, zero)
-
-
-def local_prefix(temp, tgt, tri, own, at, recvs, rows, row0, prev, deps):
+    if share:
+        gather(copies, st_ref, slots, ab_ref, at_tgt_ref)
+
+
+def local_prefix(temp, tgt, tri, own, at, recvs, rows, row0, prev, deps, share=False):
     cols = own.shape[1]
     nt = cols // CT
     sub = min(SUB, rows)
+    small = (128, 8) if share else (8,)
     extra = ([] if prev is None else [prev]) + list(deps)
     extra_specs = ([] if prev is None else [pl.BlockSpec((8, 128), lambda i: (0, 0))])
     extra_specs += [pl.BlockSpec(memory_space=pl.ANY)] * len(deps)
     return pl.pallas_call(
         functools.partial(
-            local_kernel, npieces=len(recvs), has_prev=int(prev is not None), skip=len(deps), at=at, group=7),
+            local_kernel, npieces=len(recvs), has_prev=int(prev is not None), skip=len(deps), at=at, group=7, share=share),
         grid=(rows // sub,),
-        out_shape=[jax.ShapeDtypeStruct((rows, cols), jnp.float32), jax.ShapeDtypeStruct((8, 128), jnp.float32)],
+        out_shape=[jax.ShapeDtypeStruct((rows, cols), jnp.float32)]
+        + [jax.ShapeDtypeStruct((n, 128), jnp.float32) for n in small],
         in_specs=[
             pl.BlockSpec((sub, 1), lambda i: (row0 // sub + i, 0)),
             pl.BlockSpec((sub, 1), lambda i: (row0 // sub + i, 0)),
             pl.BlockSpec((CT, CT), lambda i: (0, 0)),
             pl.BlockSpec((sub, cols), lambda i: (at // sub + i, 0)),
         ] + [pl.BlockSpec((sub, r.shape[1]), lambda i: (i, 0)) for r in recvs] + extra_specs,
-        out_specs=[pl.BlockSpec((sub, cols), lambda i: (i, 0)), pl.BlockSpec((8, 128), lambda i: (0, 0))],
+        out_specs=[pl.BlockSpec((sub, cols), lambda i: (i, 0))]
+        + [pl.BlockSpec((n, 128), lambda i: (0, 0)) for n in small],
         scratch_shapes=[
             pltpu.VMEM((nt, sub, CT), jnp.float32),
             pltpu.VMEM((nt, sub, CT), jnp.bfloat16),
             pltpu.VMEM((nt, sub, CT), jnp.bfloat16),
             pltpu.VMEM((nt, sub, CT), jnp.bfloat16),
             pltpu.VMEM((128, 128), jnp.float32),
-        ],
+        ] + ([
+            pltpu.VMEM((8, 128), jnp.float32),
+            pltpu.VMEM((7, 8, 128), jnp.float32),
+            pltpu.SemaphoreType.DMA((7,)),
+            pltpu.SemaphoreType.DMA((7,)),
+        ] if share else []),
         cost_estimate=pl.CostEstimate(
             flops=6 * rows * cols * CT, bytes_accessed=rows * cols * 12, transcendentals=rows * cols),
-        compiler_params=pltpu.CompilerParams(dimension_semantics=("arbitrary",), vmem_limit_bytes=ALL_VMEM),
+        compiler_params=pltpu.CompilerParams(
+            dimension_semantics=("arbitrary",), vmem_limit_bytes=ALL_VMEM,
+            **(dict(collective_id=0, has_side_effects=True) if share else {})),
     )(temp, tgt, tri, own, *recvs, *extra)
 
 
-def combine(stats, me):
-    top = functools.reduce(jnp.maximum, [st[0:1] for _, st in stats])
-    total = below = at_tgt = jnp.zeros_like(top)
-    scale = jnp.exp(stats[0][1][0:1] - top)
-    for index, st in stats:
+STEPS = [(dv, dh) for dv in range(4) for dh in range(2)][1:]
+
+
+def device(dv, dh):
+    return {"vocab": lax.rem(lax.axis_index("vocab") + dv, 4), "hid": lax.rem(lax.axis_index("hid") + dh, 2)}
+
+
+def announce():
+    barrier = pltpu.get_barrier_semaphore()
+    for dv, dh in STEPS:
+        pl.semaphore_signal(barrier, inc=1, device_id=device(dv, dh), device_id_type=pl.DeviceIdType.MESH)
+
+
+def spread(st_ref, slots, send_sem, recv_sem):
+    pl.semaphore_wait(pltpu.get_barrier_semaphore(), len(STEPS))
+    copies = []
+    for i, (dv, dh) in enumerate(STEPS):
+        copy = pltpu.make_async_remote_copy(
+            src_ref=st_ref,
+            dst_ref=slots.at[i],
+            send_sem=send_sem.at[i],
+            recv_sem=recv_sem.at[i],
+            device_id=device(dv, dh),
+            device_id_type=pl.DeviceIdType.MESH,
+        )
+        copy.start()
+        copies.append(copy)
+    return copies
+
+
+def gather(copies, st_ref, slots, ab_ref, at_tgt_ref):
+    for copy in copies:
+        copy.wait()
+    voc = lax.axis_index("vocab")
+    hid = lax.axis_index("hid")
+    me = voc * 2 + hid
+    stats = []
+    for i, (dv, dh) in enumerate(STEPS):
+        index = lax.rem(voc + 4 - dv, 4) * 2 + lax.rem(hid + 2 - dh, 2)
+        st = slots[i]
+        stats.append((st, jnp.where(index < me, st[1:2], 0.0)))
+    ab, at_tgt = combine(st_ref[...], stats)
+    ab_ref[...] = ab
+    at_tgt_ref[...] = jnp.broadcast_to(at_tgt, at_tgt_ref.shape)
+
+
+def combine(own, others):
+    top = functools.reduce(jnp.maximum, [st[0:1] for st, _ in others], own[0:1])
+    scale = jnp.exp(own[0:1] - top)
+    total = own[1:2] * scale
+    at_tgt = own[2:3] * scale
+    below = jnp.zeros_like(top)
+    for st, lower in others:
         f = jnp.exp(st[0:1] - top)
-        s = st[1:2] * f
-        total += s
+        total += st[1:2] * f
         at_tgt += st[2:3] * f
-        below += jnp.where(index < me, s, 0.0)
+        below += lower * f
     inv = 1.0 / total
     first = lax.broadcasted_iota(jnp.int32, (128, 128), 0) == 0
     return jnp.where(first, scale * inv, below * inv).T, at_tgt * inv
+
+
+def group_kernel(pos_ref, mine_ref, group_ref):
+    voc, hid = pos_ref[0], pos_ref[1]
+    nv = mine_ref.shape[0]
+    top = functools.reduce(jnp.maximum, [mine_ref[v, 0:1] for v in range(nv)])
+    total = at_tgt = below = jnp.zeros_like(top)
+    for v in range(nv):
+        f = jnp.exp(mine_ref[v, 0:1] - top)
+        s = mine_ref[v, 1:2] * f
+        total += s
+        at_tgt += mine_ref[v, 2:3] * f
+        below += jnp.where((v < voc) | ((v == voc) & (hid == 0)), s, 0.0)
+    row = lax.broadcasted_iota(jnp.int32, group_ref.shape, 0)
+    group_ref[...] = jnp.where(row == 0, top, jnp.where(row == 1, total, jnp.where(row == 2, at_tgt, below)))
+
+
+def group_stats(pos, mine):
+    return pl.pallas_call(
+        group_kernel,
+        out_shape=jax.ShapeDtypeStruct(mine.shape[1:], jnp.float32),
+        grid_spec=pltpu.PrefetchScalarGridSpec(
+            num_scalar_prefetch=1,
+            grid=(1,),
+            in_specs=[pl.BlockSpec(mine.shape, lambda i, s: (0, 0, 0))],
+            out_specs=pl.BlockSpec(mine.shape[1:], lambda i, s: (0, 0)),
+        ),
+        compiler_params=pltpu.CompilerParams(dimension_semantics=("arbitrary",), vmem_limit_bytes=ALL_VMEM),
+        name="group_stats",
+    )(pos, mine)
 
 
 def merged(ct, at_tgt, blk, at, rows):
@@ -179,16 +281,15 @@
 
     @pl.when(step == 0)
     def _():
-        voc, hid = pos_ref[0], pos_ref[1]
-        nv = mine_ref.shape[0]
-        me = voc * 2 + hid
+        voc = pos_ref[0]
         own = st_ref[...]
-        stats = [(me, own)]
-        real = lax.broadcasted_iota(jnp.int32, own.shape, 0) == 0
-        for v in range(nv):
-            stats.append((v * 2 + hid, jnp.where(real | (v != voc), mine_ref[v], 0.0)))
-            stats.append((v * 2 + 1 - hid, other_ref[v]))
-        ab, at_tgt = combine(stats, me)
+        others = []
+        row = lax.broadcasted_iota(jnp.int32, own.shape, 0)
+        for v in range(mine_ref.shape[0]):
+            st = jnp.where((row == 0) | (v != voc), mine_ref[v], 0.0)
+            others.append((st, jnp.where(v < voc, st[1:2], 0.0)))
+        others.append((other_ref[...], other_ref[3:4]))
+        ab, at_tgt = combine(own, others)
         ab_s[...] = ab
         ct_ref[...] = merged(ctin_ref[...], at_tgt, blk, at, rows)
 
@@ -208,7 +309,7 @@
         grid_spec=pltpu.PrefetchScalarGridSpec(
             num_scalar_prefetch=1,
             grid=(rows // sub,),
-            in_specs=[pl.BlockSpec((sub, cols), lambda i, s: (i, 0)), small, wide, wide, small]
+            in_specs=[pl.BlockSpec((sub, cols), lambda i, s: (i, 0)), small, wide, small, small]
             + [pl.BlockSpec(memory_space=pl.ANY)] * len(tail),
             out_specs=[pl.BlockSpec((sub, cols), lambda i, s: (row0 // sub + i, 0)), small],
             scratch_shapes=[pltpu.VMEM((128, 128), jnp.float32)],
@@ -217,55 +318,6 @@
         cost_estimate=pl.CostEstimate(flops=64 * rows * cols, bytes_accessed=rows * cols * 8, transcendentals=0),
         compiler_params=pltpu.CompilerParams(dimension_semantics=("arbitrary",), vmem_limit_bytes=ALL_VMEM),
     )(pos, pre, st, mine, other, ct, *tail)
-
-
-def exchange_kernel(st_ref, ab_ref, at_tgt_ref, slots, send_sem, recv_sem):
-    voc = lax.axis_index("vocab")
-    hid = lax.axis_index("hid")
-    steps = [(dv, dh) for dv in range(4) for dh in range(2)][1:]
-    barrier = pltpu.get_barrier_semaphore()
-    for dv, dh in steps:
-        pl.semaphore_signal(
-            barrier, inc=1, device_id={"vocab": lax.rem(voc + dv, 4), "hid": lax.rem(hid + dh, 2)},
-            device_id_type=pl.DeviceIdType.MESH)
-    pl.semaphore_wait(barrier, len(steps))
-    copies = []
-    for i, (dv, dh) in enumerate(steps):
-        copy = pltpu.make_async_remote_copy(
-            src_ref=st_ref,
-            dst_ref=slots.at[i],
-            send_sem=send_sem.at[i],
-            recv_sem=recv_sem.at[i],
-            device_id={"vocab": lax.rem(voc + dv, 4), "hid": lax.rem(hid + dh, 2)},
-            device_id_type=pl.DeviceIdType.MESH,
-        )
-        copy.start()
-        copies.append(copy)
-    for copy in copies:
-        copy.wait()
-    me = voc * 2 + hid
-    stats = [(me, st_ref[...])]
-    for i, (dv, dh) in enumerate(steps):
-        stats.append((lax.rem(voc + 4 - dv, 4) * 2 + lax.rem(hid + 2 - dh, 2), slots[i]))
-    ab, at_tgt = combine(stats, me)
-    ab_ref[...] = ab
-    at_tgt_ref[...] = jnp.broadcast_to(at_tgt, at_tgt_ref.shape)
-
-
-def exchange(st):
-    return pl.pallas_call(
-        exchange_kernel,
-        out_shape=[jax.ShapeDtypeStruct((128, 128), jnp.float32), jax.ShapeDtypeStruct((8, 128), jnp.float32)],
-        in_specs=[pl.BlockSpec(memory_space=pltpu.VMEM)],
-        out_specs=[pl.BlockSpec(memory_space=pltpu.VMEM)] * 2,
-        scratch_shapes=[
-            pltpu.VMEM((7, 8, 128), jnp.float32),
-            pltpu.SemaphoreType.DMA((7,)),
-            pltpu.SemaphoreType.DMA((7,)),
-        ],
-        compiler_params=pltpu.CompilerParams(collective_id=0, has_side_effects=True, vmem_limit_bytes=ALL_VMEM),
-        name="exchange",
-    )(st)
 
 
 def last_kernel(ab_ref, at_tgt_ref, ctin_ref, *refs, blk, at, rows, nparts):
@@ -341,10 +393,13 @@
                 return
             tok = owns[b] = partial_products(h, w, own_half, b * blk, (blk,), 0, ht, tn, ht, (tok,))[0]
 
-        tok = partial_products(h, w, peer_half, 0, (blk,), 0, 2, tn // 2, 2 * ht)[0]
-        parts[0] = [tok]
-        tok = partial_products(h, w, peer_half, 0, (blk,), 1, ht - 1, tn, ht, (tok,))[0]
-        parts[0].append(tok)
+        at = 0
+        parts[0] = []
+        for i, n in enumerate((1, 2, 2 * ht - 3)):
+            tok = partial_products(
+                h, w, peer_half, 0, (blk,), at, n, tn // 2, 2 * ht, () if i == 0 else (tok,))[0]
+            parts[0].append(tok)
+            at += n
         peer(1)
         peer(2)
         mine_half(0)
@@ -353,7 +408,7 @@
         def send(arrays):
             return [lax.ppermute(a, "hid", swap) for a in arrays]
 
-        recvs = {0: send(parts[0][:1]) + send(parts[0][1:]), 1: send(parts[1])}
+        recvs = {0: [send([p])[0] for p in parts[0]], 1: send(parts[1])}
         pres, stats = {}, {}
         out = None
         ct = jnp.zeros((nblk, blk), jnp.float32)
@@ -366,24 +421,24 @@
 
         prev = None
         for k, (b, at, rows) in enumerate(units):
-            pres[k], st = local_prefix(
-                temp2, tgt2, tri, owns[b], at, recvs[k], rows, b * blk + at, prev, (tok,))
-            tok = st
+            share = k == nu - 1
+            pres[k], *small = local_prefix(
+                temp2, tgt2, tri, owns[b], at, recvs[k], rows, b * blk + at, prev, (tok,), share)
+            if share:
+                at = units[k - 1][1]
+                out, ct = finish_last(*small, ct, [pres[k - 1], pres[k]], out, b, at, b * blk + at, (tok,))
+                break
+            tok = st = small[0]
             if k == nu - 2:
                 prev = st
                 close(k - 1)
                 continue
-            if k == nu - 1:
-                ab, at_tgt = exchange(st)
-                at = units[k - 1][1]
-                out, ct = finish_last(ab, at_tgt, ct, [pres[k - 1], pres[k]], out, b, at, b * blk + at, (tok,))
-                break
             mine = lax.all_gather(st, "vocab")
-            if k + 2 < nu:
-                *sent, mine = lax.optimization_barrier((*parts[k + 2], mine))
-                stats[k] = (st, mine, send([mine])[0])
-                recvs[k + 2] = send(sent)
-            tok = mine
+            grp = group_stats(pos, mine)
+            *sent, grp = lax.optimization_barrier((*parts[k + 2], grp))
+            stats[k] = (st, mine, send([grp])[0])
+            recvs[k + 2] = send(sent)
+            tok = grp
             if k >= 1:
                 close(k - 1)
             peer(k + 3)

time: 1420 us -> 1430 us (level)
  Pallas kernels: 605 us -> 625 us
    ppermute x21 -> x22, waiting for transfers between devices: 718 us -> 707 us  [send(): return [lax.ppermute(a, 'hid', swap) for a in arrays]]
    pallas_call x17 -> x18, Pallas kernels: 388 us -> 394 us  [partial_products(): pl.pallas_call(functools.partial(mm_kernel, splits=splits), out_shape=[ja...]
  transfers between devices with their start and end apart: 21 -> 22, of which waited for: 8 -> 9; matrix products, arithmetic and copies ran while one was open for 0% -> 0% of each run, Pallas kernels for 40% -> 41%
where the time goes in v2:
time: 1430 us
  waiting for transfers between devices  707 us (49%)
  Pallas kernels  625 us (44%)
  blocking collectives  64.5 us (5%)
  starting transfers between devices  25.8 us (2%)
    ppermute x22, waiting for transfers between devices, send(): return [lax.ppermute(a, 'hid', swap) for a in arrays]  707 us
    pallas_call x18, Pallas kernels, partial_products(): pl.pallas_call(functools.partial(mm_kernel, splits=splits), out_shape=[ja...  394 us
    pallas_call x11, Pallas kernels, local_prefix(): pl.pallas_call(functools.partial(local_kernel, npieces=len(recvs), has_pr...  153 us
    all_gather x9, blocking collectives, pipeline(): mine = lax.all_gather(st, 'vocab')  64.5 us
    pallas_call x9, Pallas kernels, finish(): pl.pallas_call(functools.partial(final_kernel, blk=blk, at=at, rows=rows)...  57.4 us
  transfers between devices with their start and end apart: 22, of which 9 were waited for; matrix products, arithmetic and copies ran while one was open for 0% of the time, Pallas kernels for 41%

profile of v2, /device:TPU:0, one launch (start us, length us, event | category | flops | bytes accessed | tf_op | source)
XLA Modules:
  0.0 1429.4 jit_solution(2095939503680025710)
XLA Ops:
  10.3 22.3 %shard_map.61.refs_0_ = f32[128,9856]{1,0:T(8,128)} custom-call(s32[1]{0:T(128)} %bitcast.4.sel_ref, bf16[1024,2560]{1,0:T(8,128)(2,1)} %h_ref.35, bf16[2560,25088]{1,0:T(8,128)(2,1)} %w_ref.35, f32[128,1792]{1,0:T(8,128)} %shard_map.60.refs_0_), custom_call_target="tpu_custom_call" | custom-call | flops 6459228160 | bytes 55508992 | tf_op jit(solution)/shard_map/pallas_call | solution.py:29
  38.0 24.1 %shard_map.62.refs_0_ = f32[128,12544]{1,0:T(8,128)} custom-call(s32[1]{0:T(128)} %bitcast.4.sel_ref, bf16[1024,2560]{1,0:T(8,128)(2,1)} %h_ref.35, bf16[2560,25088]{1,0:T(8,128)(2,1)} %w_ref.35, f32[128,9856]{1,0:T(8,128)} %shard_map.61.refs_0_), custom_call_target="tpu_custom_call" | custom-call | flops 8220835840 | bytes 70647808 | tf_op jit(solution)/shard_map/pallas_call | solution.py:29
  63.4 24.1 %shard_map.63.refs_0_ = f32[128,12544]{1,0:T(8,128)} custom-call(s32[1]{0:T(128)} %bitcast.4.sel_ref, bf16[1024,2560]{1,0:T(8,128)(2,1)} %h_ref.35, bf16[2560,25088]{1,0:T(8,128)(2,1)} %w_ref.35, f32[128,12544]{1,0:T(8,128)} %shard_map.62.refs_0_), custom_call_target="tpu_custom_call" | custom-call | flops 8220835840 | bytes 70647808 | tf_op jit(solution)/shard_map/pallas_call | solution.py:29
  87.5 24.1 %shard_map.64.refs_0_.own_ref = f32[128,12544]{1,0:T(8,128)} custom-call(s32[1]{0:T(128)} %bitcast.2.sel_ref, bf16[1024,2560]{1,0:T(8,128)(2,1)} %h_ref.35, bf16[2560,25088]{1,0:T(8,128)(2,1)} %w_ref.35, f32[128,12544]{1,0:T(8,128)} %shard_map.63.refs_0_), custom_call_target="tpu_custom_call" | custom-call | flops 8220835840 | bytes 70647808 | tf_op jit(solution)/shard_map/pallas_call | solution.py:29
  116.3 24.2 %shard_map.65.refs_3_.own_ref = f32[128,12544]{1,0:T(8,128)} custom-call(s32[1]{0:T(128)} %bitcast.2.sel_ref, bf16[1024,2560]{1,0:T(8,128)(2,1)} %h_ref.35, bf16[2560,25088]{1,0:T(8,128)(2,1)} %w_ref.35, f32[128,12544]{1,0:T(8,128)} %shard_map.64.refs_0_.own_ref), custom_call_target="tpu_custom_call" | custom-call | flops 8220835840 | bytes 70647808 | tf_op jit(solution)/shard_map/pallas_call | solution.py:29
  155.8 19.7 %collective-permute-done.2.refs_1_ = f32[128,1792]{1,0:T(8,128)} collective-permute-done((f32[128,1792]{1,0:T(8,128)}, f32[128,1792]{1,0:T(8,128)}, u32[]{:S(2)}, u32[]{:S(2)}) %collective-permute-start.2) | collective-permute-done | bytes 917536 | tf_op jit(solution)/shard_map/ppermute | solution.py:409
  205.3 24.1 %shard_map.67.refs_0_ = f32[128,12544]{1,0:T(8,128)} custom-call(s32[1]{0:T(128)} %bitcast.4.sel_ref, bf16[1024,2560]{1,0:T(8,128)(2,1)} %h_ref.35, bf16[2560,25088]{1,0:T(8,128)(2,1)} %w_ref.35, f32[8,128]{1,0:T(8,128)} %group_stats.9.refs_0_), custom_call_target="tpu_custom_call" | custom-call | flops 8220835840 | bytes 70647808 | tf_op jit(solution)/shard_map/pallas_call | solution.py:29
  229.4 24.1 %shard_map.68.refs_1_.own_ref = f32[128,12544]{1,0:T(8,128)} custom-call(s32[1]{0:T(128)} %bitcast.2.sel_ref, bf16[1024,2560]{1,0:T(8,128)(2,1)} %h_ref.35, bf16[2560,25088]{1,0:T(8,128)(2,1)} %w_ref.35, f32[128,12544]{1,0:T(8,128)} %shard_map.67.refs_0_), custom_call_target="tpu_custom_call" | custom-call | flops 8220835840 | bytes 70647808 | tf_op jit(solution)/shard_map/pallas_call | solution.py:29
  253.6 59.6 %collective-permute-done.refs_0_ = f32[128,12544]{1,0:T(8,128)} collective-permute-done((f32[128,12544]{1,0:T(8,128)}, f32[128,12544]{1,0:T(8,128)}, u32[]{:S(2)}, u32[]{:S(2)}) %collective-permute-start) | collective-permute-done | bytes 6422560 | tf_op jit(solution)/shard_map/ppermute | solution.py:409
  341.9 108.9 %collective-permute-done.5.other_ref = f32[8,128]{1,0:T(8,128)} collective-permute-done((f32[8,128]{1,0:T(8,128)}, f32[8,128]{1,0:T(8,128)}, u32[]{:S(2)}, u32[]{:S(2)}) %collective-permute-start.5) | collective-permute-done | bytes 4128 | tf_op jit(solution)/shard_map/ppermute | solution.py:409
  458.5 24.1 %shard_map.71.refs_0_ = f32[128,12544]{1,0:T(8,128)} custom-call(s32[1]{0:T(128)} %bitcast.4.sel_ref, bf16[1024,2560]{1,0:T(8,128)(2,1)} %h_ref.35, bf16[2560,25088]{1,0:T(8,128)(2,1)} %w_ref.35, f32[8,128]{1,0:T(8,128)} %get-tuple-element.73.refs_0_.ctin_ref), custom_call_target="tpu_custom_call" | custom-call | flops 8220835840 | bytes 70647808 | tf_op jit(solution)/shard_map/pallas_call | solution.py:29
  482.6 24.1 %shard_map.72.refs_1_.own_ref = f32[128,12544]{1,0:T(8,128)} custom-call(s32[1]{0:T(128)} %bitcast.2.sel_ref, bf16[1024,2560]{1,0:T(8,128)(2,1)} %h_ref.35, bf16[2560,25088]{1,0:T(8,128)(2,1)} %w_ref.35, f32[128,12544]{1,0:T(8,128)} %shard_map.71.refs_0_), custom_call_target="tpu_custom_call" | custom-call | flops 8220835840 | bytes 70647808 | tf_op jit(solution)/shard_map/pallas_call | solution.py:29
  537.5 187.9 %collective-permute-done.4.other_ref = f32[8,128]{1,0:T(8,128)} collective-permute-done((f32[8,128]{1,0:T(8,128)}, f32[8,128]{1,0:T(8,128)}, u32[]{:S(2)}, u32[]{:S(2)}) %collective-permute-start.4) | collective-permute-done | bytes 4128 | tf_op jit(solution)/shard_map/ppermute | solution.py:409
  732.5 24.1 %shard_map.75.refs_0_ = f32[128,12544]{1,0:T(8,128)} custom-call(s32[1]{0:T(128)} %bitcast.4.sel_ref, bf16[1024,2560]{1,0:T(8,128)(2,1)} %h_ref.35, bf16[2560,25088]{1,0:T(8,128)(2,1)} %w_ref.35, f32[8,128]{1,0:T(8,128)} %get-tuple-element.78.refs_0_.ctin_ref), custom_call_target="tpu_custom_call" | custom-call | flops 8220835840 | bytes 70647808 | tf_op jit(solution)/shard_map/pallas_call | solution.py:29
  756.6 24.1 %shard_map.76.refs_1_.own_ref = f32[128,12544]{1,0:T(8,128)} custom-call(s32[1]{0:T(128)} %bitcast.2.sel_ref, bf16[1024,2560]{1,0:T(8,128)(2,1)} %h_ref.35, bf16[2560,25088]{1,0:T(8,128)(2,1)} %w_ref.35, f32[128,12544]{1,0:T(8,128)} %shard_map.75.refs_0_), custom_call_target="tpu_custom_call" | custom-call | flops 8220835840 | bytes 70647808 | tf_op jit(solution)/shard_map/pallas_call | solution.py:29
  816.5 24.1 %shard_map.79.refs_0_ = f32[128,12544]{1,0:T(8,128)} custom-call(s32[1]{0:T(128)} %bitcast.4.sel_ref, bf16[1024,2560]{1,0:T(8,128)(2,1)} %h_ref.35, bf16[2560,25088]{1,0:T(8,128)(2,1)} %w_ref.35, f32[8,128]{1,0:T(8,128)} %get-tuple-element.85.refs_0_.ctin_ref), custom_call_target="tpu_custom_call" | custom-call | flops 8220835840 | bytes 70647808 | tf_op jit(solution)/shard_map/pallas_call | solution.py:29
  840.6 24.1 %shard_map.80.refs_1_.own_ref = f32[128,12544]{1,0:T(8,128)} custom-call(s32[1]{0:T(128)} %bitcast.2.sel_ref, bf16[1024,2560]{1,0:T(8,128)(2,1)} %h_ref.35, bf16[2560,25088]{1,0:T(8,128)(2,1)} %w_ref.35, f32[128,12544]{1,0:T(8,128)} %shard_map.79.refs_0_), custom_call_target="tpu_custom_call" | custom-call | flops 8220835840 | bytes 70647808 | tf_op jit(solution)/shard_map/pallas_call | solution.py:29
  892.9 193.5 %collective-permute-done.11.other_ref = f32[8,128]{1,0:T(8,128)} collective-permute-done((f32[8,128]{1,0:T(8,128)}, f32[8,128]{1,0:T(8,128)}, u32[]{:S(2)}, u32[]{:S(2)}) %collective-permute-start.11) | collective-permute-done | bytes 4128 | tf_op jit(solution)/shard_map/ppermute | solution.py:409
  1093.5 24.1 %shard_map.83 = (f32[64,12544]{1,0:T(8,128)}, f32[32,12544]{1,0:T(8,128)}, f32[16,12544]{1,0:T(8,128)}, f32[16,12544]{1,0:T(8,128)}) custom-call(s32[1]{0:T(128)} %bitcast.4.sel_ref, bf16[1024,2560]{1,0:T(8,128)(2,1)} %h_ref.35, bf16[2560,25088]{1,0:T(8,128)(2,1)} %w_ref.35, f32[8,128]{1,0:T(8,128)} %get-tuple-element.91.refs_0_.ctin_ref), custom_call_target="tpu_custom_call" | custom-call | flops 8220835840 | bytes 70647808 | tf_op jit(solution)/shard_map/pallas_call | solution.py:29
  1117.7 24.1 %shard_map.84.refs_1_.own_ref = f32[128,12544]{1,0:T(8,128)} custom-call(s32[1]{0:T(128)} %bitcast.2.sel_ref, bf16[1024,2560]{1,0:T(8,128)(2,1)} %h_ref.35, bf16[2560,25088]{1,0:T(8,128)(2,1)} %w_ref.35, f32[64,12544]{1,0:T(8,128)} %get-tuple-element.110.refs_0_), custom_call_target="tpu_custom_call" | custom-call | flops 8220835840 | bytes 70647808 | tf_op jit(solution)/shard_map/pallas_call | solution.py:29
  1170.1 69.9 %collective-permute-done.10.other_ref = f32[8,128]{1,0:T(8,128)} collective-permute-done((f32[8,128]{1,0:T(8,128)}, f32[8,128]{1,0:T(8,128)}, u32[]{:S(2)}, u32[]{:S(2)}) %collective-permute-start.10) | collective-permute-done | bytes 4128 | tf_op jit(solution)/shard_map/ppermute | solution.py:409
  1247.1 24.1 %shard_map.87.refs_1_.own_ref = f32[128,12544]{1,0:T(8,128)} custom-call(s32[1]{0:T(128)} %bitcast.2.sel_ref, bf16[1024,2560]{1,0:T(8,128)(2,1)} %h_ref.35, bf16[2560,25088]{1,0:T(8,128)(2,1)} %w_ref.35, f32[8,128]{1,0:T(8,128)} %get-tuple-element.97.refs_0_.ctin_ref), custom_call_target="tpu_custom_call" | custom-call | flops 8220835840 | bytes 70647808 | tf_op jit(solution)/shard_map/pallas_call | solution.py:29
  1301.4 34.2 %collective-permute-done.16.other_ref = f32[8,128]{1,0:T(8,128)} collective-permute-done((f32[8,128]{1,0:T(8,128)}, f32[8,128]{1,0:T(8,128)}, u32[]{:S(2)}, u32[]{:S(2)}) %collective-permute-start.16) | collective-permute-done | bytes 4128 | tf_op jit(solution)/shard_map/ppermute | solution.py:409
  1388.4 18.1 %collective-permute-done.20.other_ref = f32[8,128]{1,0:T(8,128)} collective-permute-done((f32[8,128]{1,0:T(8,128)}, f32[8,128]{1,0:T(8,128)}, u32[]{:S(2)}, u32[]{:S(2)}) %collective-permute-start.20) | collective-permute-done | bytes 4128 | tf_op jit(solution)/shard_map/ppermute | solution.py:409
  (83 shorter events, 353.0 us)
Async XLA Ops:
  32.6 142.9 %collective-permute-start.3 = (f32[128,9856]{1,0:T(8,128)}, f32[128,9856]{1,0:T(8,128)}, u32[]{:S(2)}, u32[]{:S(2)}) collective-permute-start(f32[128,9856]{1,0:T(8,128)} %shard_map.61.refs_0_), channel_id=1, source_target_pairs={{0,4},{4,0},{1,5},{5,1},{2,6},{6,2},{3,7},{7,3}} | collective-permute-start | bytes 15138824 | tf_op jit(solution)/shard_map/ppermute | solution.py:409
  36.0 119.8 %collective-permute-start.1 = (f32[128,896]{1,0:T(8,128)}, f32[128,896]{1,0:T(8,128)}, u32[]{:S(2)}, u32[]{:S(2)}) collective-permute-start(f32[128,896]{1,0:T(8,128)} %shard_map.59.refs_0_), channel_id=1, source_target_pairs={{0,4},{4,0},{1,5},{5,1},{2,6},{6,2},{3,7},{7,3}} | collective-permute-start | bytes 1376264 | tf_op jit(solution)/shard_map/ppermute | solution.py:409
  36.0 139.5 %collective-permute-start.2 = (f32[128,1792]{1,0:T(8,128)}, f32[128,1792]{1,0:T(8,128)}, u32[]{:S(2)}, u32[]{:S(2)}) collective-permute-start(f32[128,1792]{1,0:T(8,128)} %shard_map.60.refs_0_), channel_id=1, source_target_pairs={{0,4},{4,0},{1,5},{5,1},{2,6},{6,2},{3,7},{7,3}} | collective-permute-start | bytes 2752520 | tf_op jit(solution)/shard_map/ppermute | solution.py:409
  62.1 251.0 %collective-permute-start = (f32[128,12544]{1,0:T(8,128)}, f32[128,12544]{1,0:T(8,128)}, u32[]{:S(2)}, u32[]{:S(2)}) collective-permute-start(f32[128,12544]{1,0:T(8,128)} %shard_map.62.refs_0_), channel_id=1, source_target_pairs={{0,4},{4,0},{1,5},{5,1},{2,6},{6,2},{3,7},{7,3}} | collective-permute-start | bytes 19267592 | tf_op jit(solution)/shard_map/ppermute | solution.py:409
  203.3 303.4 %collective-permute-start.6 = (f32[128,12544]{1,0:T(8,128)}, f32[128,12544]{1,0:T(8,128)}, u32[]{:S(2)}, u32[]{:S(2)}) collective-permute-start(f32[128,12544]{1,0:T(8,128)} %shard_map.63.refs_0_), channel_id=1, source_target_pairs={{0,4},{4,0},{1,5},{5,1},{2,6},{6,2},{3,7},{7,3}} | collective-permute-start | bytes 19267592 | tf_op jit(solution)/shard_map/ppermute | solution.py:409
  204.9 246.0 %collective-permute-start.5 = (f32[8,128]{1,0:T(8,128)}, f32[8,128]{1,0:T(8,128)}, u32[]{:S(2)}, u32[]{:S(2)}) collective-permute-start(f32[8,128]{1,0:T(8,128)} %group_stats.9.refs_0_), channel_id=1, source_target_pairs={{0,4},{4,0},{1,5},{5,1},{2,6},{6,2},{3,7},{7,3}} | collective-permute-start | bytes 12296 | tf_op jit(solution)/shard_map/ppermute | solution.py:409
  340.3 440.3 %collective-permute-start.9 = (f32[128,12544]{1,0:T(8,128)}, f32[128,12544]{1,0:T(8,128)}, u32[]{:S(2)}, u32[]{:S(2)}) collective-permute-start(f32[128,12544]{1,0:T(8,128)} %shard_map.67.refs_0_), channel_id=1, source_target_pairs={{0,4},{4,0},{1,5},{5,1},{2,6},{6,2},{3,7},{7,3}} | collective-permute-start | bytes 19267592 | tf_op jit(solution)/shard_map/ppermute | solution.py:409
  533.9 330.7 %collective-permute-start.7 = (f32[128,12544]{1,0:T(8,128)}, f32[128,12544]{1,0:T(8,128)}, u32[]{:S(2)}, u32[]{:S(2)}) collective-permute-start(f32[128,12544]{1,0:T(8,128)} %shard_map.71.refs_0_), channel_id=1, source_target_pairs={{0,4},{4,0},{1,5},{5,1},{2,6},{6,2},{3,7},{7,3}} | collective-permute-start | bytes 19267592 | tf_op jit(solution)/shard_map/ppermute | solution.py:409
  535.5 189.9 %collective-permute-start.4 = (f32[8,128]{1,0:T(8,128)}, f32[8,128]{1,0:T(8,128)}, u32[]{:S(2)}, u32[]{:S(2)}) collective-permute-start(f32[8,128]{1,0:T(8,128)} %group_stats.10.refs_0_), channel_id=1, source_target_pairs={{0,4},{4,0},{1,5},{5,1},{2,6},{6,2},{3,7},{7,3}} | collective-permute-start | bytes 12296 | tf_op jit(solution)/shard_map/ppermute | solution.py:409
  536.0 273.4 %collective-permute-start.8 = (f32[8,128]{1,0:T(8,128)}, f32[8,128]{1,0:T(8,128)}, u32[]{:S(2)}, u32[]{:S(2)}) collective-permute-start(f32[8,128]{1,0:T(8,128)} %group_stats.11.refs_1_), channel_id=1, source_target_pairs={{0,4},{4,0},{1,5},{5,1},{2,6},{6,2},{3,7},{7,3}} | collective-permute-start | bytes 12296 | tf_op jit(solution)/shard_map/ppermute | solution.py:409
  807.8 333.9 %collective-permute-start.12 = (f32[128,12544]{1,0:T(8,128)}, f32[128,12544]{1,0:T(8,128)}, u32[]{:S(2)}, u32[]{:S(2)}) collective-permute-start(f32[128,12544]{1,0:T(8,128)} %shard_map.75.refs_0_), channel_id=1, source_target_pairs={{0,4},{4,0},{1,5},{5,1},{2,6},{6,2},{3,7},{7,3}} | collective-permute-start | bytes 19267592 | tf_op jit(solution)/shard_map/ppermute | solution.py:409
  890.9 380.3 %collective-permute-start.13 = (f32[128,12544]{1,0:T(8,128)}, f32[128,12544]{1,0:T(8,128)}, u32[]{:S(2)}, u32[]{:S(2)}) collective-permute-start(f32[128,12544]{1,0:T(8,128)} %shard_map.79.refs_0_), channel_id=1, source_target_pairs={{0,4},{4,0},{1,5},{5,1},{2,6},{6,2},{3,7},{7,3}} | collective-permute-start | bytes 19267592 | tf_op jit(solution)/shard_map/ppermute | solution.py:409
  891.4 195.1 %collective-permute-start.11 = (f32[8,128]{1,0:T(8,128)}, f32[8,128]{1,0:T(8,128)}, u32[]{:S(2)}, u32[]{:S(2)}) collective-permute-start(f32[8,128]{1,0:T(8,128)} %group_stats.12.refs_1_), channel_id=1, source_target_pairs={{0,4},{4,0},{1,5},{5,1},{2,6},{6,2},{3,7},{7,3}} | collective-permute-start | bytes 12296 | tf_op jit(solution)/shard_map/ppermute | solution.py:409
  1168.0 174.6 %collective-permute-start.17 = (f32[64,12544]{1,0:T(8,128)}, f32[64,12544]{1,0:T(8,128)}, u32[]{:S(2)}, u32[]{:S(2)}) collective-permute-start(f32[64,12544]{1,0:T(8,128)} %get-tuple-element.110.refs_0_), channel_id=1, source_target_pairs={{0,4},{4,0},{1,5},{5,1},{2,6},{6,2},{3,7},{7,3}} | collective-permute-start | bytes 9633800 | tf_op jit(solution)/shard_map/ppermute | solution.py:409
  1169.6 70.4 %collective-permute-start.10 = (f32[8,128]{1,0:T(8,128)}, f32[8,128]{1,0:T(8,128)}, u32[]{:S(2)}, u32[]{:S(2)}) collective-permute-start(f32[8,128]{1,0:T(8,128)} %group_stats.13.refs_1_), channel_id=1, source_target_pairs={{0,4},{4,0},{1,5},{5,1},{2,6},{6,2},{3,7},{7,3}} | collective-permute-start | bytes 12296 | tf_op jit(solution)/shard_map/ppermute | solution.py:409
  1297.8 72.6 %collective-permute-start.14 = (f32[32,12544]{1,0:T(8,128)}, f32[32,12544]{1,0:T(8,128)}, u32[]{:S(2)}, u32[]{:S(2)}) collective-permute-start(f32[32,12544]{1,0:T(8,128)} %get-tuple-element.102), channel_id=1, source_target_pairs={{0,4},{4,0},{1,5},{5,1},{2,6},{6,2},{3,7},{7,3}} | collective-permute-start | bytes 4816904 | tf_op jit(solution)/shard_map/ppermute | solution.py:409
  1299.3 36.3 %collective-permute-start.16 = (f32[8,128]{1,0:T(8,128)}, f32[8,128]{1,0:T(8,128)}, u32[]{:S(2)}, u32[]{:S(2)}) collective-permute-start(f32[8,128]{1,0:T(8,128)} %group_stats.14.refs_1_), channel_id=1, source_target_pairs={{0,4},{4,0},{1,5},{5,1},{2,6},{6,2},{3,7},{7,3}} | collective-permute-start | bytes 12296 | tf_op jit(solution)/shard_map/ppermute | solution.py:409
  1299.8 63.5 %collective-permute-start.15 = (f32[8,128]{1,0:T(8,128)}, f32[8,128]{1,0:T(8,128)}, u32[]{:S(2)}, u32[]{:S(2)}) collective-permute-start(f32[8,128]{1,0:T(8,128)} %group_stats.15.refs_1_), channel_id=1, source_target_pairs={{0,4},{4,0},{1,5},{5,1},{2,6},{6,2},{3,7},{7,3}} | collective-permute-start | bytes 12296 | tf_op jit(solution)/shard_map/ppermute | solution.py:409
  1361.7 49.0 %collective-permute-start.19 = (f32[16,12544]{1,0:T(8,128)}, f32[16,12544]{1,0:T(8,128)}, u32[]{:S(2)}, u32[]{:S(2)}) collective-permute-start(f32[16,12544]{1,0:T(8,128)} %get-tuple-element.116), channel_id=1, source_target_pairs={{0,4},{4,0},{1,5},{5,1},{2,6},{6,2},{3,7},{7,3}} | collective-permute-start | bytes 2408456 | tf_op jit(solution)/shard_map/ppermute | solution.py:409
  1385.9 33.6 %collective-permute-start.18 = (f32[16,12544]{1,0:T(8,128)}, f32[16,12544]{1,0:T(8,128)}, u32[]{:S(2)}, u32[]{:S(2)}) collective-permute-start(f32[16,12544]{1,0:T(8,128)} %get-tuple-element.115), channel_id=1, source_target_pairs={{0,4},{4,0},{1,5},{5,1},{2,6},{6,2},{3,7},{7,3}} | collective-permute-start | bytes 2408456 | tf_op jit(solution)/shard_map/ppermute | solution.py:409
  1386.4 20.1 %collective-permute-start.20 = (f32[8,128]{1,0:T(8,128)}, f32[8,128]{1,0:T(8,128)}, u32[]{:S(2)}, u32[]{:S(2)}) collective-permute-start(f32[8,128]{1,0:T(8,128)} %group_stats.16.refs_1_), channel_id=1, source_target_pairs={{0,4},{4,0},{1,5},{5,1},{2,6},{6,2},{3,7},{7,3}} | collective-permute-start | bytes 12296 | tf_op jit(solution)/shard_map/ppermute | solution.py:409
  1387.9 28.0 %collective-permute-start.21 = (f32[8,128]{1,0:T(8,128)}, f32[8,128]{1,0:T(8,128)}, u32[]{:S(2)}, u32[]{:S(2)}) collective-permute-start(f32[8,128]{1,0:T(8,128)} %group_stats.17.refs_1_), channel_id=1, source_target_pairs={{0,4},{4,0},{1,5},{5,1},{2,6},{6,2},{3,7},{7,3}} | collective-permute-start | bytes 12296 | tf_op jit(solution)/shard_map/ppermute | solution.py:409

commit v3 on v2

--- a/solution.py
+++ b/solution.py
@@ -1,4 +1,5 @@
 import functools
+import math
 
 import jax
 import jax.numpy as jnp
@@ -13,34 +14,42 @@
 ALL_VMEM = 67043328
 
 
-def mm_kernel(sel_ref, h_ref, w_ref, *refs, splits):
+def mm_kernel(sel_ref, h_ref, w_ref, *refs, splits, ksteps):
     out_refs = refs[len(refs) - len(splits):]
     res = jnp.dot(h_ref[...], w_ref[...], preferred_element_type=jnp.float32)
-    at = 0
-    for ref, rows in zip(out_refs, splits):
-        ref[...] = res[at:at + rows]
-        at += rows
-
-
-def partial_products(h, w, half, row0, splits, tile0, ntiles, tn, half_tiles, deps=()):
+
+    def put(add):
+        at = 0
+        for ref, rows in zip(out_refs, splits):
+            ref[...] = ref[...] + res[at:at + rows] if add else res[at:at + rows]
+            at += rows
+
+    if ksteps == 1:
+        put(False)
+    else:
+        pl.when(pl.program_id(1) == 0)(functools.partial(put, False))
+        pl.when(pl.program_id(1) > 0)(functools.partial(put, True))
+
+
+def partial_products(h, w, half, row0, splits, tile0, ntiles, tn, half_tiles, deps=(), ksteps=1):
     rows = sum(splits)
     depth = h.shape[1]
     cols = ntiles * tn
     return pl.pallas_call(
-        functools.partial(mm_kernel, splits=splits),
+        functools.partial(mm_kernel, splits=splits, ksteps=ksteps),
         out_shape=[jax.ShapeDtypeStruct((r, cols), jnp.float32) for r in splits],
         grid_spec=pltpu.PrefetchScalarGridSpec(
             num_scalar_prefetch=1,
-            grid=(ntiles,),
+            grid=(ntiles, ksteps),
             in_specs=[
-                pl.BlockSpec((rows, depth), lambda j, s: (row0 // rows, 0)),
-                pl.BlockSpec((depth, tn), lambda j, s: (0, s[0] * half_tiles + tile0 + j)),
+                pl.BlockSpec((rows, depth // ksteps), lambda j, k, s: (row0 // rows, k)),
+                pl.BlockSpec((depth // ksteps, tn), lambda j, k, s: (k, s[0] * half_tiles + tile0 + j)),
             ] + [pl.BlockSpec(memory_space=pl.ANY)] * len(deps),
-            out_specs=[pl.BlockSpec((r, tn), lambda j, s: (0, j)) for r in splits],
+            out_specs=[pl.BlockSpec((r, tn), lambda j, k, s: (0, j)) for r in splits],
         ),
         cost_estimate=pl.CostEstimate(
             flops=2 * rows * depth * cols, bytes_accessed=depth * cols * 2 + rows * cols * 4, transcendentals=0),
-        compiler_params=pltpu.CompilerParams(dimension_semantics=("arbitrary",), vmem_limit_bytes=ALL_VMEM),
+        compiler_params=pltpu.CompilerParams(dimension_semantics=("arbitrary", "arbitrary"), vmem_limit_bytes=ALL_VMEM),
     )(half, h, w, *deps)
 
 
@@ -48,8 +57,9 @@
     recv_refs = refs[:npieces]
     prev_ref = refs[npieces] if has_prev else None
     if share:
-        pre_ref, ab_ref, at_tgt_ref, z_s, hi_s, mid_s, lo_s, st_s, st_ref, slots, send_sem, recv_sem = refs[npieces + has_prev + skip:]
+        pre_ref, ab_ref, at_tgt_ref, z_s, hi_s, mid_s, lo_s, st_s, st_ref, slots, send_sem, recv_sem, pre_s, out_sem = refs[npieces + has_prev + skip:]
         announce()
+        pre_hbm, pre_ref = pre_ref, pre_s
     else:
         pre_ref, st_ref, z_s, hi_s, mid_s, lo_s, st_s = refs[npieces + has_prev + skip:]
     step, nsteps = pl.program_id(0), pl.num_programs(0)
@@ -131,13 +141,16 @@
 
     lax.fori_loop(0, nt // group, prefix_step, zero)
     if share:
+        put = pltpu.make_async_copy(pre_ref, pre_hbm, out_sem)
+        put.start()
         gather(copies, st_ref, slots, ab_ref, at_tgt_ref)
+        put.wait()
 
 
 def local_prefix(temp, tgt, tri, own, at, recvs, rows, row0, prev, deps, share=False):
     cols = own.shape[1]
     nt = cols // CT
-    sub = min(SUB, rows)
+    sub = math.gcd(SUB, rows, at)
     small = (128, 8) if share else (8,)
     extra = ([] if prev is None else [prev]) + list(deps)
     extra_specs = ([] if prev is None else [pl.BlockSpec((8, 128), lambda i: (0, 0))])
@@ -154,7 +167,7 @@
             pl.BlockSpec((CT, CT), lambda i: (0, 0)),
             pl.BlockSpec((sub, cols), lambda i: (at // sub + i, 0)),
         ] + [pl.BlockSpec((sub, r.shape[1]), lambda i: (i, 0)) for r in recvs] + extra_specs,
-        out_specs=[pl.BlockSpec((sub, cols), lambda i: (i, 0))]
+        out_specs=[pl.BlockSpec(memory_space=pl.ANY) if share else pl.BlockSpec((sub, cols), lambda i: (i, 0))]
         + [pl.BlockSpec((n, 128), lambda i: (0, 0)) for n in small],
         scratch_shapes=[
             pltpu.VMEM((nt, sub, CT), jnp.float32),
@@ -167,6 +180,8 @@
             pltpu.VMEM((7, 8, 128), jnp.float32),
             pltpu.SemaphoreType.DMA((7,)),
             pltpu.SemaphoreType.DMA((7,)),
+            pltpu.VMEM((rows, cols), jnp.float32),
+            pltpu.SemaphoreType.DMA,
         ] if share else []),
         cost_estimate=pl.CostEstimate(
             flops=6 * rows * cols * CT, bytes_accessed=rows * cols * 12, transcendentals=rows * cols),
@@ -299,7 +314,7 @@
 
 def finish(pos, pre, st, mine, other, out, ct, all_rows, blk, at, row0, deps):
     rows, cols = pre.shape
-    sub = min(SUB, rows)
+    sub = math.gcd(SUB, rows, at)
     tail = ([] if out is None else [out]) + list(deps)
     small = pl.BlockSpec((8, 128), lambda i, s: (0, 0))
     wide = pl.BlockSpec(mine.shape, lambda i, s: (0, 0, 0))
@@ -320,31 +335,36 @@
     )(pos, pre, st, mine, other, ct, *tail)
 
 
-def last_kernel(ab_ref, at_tgt_ref, ctin_ref, *refs, blk, at, rows, nparts):
+def last_kernel(ab_ref, at_tgt_ref, ctin_ref, *refs, blk, at, rows, ends):
     out_ref, ct_ref = refs[-2:]
     step = pl.program_id(0)
     sub = out_ref.shape[0]
     ab = ab_ref[pl.ds(pl.multiple_of(at + step * sub, sub), sub), :]
     ct_ref[...] = merged(ctin_ref[...], at_tgt_ref[...], blk, at, rows)
-    for i in range(nparts):
-        @pl.when(step == i)
+    for i, (lo, hi) in enumerate(ends):
+        @pl.when((step >= lo) & (step < hi))
         def _(pre_ref=refs[i]):
             out_ref[...] = pre_ref[...] * ab[:, 0:1] + ab[:, 1:2]
 
 
 def finish_last(ab, at_tgt, ct, pres, out, blk, at, row0, deps):
-    sub, cols = pres[0].shape
-    n = len(pres)
+    cols = out.shape[1]
+    rows = [p.shape[0] for p in pres]
+    sub = math.gcd(*rows)
+    ends, lo = [], 0
+    for r in rows:
+        ends.append((lo, lo + r // sub))
+        lo += r // sub
     small = pl.BlockSpec((8, 128), lambda i: (0, 0))
     return pl.pallas_call(
-        functools.partial(last_kernel, blk=blk, at=at, rows=sub * n, nparts=n),
-        grid=(n,),
+        functools.partial(last_kernel, blk=blk, at=at, rows=sum(rows), ends=tuple(ends)),
+        grid=(lo,),
         out_shape=[jax.ShapeDtypeStruct(out.shape, jnp.float32), jax.ShapeDtypeStruct((8, 128), jnp.float32)],
         in_specs=[pl.BlockSpec((128, 128), lambda i: (0, 0)), small, small]
-        + [pl.BlockSpec((sub, cols), lambda i: (0, 0))] * n
+        + [pl.BlockSpec((sub, cols), lambda i, lo=lo, hi=hi: (jnp.clip(i - lo, 0, hi - lo - 1), 0)) for lo, hi in ends]
         + [pl.BlockSpec(memory_space=pl.ANY)] * (1 + len(deps)),
         out_specs=[pl.BlockSpec((sub, cols), lambda i: (row0 // sub + i, 0)), small],
-        input_output_aliases={3 + n: 0},
+        input_output_aliases={3 + len(pres): 0},
         compiler_params=pltpu.CompilerParams(dimension_semantics=("arbitrary",), vmem_limit_bytes=ALL_VMEM),
         name="finish_last",
     )(ab, at_tgt, ct, *pres, out, *deps)
@@ -366,7 +386,7 @@
 
         blk = 128
         nblk = rows_all // blk
-        last = (64, 32, 16, 16)
+        last = (32, 48, 32, 16)
         tn = 7 * CT
         ht = cols // tn
 
@@ -395,9 +415,10 @@
 
         at = 0
         parts[0] = []
-        for i, n in enumerate((1, 2, 2 * ht - 3)):
+        for i, n in enumerate((1, 4, 2 * ht - 5)):
             tok = partial_products(
-                h, w, peer_half, 0, (blk,), at, n, tn // 2, 2 * ht, () if i == 0 else (tok,))[0]
+                h, w, peer_half, 0, (blk,), at, n, tn // 2, 2 * ht, () if i == 0 else (tok,),
+                2 if i == 0 else 1)[0]
             parts[0].append(tok)
             at += n
         peer(1)

time: 1430 us -> 1420 us (level)
  waiting for transfers between devices: 707 us -> 690 us
    ppermute x22, waiting for transfers between devices: 707 us -> 690 us  [send(): return [lax.ppermute(a, 'hid', swap) for a in arrays]]
  transfers between devices with their start and end apart: 22 -> 22, of which waited for: 9 -> 8; matrix products, arithmetic and copies ran while one was open for 0% -> 0% of each run, Pallas kernels for 41% -> 41%
where the time goes in v3:
time: 1420 us
  waiting for transfers between devices  690 us (49%)
  Pallas kernels  630 us (44%)
  blocking collectives  66.4 us (5%)
  starting transfers between devices  23.2 us (2%)
    ppermute x22, waiting for transfers between devices, send(): return [lax.ppermute(a, 'hid', swap) for a in arrays]  690 us
    pallas_call x18, Pallas kernels, partial_products(): pl.pallas_call(functools.partial(mm_kernel, splits=splits, ksteps=ksteps)...  393 us
    pallas_call x11, Pallas kernels, local_prefix(): pl.pallas_call(functools.partial(local_kernel, npieces=len(recvs), has_pr...  157 us
    all_gather x9, blocking collectives, pipeline(): mine = lax.all_gather(st, 'vocab')  66.4 us
    pallas_call x9, Pallas kernels, finish(): pl.pallas_call(functools.partial(final_kernel, blk=blk, at=at, rows=rows)...  58.1 us
  transfers between devices with their start and end apart: 22, of which 8 were waited for; matrix products, arithmetic and copies ran while one was open for 0% of the time, Pallas kernels for 41%

profile of v3, /device:TPU:0, one launch (start us, length us, event | category | flops | bytes accessed | tf_op | source)
XLA Modules:
  0.0 1416.0 jit_solution(15052461787424771523)
XLA Ops:
  13.8 18.7 %shard_map.61.refs_0_ = f32[128,8064]{1,0:T(8,128)} custom-call(s32[1]{0:T(128)} %bitcast.4.sel_ref, bf16[1024,2560]{1,0:T(8,128)(2,1)} %h_ref.35, bf16[2560,25088]{1,0:T(8,128)(2,1)} %w_ref.35, f32[128,3584]{1,0:T(8,128)} %shard_map.60.refs_0_), custom_call_target="tpu_custom_call" | custom-call | flops 5284823040 | bytes 45416448 | tf_op jit(solution)/shard_map/pallas_call | solution.py:38
  37.4 24.1 %shard_map.62.refs_0_ = f32[128,12544]{1,0:T(8,128)} custom-call(s32[1]{0:T(128)} %bitcast.4.sel_ref, bf16[1024,2560]{1,0:T(8,128)(2,1)} %h_ref.35, bf16[2560,25088]{1,0:T(8,128)(2,1)} %w_ref.35, f32[128,8064]{1,0:T(8,128)} %shard_map.61.refs_0_), custom_call_target="tpu_custom_call" | custom-call | flops 8220835840 | bytes 70647808 | tf_op jit(solution)/shard_map/pallas_call | solution.py:38
  62.1 24.1 %shard_map.63.refs_0_ = f32[128,12544]{1,0:T(8,128)} custom-call(s32[1]{0:T(128)} %bitcast.4.sel_ref, bf16[1024,2560]{1,0:T(8,128)(2,1)} %h_ref.35, bf16[2560,25088]{1,0:T(8,128)(2,1)} %w_ref.35, f32[128,12544]{1,0:T(8,128)} %shard_map.62.refs_0_), custom_call_target="tpu_custom_call" | custom-call | flops 8220835840 | bytes 70647808 | tf_op jit(solution)/shard_map/pallas_call | solution.py:38
  90.3 24.1 %shard_map.64.refs_0_.own_ref = f32[128,12544]{1,0:T(8,128)} custom-call(s32[1]{0:T(128)} %bitcast.2.sel_ref, bf16[1024,2560]{1,0:T(8,128)(2,1)} %h_ref.35, bf16[2560,25088]{1,0:T(8,128)(2,1)} %w_ref.35, f32[128,12544]{1,0:T(8,128)} %shard_map.63.refs_0_), custom_call_target="tpu_custom_call" | custom-call | flops 8220835840 | bytes 70647808 | tf_op jit(solution)/shard_map/pallas_call | solution.py:38
  114.4 24.2 %shard_map.65.refs_3_.own_ref = f32[128,12544]{1,0:T(8,128)} custom-call(s32[1]{0:T(128)} %bitcast.2.sel_ref, bf16[1024,2560]{1,0:T(8,128)(2,1)} %h_ref.35, bf16[2560,25088]{1,0:T(8,128)(2,1)} %w_ref.35, f32[128,12544]{1,0:T(8,128)} %shard_map.64.refs_0_.own_ref), custom_call_target="tpu_custom_call" | custom-call | flops 8220835840 | bytes 70647808 | tf_op jit(solution)/shard_map/pallas_call | solution.py:38
  138.5 36.3 %collective-permute-done.2.refs_1_ = f32[128,3584]{1,0:T(8,128)} collective-permute-done((f32[128,3584]{1,0:T(8,128)}, f32[128,3584]{1,0:T(8,128)}, u32[]{:S(2)}, u32[]{:S(2)}) %collective-permute-start.2) | collective-permute-done | bytes 1835040 | tf_op jit(solution)/shard_map/ppermute | solution.py:430
  174.8 18.7 %shard_map.66 = (f32[128,12544]{1,0:T(8,128)}, f32[8,128]{1,0:T(8,128)}) custom-call(f32[1024,1]{1,0:T(8,128)} %copy.35.temp_ref, s32[1024,1]{1,0:T(8,128)} %copy.36.tgt_ref, bf16[256,256]{1,0:T(8,128)(2,1)} %fusion.tri_ref, f32[128,12544]{1,0:T(8,128)} %shard_map.64.refs_0_.own_ref, f32[128,896]{1,0:T(8,128)} %collective-permute-done.1.refs_0_, ...), custom_call_target="tpu_custom_call" | custom-call | flops 2466250752 | bytes 19267584 | tf_op jit(solution)/shard_map/pallas_call | solution.py:158
  205.8 24.1 %shard_map.67.refs_0_ = f32[128,12544]{1,0:T(8,128)} custom-call(s32[1]{0:T(128)} %bitcast.4.sel_ref, bf16[1024,2560]{1,0:T(8,128)(2,1)} %h_ref.35, bf16[2560,25088]{1,0:T(8,128)(2,1)} %w_ref.35, f32[8,128]{1,0:T(8,128)} %group_stats.9.refs_0_), custom_call_target="tpu_custom_call" | custom-call | flops 8220835840 | bytes 70647808 | tf_op jit(solution)/shard_map/pallas_call | solution.py:38
  229.9 24.1 %shard_map.68.refs_1_.own_ref = f32[128,12544]{1,0:T(8,128)} custom-call(s32[1]{0:T(128)} %bitcast.2.sel_ref, bf16[1024,2560]{1,0:T(8,128)(2,1)} %h_ref.35, bf16[2560,25088]{1,0:T(8,128)(2,1)} %w_ref.35, f32[128,12544]{1,0:T(8,128)} %shard_map.67.refs_0_), custom_call_target="tpu_custom_call" | custom-call | flops 8220835840 | bytes 70647808 | tf_op jit(solution)/shard_map/pallas_call | solution.py:38
  254.0 58.5 %collective-permute-done.refs_0_ = f32[128,12544]{1,0:T(8,128)} collective-permute-done((f32[128,12544]{1,0:T(8,128)}, f32[128,12544]{1,0:T(8,128)}, u32[]{:S(2)}, u32[]{:S(2)}) %collective-permute-start) | collective-permute-done | bytes 6422560 | tf_op jit(solution)/shard_map/ppermute | solution.py:430
  341.4 108.8 %collective-permute-done.5.other_ref = f32[8,128]{1,0:T(8,128)} collective-permute-done((f32[8,128]{1,0:T(8,128)}, f32[8,128]{1,0:T(8,128)}, u32[]{:S(2)}, u32[]{:S(2)}) %collective-permute-start.5) | collective-permute-done | bytes 4128 | tf_op jit(solution)/shard_map/ppermute | solution.py:430
  457.9 24.1 %shard_map.71.refs_0_ = f32[128,12544]{1,0:T(8,128)} custom-call(s32[1]{0:T(128)} %bitcast.4.sel_ref, bf16[1024,2560]{1,0:T(8,128)(2,1)} %h_ref.35, bf16[2560,25088]{1,0:T(8,128)(2,1)} %w_ref.35, f32[8,128]{1,0:T(8,128)} %get-tuple-element.73.refs_0_.ctin_ref), custom_call_target="tpu_custom_call" | custom-call | flops 8220835840 | bytes 70647808 | tf_op jit(solution)/shard_map/pallas_call | solution.py:38
  482.0 24.1 %shard_map.72.refs_1_.own_ref = f32[128,12544]{1,0:T(8,128)} custom-call(s32[1]{0:T(128)} %bitcast.2.sel_ref, bf16[1024,2560]{1,0:T(8,128)(2,1)} %h_ref.35, bf16[2560,25088]{1,0:T(8,128)(2,1)} %w_ref.35, f32[128,12544]{1,0:T(8,128)} %shard_map.71.refs_0_), custom_call_target="tpu_custom_call" | custom-call | flops 8220835840 | bytes 70647808 | tf_op jit(solution)/shard_map/pallas_call | solution.py:38
  536.9 187.8 %collective-permute-done.4.other_ref = f32[8,128]{1,0:T(8,128)} collective-permute-done((f32[8,128]{1,0:T(8,128)}, f32[8,128]{1,0:T(8,128)}, u32[]{:S(2)}, u32[]{:S(2)}) %collective-permute-start.4) | collective-permute-done | bytes 4128 | tf_op jit(solution)/shard_map/ppermute | solution.py:430
  731.8 24.1 %shard_map.75.refs_0_ = f32[128,12544]{1,0:T(8,128)} custom-call(s32[1]{0:T(128)} %bitcast.4.sel_ref, bf16[1024,2560]{1,0:T(8,128)(2,1)} %h_ref.35, bf16[2560,25088]{1,0:T(8,128)(2,1)} %w_ref.35, f32[8,128]{1,0:T(8,128)} %get-tuple-element.78.refs_0_.ctin_ref), custom_call_target="tpu_custom_call" | custom-call | flops 8220835840 | bytes 70647808 | tf_op jit(solution)/shard_map/pallas_call | solution.py:38
  755.9 24.1 %shard_map.76.refs_1_.own_ref = f32[128,12544]{1,0:T(8,128)} custom-call(s32[1]{0:T(128)} %bitcast.2.sel_ref, bf16[1024,2560]{1,0:T(8,128)(2,1)} %h_ref.35, bf16[2560,25088]{1,0:T(8,128)(2,1)} %w_ref.35, f32[128,12544]{1,0:T(8,128)} %shard_map.75.refs_0_), custom_call_target="tpu_custom_call" | custom-call | flops 8220835840 | bytes 70647808 | tf_op jit(solution)/shard_map/pallas_call | solution.py:38
  815.6 24.1 %shard_map.79.refs_0_ = f32[128,12544]{1,0:T(8,128)} custom-call(s32[1]{0:T(128)} %bitcast.4.sel_ref, bf16[1024,2560]{1,0:T(8,128)(2,1)} %h_ref.35, bf16[2560,25088]{1,0:T(8,128)(2,1)} %w_ref.35, f32[8,128]{1,0:T(8,128)} %get-tuple-element.85.refs_0_.ctin_ref), custom_call_target="tpu_custom_call" | custom-call | flops 8220835840 | bytes 70647808 | tf_op jit(solution)/shard_map/pallas_call | solution.py:38
  839.7 24.1 %shard_map.80.refs_1_.own_ref = f32[128,12544]{1,0:T(8,128)} custom-call(s32[1]{0:T(128)} %bitcast.2.sel_ref, bf16[1024,2560]{1,0:T(8,128)(2,1)} %h_ref.35, bf16[2560,25088]{1,0:T(8,128)(2,1)} %w_ref.35, f32[128,12544]{1,0:T(8,128)} %shard_map.79.refs_0_), custom_call_target="tpu_custom_call" | custom-call | flops 8220835840 | bytes 70647808 | tf_op jit(solution)/shard_map/pallas_call | solution.py:38
  893.3 192.9 %collective-permute-done.11.other_ref = f32[8,128]{1,0:T(8,128)} collective-permute-done((f32[8,128]{1,0:T(8,128)}, f32[8,128]{1,0:T(8,128)}, u32[]{:S(2)}, u32[]{:S(2)}) %collective-permute-start.11) | collective-permute-done | bytes 4128 | tf_op jit(solution)/shard_map/ppermute | solution.py:430
  1093.2 24.1 %shard_map.83 = (f32[32,12544]{1,0:T(8,128)}, f32[48,12544]{1,0:T(8,128)}, f32[32,12544]{1,0:T(8,128)}, f32[16,12544]{1,0:T(8,128)}) custom-call(s32[1]{0:T(128)} %bitcast.4.sel_ref, bf16[1024,2560]{1,0:T(8,128)(2,1)} %h_ref.35, bf16[2560,25088]{1,0:T(8,128)(2,1)} %w_ref.35, f32[8,128]{1,0:T(8,128)} %get-tuple-element.91.refs_0_.ctin_ref), custom_call_target="tpu_custom_call" | custom-call | flops 8220835840 | bytes 70647808 | tf_op jit(solution)/shard_map/pallas_call | solution.py:38
  1117.3 24.1 %shard_map.84.refs_1_.own_ref = f32[128,12544]{1,0:T(8,128)} custom-call(s32[1]{0:T(128)} %bitcast.2.sel_ref, bf16[1024,2560]{1,0:T(8,128)(2,1)} %h_ref.35, bf16[2560,25088]{1,0:T(8,128)(2,1)} %w_ref.35, f32[32,12544]{1,0:T(8,128)} %get-tuple-element.110.refs_0_), custom_call_target="tpu_custom_call" | custom-call | flops 8220835840 | bytes 70647808 | tf_op jit(solution)/shard_map/pallas_call | solution.py:38
  1175.8 24.1 %shard_map.87.refs_1_.own_ref = f32[128,12544]{1,0:T(8,128)} custom-call(s32[1]{0:T(128)} %bitcast.2.sel_ref, bf16[1024,2560]{1,0:T(8,128)(2,1)} %h_ref.35, bf16[2560,25088]{1,0:T(8,128)(2,1)} %w_ref.35, f32[8,128]{1,0:T(8,128)} %get-tuple-element.97.refs_0_.ctin_ref), custom_call_target="tpu_custom_call" | custom-call | flops 8220835840 | bytes 70647808 | tf_op jit(solution)/shard_map/pallas_call | solution.py:38
  1228.3 52.9 %collective-permute-done.16.other_ref = f32[8,128]{1,0:T(8,128)} collective-permute-done((f32[8,128]{1,0:T(8,128)}, f32[8,128]{1,0:T(8,128)}, u32[]{:S(2)}, u32[]{:S(2)}) %collective-permute-start.16) | collective-permute-done | bytes 4128 | tf_op jit(solution)/shard_map/ppermute | solution.py:430
  1305.8 35.7 %collective-permute-done.15.other_ref = f32[8,128]{1,0:T(8,128)} collective-permute-done((f32[8,128]{1,0:T(8,128)}, f32[8,128]{1,0:T(8,128)}, u32[]{:S(2)}, u32[]{:S(2)}) %collective-permute-start.15) | collective-permute-done | bytes 4128 | tf_op jit(solution)/shard_map/ppermute | solution.py:430
  (83 shorter events, 343.4 us)
Async XLA Ops:
  32.5 142.3 %collective-permute-start.3 = (f32[128,8064]{1,0:T(8,128)}, f32[128,8064]{1,0:T(8,128)}, u32[]{:S(2)}, u32[]{:S(2)}) collective-permute-start(f32[128,8064]{1,0:T(8,128)} %shard_map.61.refs_0_), channel_id=1, source_target_pairs={{0,4},{4,0},{1,5},{5,1},{2,6},{6,2},{3,7},{7,3}} | collective-permute-start | bytes 12386312 | tf_op jit(solution)/shard_map/ppermute | solution.py:430
  35.4 103.2 %collective-permute-start.1 = (f32[128,896]{1,0:T(8,128)}, f32[128,896]{1,0:T(8,128)}, u32[]{:S(2)}, u32[]{:S(2)}) collective-permute-start(f32[128,896]{1,0:T(8,128)} %shard_map.59.refs_0_), channel_id=1, source_target_pairs={{0,4},{4,0},{1,5},{5,1},{2,6},{6,2},{3,7},{7,3}} | collective-permute-start | bytes 1376264 | tf_op jit(solution)/shard_map/ppermute | solution.py:430
  35.4 139.5 %collective-permute-start.2 = (f32[128,3584]{1,0:T(8,128)}, f32[128,3584]{1,0:T(8,128)}, u32[]{:S(2)}, u32[]{:S(2)}) collective-permute-start(f32[128,3584]{1,0:T(8,128)} %shard_map.60.refs_0_), channel_id=1, source_target_pairs={{0,4},{4,0},{1,5},{5,1},{2,6},{6,2},{3,7},{7,3}} | collective-permute-start | bytes 5505032 | tf_op jit(solution)/shard_map/ppermute | solution.py:430
  61.4 251.0 %collective-permute-start = (f32[128,12544]{1,0:T(8,128)}, f32[128,12544]{1,0:T(8,128)}, u32[]{:S(2)}, u32[]{:S(2)}) collective-permute-start(f32[128,12544]{1,0:T(8,128)} %shard_map.62.refs_0_), channel_id=1, source_target_pairs={{0,4},{4,0},{1,5},{5,1},{2,6},{6,2},{3,7},{7,3}} | collective-permute-start | bytes 19267592 | tf_op jit(solution)/shard_map/ppermute | solution.py:430
  203.8 302.3 %collective-permute-start.6 = (f32[128,12544]{1,0:T(8,128)}, f32[128,12544]{1,0:T(8,128)}, u32[]{:S(2)}, u32[]{:S(2)}) collective-permute-start(f32[128,12544]{1,0:T(8,128)} %shard_map.63.refs_0_), channel_id=1, source_target_pairs={{0,4},{4,0},{1,5},{5,1},{2,6},{6,2},{3,7},{7,3}} | collective-permute-start | bytes 19267592 | tf_op jit(solution)/shard_map/ppermute | solution.py:430
  204.8 245.4 %collective-permute-start.5 = (f32[8,128]{1,0:T(8,128)}, f32[8,128]{1,0:T(8,128)}, u32[]{:S(2)}, u32[]{:S(2)}) collective-permute-start(f32[8,128]{1,0:T(8,128)} %group_stats.9.refs_0_), channel_id=1, source_target_pairs={{0,4},{4,0},{1,5},{5,1},{2,6},{6,2},{3,7},{7,3}} | collective-permute-start | bytes 12296 | tf_op jit(solution)/shard_map/ppermute | solution.py:430
  340.4 439.6 %collective-permute-start.9 = (f32[128,12544]{1,0:T(8,128)}, f32[128,12544]{1,0:T(8,128)}, u32[]{:S(2)}, u32[]{:S(2)}) collective-permute-start(f32[128,12544]{1,0:T(8,128)} %shard_map.67.refs_0_), channel_id=1, source_target_pairs={{0,4},{4,0},{1,5},{5,1},{2,6},{6,2},{3,7},{7,3}} | collective-permute-start | bytes 19267592 | tf_op jit(solution)/shard_map/ppermute | solution.py:430
  533.8 330.0 %collective-permute-start.7 = (f32[128,12544]{1,0:T(8,128)}, f32[128,12544]{1,0:T(8,128)}, u32[]{:S(2)}, u32[]{:S(2)}) collective-permute-start(f32[128,12544]{1,0:T(8,128)} %shard_map.71.refs_0_), channel_id=1, source_target_pairs={{0,4},{4,0},{1,5},{5,1},{2,6},{6,2},{3,7},{7,3}} | collective-permute-start | bytes 19267592 | tf_op jit(solution)/shard_map/ppermute | solution.py:430
  534.9 189.9 %collective-permute-start.4 = (f32[8,128]{1,0:T(8,128)}, f32[8,128]{1,0:T(8,128)}, u32[]{:S(2)}, u32[]{:S(2)}) collective-permute-start(f32[8,128]{1,0:T(8,128)} %group_stats.10.refs_0_), channel_id=1, source_target_pairs={{0,4},{4,0},{1,5},{5,1},{2,6},{6,2},{3,7},{7,3}} | collective-permute-start | bytes 12296 | tf_op jit(solution)/shard_map/ppermute | solution.py:430
  535.8 272.6 %collective-permute-start.8 = (f32[8,128]{1,0:T(8,128)}, f32[8,128]{1,0:T(8,128)}, u32[]{:S(2)}, u32[]{:S(2)}) collective-permute-start(f32[8,128]{1,0:T(8,128)} %group_stats.11.refs_1_), channel_id=1, source_target_pairs={{0,4},{4,0},{1,5},{5,1},{2,6},{6,2},{3,7},{7,3}} | collective-permute-start | bytes 12296 | tf_op jit(solution)/shard_map/ppermute | solution.py:430
  807.5 334.0 %collective-permute-start.12 = (f32[128,12544]{1,0:T(8,128)}, f32[128,12544]{1,0:T(8,128)}, u32[]{:S(2)}, u32[]{:S(2)}) collective-permute-start(f32[128,12544]{1,0:T(8,128)} %shard_map.75.refs_0_), channel_id=1, source_target_pairs={{0,4},{4,0},{1,5},{5,1},{2,6},{6,2},{3,7},{7,3}} | collective-permute-start | bytes 19267592 | tf_op jit(solution)/shard_map/ppermute | solution.py:430
  890.2 309.6 %collective-permute-start.13 = (f32[128,12544]{1,0:T(8,128)}, f32[128,12544]{1,0:T(8,128)}, u32[]{:S(2)}, u32[]{:S(2)}) collective-permute-start(f32[128,12544]{1,0:T(8,128)} %shard_map.79.refs_0_), channel_id=1, source_target_pairs={{0,4},{4,0},{1,5},{5,1},{2,6},{6,2},{3,7},{7,3}} | collective-permute-start | bytes 19267592 | tf_op jit(solution)/shard_map/ppermute | solution.py:430
  891.3 194.9 %collective-permute-start.11 = (f32[8,128]{1,0:T(8,128)}, f32[8,128]{1,0:T(8,128)}, u32[]{:S(2)}, u32[]{:S(2)}) collective-permute-start(f32[8,128]{1,0:T(8,128)} %group_stats.12.refs_1_), channel_id=1, source_target_pairs={{0,4},{4,0},{1,5},{5,1},{2,6},{6,2},{3,7},{7,3}} | collective-permute-start | bytes 12296 | tf_op jit(solution)/shard_map/ppermute | solution.py:430
  892.3 276.4 %collective-permute-start.10 = (f32[8,128]{1,0:T(8,128)}, f32[8,128]{1,0:T(8,128)}, u32[]{:S(2)}, u32[]{:S(2)}) collective-permute-start(f32[8,128]{1,0:T(8,128)} %group_stats.13.refs_1_), channel_id=1, source_target_pairs={{0,4},{4,0},{1,5},{5,1},{2,6},{6,2},{3,7},{7,3}} | collective-permute-start | bytes 12296 | tf_op jit(solution)/shard_map/ppermute | solution.py:430
  1167.7 120.7 %collective-permute-start.17 = (f32[32,12544]{1,0:T(8,128)}, f32[32,12544]{1,0:T(8,128)}, u32[]{:S(2)}, u32[]{:S(2)}) collective-permute-start(f32[32,12544]{1,0:T(8,128)} %get-tuple-element.110.refs_0_), channel_id=1, source_target_pairs={{0,4},{4,0},{1,5},{5,1},{2,6},{6,2},{3,7},{7,3}} | collective-permute-start | bytes 4816904 | tf_op jit(solution)/shard_map/ppermute | solution.py:430
  1226.3 122.3 %collective-permute-start.14 = (f32[48,12544]{1,0:T(8,128)}, f32[48,12544]{1,0:T(8,128)}, u32[]{:S(2)}, u32[]{:S(2)}) collective-permute-start(f32[48,12544]{1,0:T(8,128)} %get-tuple-element.102), channel_id=1, source_target_pairs={{0,4},{4,0},{1,5},{5,1},{2,6},{6,2},{3,7},{7,3}} | collective-permute-start | bytes 7225352 | tf_op jit(solution)/shard_map/ppermute | solution.py:430
  1227.3 54.0 %collective-permute-start.16 = (f32[8,128]{1,0:T(8,128)}, f32[8,128]{1,0:T(8,128)}, u32[]{:S(2)}, u32[]{:S(2)}) collective-permute-start(f32[8,128]{1,0:T(8,128)} %group_stats.14.refs_1_), channel_id=1, source_target_pairs={{0,4},{4,0},{1,5},{5,1},{2,6},{6,2},{3,7},{7,3}} | collective-permute-start | bytes 12296 | tf_op jit(solution)/shard_map/ppermute | solution.py:430
  1303.7 88.8 %collective-permute-start.19 = (f32[32,12544]{1,0:T(8,128)}, f32[32,12544]{1,0:T(8,128)}, u32[]{:S(2)}, u32[]{:S(2)}) collective-permute-start(f32[32,12544]{1,0:T(8,128)} %get-tuple-element.116), channel_id=1, source_target_pairs={{0,4},{4,0},{1,5},{5,1},{2,6},{6,2},{3,7},{7,3}} | collective-permute-start | bytes 4816904 | tf_op jit(solution)/shard_map/ppermute | solution.py:430
  1304.8 36.7 %collective-permute-start.15 = (f32[8,128]{1,0:T(8,128)}, f32[8,128]{1,0:T(8,128)}, u32[]{:S(2)}, u32[]{:S(2)}) collective-permute-start(f32[8,128]{1,0:T(8,128)} %group_stats.15.refs_1_), channel_id=1, source_target_pairs={{0,4},{4,0},{1,5},{5,1},{2,6},{6,2},{3,7},{7,3}} | collective-permute-start | bytes 12296 | tf_op jit(solution)/shard_map/ppermute | solution.py:430
  1368.4 37.2 %collective-permute-start.18 = (f32[16,12544]{1,0:T(8,128)}, f32[16,12544]{1,0:T(8,128)}, u32[]{:S(2)}, u32[]{:S(2)}) collective-permute-start(f32[16,12544]{1,0:T(8,128)} %get-tuple-element.115), channel_id=1, source_target_pairs={{0,4},{4,0},{1,5},{5,1},{2,6},{6,2},{3,7},{7,3}} | collective-permute-start | bytes 2408456 | tf_op jit(solution)/shard_map/ppermute | solution.py:430
  1369.4 19.6 %collective-permute-start.20 = (f32[8,128]{1,0:T(8,128)}, f32[8,128]{1,0:T(8,128)}, u32[]{:S(2)}, u32[]{:S(2)}) collective-permute-start(f32[8,128]{1,0:T(8,128)} %group_stats.16.refs_1_), channel_id=1, source_target_pairs={{0,4},{4,0},{1,5},{5,1},{2,6},{6,2},{3,7},{7,3}} | collective-permute-start | bytes 12296 | tf_op jit(solution)/shard_map/ppermute | solution.py:430
  1370.4 30.3 %collective-permute-start.21 = (f32[8,128]{1,0:T(8,128)}, f32[8,128]{1,0:T(8,128)}, u32[]{:S(2)}, u32[]{:S(2)}) collective-permute-start(f32[8,128]{1,0:T(8,128)} %group_stats.17.refs_1_), channel_id=1, source_target_pairs={{0,4},{4,0},{1,5},{5,1},{2,6},{6,2},{3,7},{7,3}} | collective-permute-start | bytes 12296 | tf_op jit(solution)/shard_map/ppermute | solution.py:430

commit v4 on v3

--- a/solution.py
+++ b/solution.py
@@ -11,6 +11,7 @@
 
 CT = 256
 SUB = 32
+LAST_VMEM = 67043328 - 9 * 512 * 1024
 ALL_VMEM = 67043328
 
 
@@ -53,13 +54,12 @@
     )(half, h, w, *deps)
 
 
-def local_kernel(temp_ref, tgt_ref, tri_ref, own_ref, *refs, npieces, has_prev, skip, at, group, share):
+def local_kernel(temp_ref, tgt_ref, tri_ref, own_ref, *refs, npieces, has_prev, skip, at, group, share, keep):
     recv_refs = refs[:npieces]
     prev_ref = refs[npieces] if has_prev else None
     if share:
-        pre_ref, ab_ref, at_tgt_ref, z_s, hi_s, mid_s, lo_s, st_s, st_ref, slots, send_sem, recv_sem, pre_s, out_sem = refs[npieces + has_prev + skip:]
+        pre_ref, ab_ref, at_tgt_ref, z_s, hi_s, mid_s, lo_s, st_s, st_ref, slots, send_sem, recv_sem = refs[npieces + has_prev + skip:]
         announce()
-        pre_hbm, pre_ref = pre_ref, pre_s
     else:
         pre_ref, st_ref, z_s, hi_s, mid_s, lo_s, st_s = refs[npieces + has_prev + skip:]
     step, nsteps = pl.program_id(0), pl.num_programs(0)
@@ -126,6 +126,7 @@
     if share:
         copies = spread(st_ref, slots, send_sem, recv_sem)
     tri = tri_ref[...]
+    out_rows = pl.ds(pl.multiple_of(step * rows, rows), rows) if keep else slice(None)
 
     def prefix_step(g, carry):
         span = pl.ds(g * group, group)
@@ -135,40 +136,39 @@
         for k in range(group):
             blk = pre[k * rows:(k + 1) * rows]
             dst = pl.ds(pl.multiple_of((g * group + k) * CT, CT), CT)
-            pre_ref[:, dst] = blk + carry
+            pre_ref[out_rows, dst] = blk + carry
             carry = carry + jnp.broadcast_to(blk[:, CT - 1:CT], (rows, CT))
         return carry
 
     lax.fori_loop(0, nt // group, prefix_step, zero)
     if share:
-        put = pltpu.make_async_copy(pre_ref, pre_hbm, out_sem)
-        put.start()
         gather(copies, st_ref, slots, ab_ref, at_tgt_ref)
-        put.wait()
-
-
-def local_prefix(temp, tgt, tri, own, at, recvs, rows, row0, prev, deps, share=False):
+
+
+def local_prefix(temp, tgt, tri, own, at, recvs, rows, row0, prev, deps, share=False, keep=False):
     cols = own.shape[1]
     nt = cols // CT
     sub = math.gcd(SUB, rows, at)
     small = (128, 8) if share else (8,)
+    vmem = pl.BlockSpec(memory_space=pltpu.VMEM)
     extra = ([] if prev is None else [prev]) + list(deps)
     extra_specs = ([] if prev is None else [pl.BlockSpec((8, 128), lambda i: (0, 0))])
     extra_specs += [pl.BlockSpec(memory_space=pl.ANY)] * len(deps)
     return pl.pallas_call(
         functools.partial(
-            local_kernel, npieces=len(recvs), has_prev=int(prev is not None), skip=len(deps), at=at, group=7, share=share),
+            local_kernel, npieces=len(recvs), has_prev=int(prev is not None), skip=len(deps), at=at, group=7 if sub > 16 else 49,
+            share=share, keep=keep),
         grid=(rows // sub,),
-        out_shape=[jax.ShapeDtypeStruct((rows, cols), jnp.float32)]
-        + [jax.ShapeDtypeStruct((n, 128), jnp.float32) for n in small],
+        out_shape=[(pltpu.VMEM if keep else jax.ShapeDtypeStruct)((rows, cols), jnp.float32)]
+        + [(pltpu.VMEM if share else jax.ShapeDtypeStruct)((n, 128), jnp.float32) for n in small],
         in_specs=[
             pl.BlockSpec((sub, 1), lambda i: (row0 // sub + i, 0)),
             pl.BlockSpec((sub, 1), lambda i: (row0 // sub + i, 0)),
             pl.BlockSpec((CT, CT), lambda i: (0, 0)),
             pl.BlockSpec((sub, cols), lambda i: (at // sub + i, 0)),
         ] + [pl.BlockSpec((sub, r.shape[1]), lambda i: (i, 0)) for r in recvs] + extra_specs,
-        out_specs=[pl.BlockSpec(memory_space=pl.ANY) if share else pl.BlockSpec((sub, cols), lambda i: (i, 0))]
-        + [pl.BlockSpec((n, 128), lambda i: (0, 0)) for n in small],
+        out_specs=[vmem if keep else pl.BlockSpec((sub, cols), lambda i: (i, 0))]
+        + ([vmem, vmem] if share else [pl.BlockSpec((8, 128), lambda i: (0, 0))]),
         scratch_shapes=[
             pltpu.VMEM((nt, sub, CT), jnp.float32),
             pltpu.VMEM((nt, sub, CT), jnp.bfloat16),
@@ -180,13 +180,11 @@
             pltpu.VMEM((7, 8, 128), jnp.float32),
             pltpu.SemaphoreType.DMA((7,)),
             pltpu.SemaphoreType.DMA((7,)),
-            pltpu.VMEM((rows, cols), jnp.float32),
-            pltpu.SemaphoreType.DMA,
         ] if share else []),
         cost_estimate=pl.CostEstimate(
             flops=6 * rows * cols * CT, bytes_accessed=rows * cols * 12, transcendentals=rows * cols),
         compiler_params=pltpu.CompilerParams(
-            dimension_semantics=("arbitrary",), vmem_limit_bytes=ALL_VMEM,
+            dimension_semantics=("arbitrary",), vmem_limit_bytes=LAST_VMEM if keep else ALL_VMEM,
             **(dict(collective_id=0, has_side_effects=True) if share else {})),
     )(temp, tgt, tri, own, *recvs, *extra)
 
@@ -312,7 +310,7 @@
     out_ref[...] = pre_ref[...] * ab[:, 0:1] + ab[:, 1:2]
 
 
-def finish(pos, pre, st, mine, other, out, ct, all_rows, blk, at, row0, deps):
+def finish(pos, pre, st, mine, other, out, ct, all_rows, blk, at, row0, deps, vmem):
     rows, cols = pre.shape
     sub = math.gcd(SUB, rows, at)
     tail = ([] if out is None else [out]) + list(deps)
@@ -331,7 +329,7 @@
         ),
         input_output_aliases={} if out is None else {6: 0},
         cost_estimate=pl.CostEstimate(flops=64 * rows * cols, bytes_accessed=rows * cols * 8, transcendentals=0),
-        compiler_params=pltpu.CompilerParams(dimension_semantics=("arbitrary",), vmem_limit_bytes=ALL_VMEM),
+        compiler_params=pltpu.CompilerParams(dimension_semantics=("arbitrary",), vmem_limit_bytes=vmem),
     )(pos, pre, st, mine, other, ct, *tail)
 
 
@@ -343,8 +341,13 @@
     ct_ref[...] = merged(ctin_ref[...], at_tgt_ref[...], blk, at, rows)
     for i, (lo, hi) in enumerate(ends):
         @pl.when((step >= lo) & (step < hi))
-        def _(pre_ref=refs[i]):
-            out_ref[...] = pre_ref[...] * ab[:, 0:1] + ab[:, 1:2]
+        def _(pre_ref=refs[i], lo=lo):
+            here = pl.ds(pl.multiple_of((step - lo) * sub, sub), sub)
+            out_ref[...] = pre_ref[here, :] * ab[:, 0:1] + ab[:, 1:2]
+
+
+def held(x):
+    return pltpu.with_memory_space_constraint(x, pltpu.VMEM)
 
 
 def finish_last(ab, at_tgt, ct, pres, out, blk, at, row0, deps):
@@ -355,19 +358,20 @@
     for r in rows:
         ends.append((lo, lo + r // sub))
         lo += r // sub
+    whole = pl.BlockSpec(memory_space=pltpu.VMEM)
     small = pl.BlockSpec((8, 128), lambda i: (0, 0))
     return pl.pallas_call(
         functools.partial(last_kernel, blk=blk, at=at, rows=sum(rows), ends=tuple(ends)),
         grid=(lo,),
         out_shape=[jax.ShapeDtypeStruct(out.shape, jnp.float32), jax.ShapeDtypeStruct((8, 128), jnp.float32)],
-        in_specs=[pl.BlockSpec((128, 128), lambda i: (0, 0)), small, small]
-        + [pl.BlockSpec((sub, cols), lambda i, lo=lo, hi=hi: (jnp.clip(i - lo, 0, hi - lo - 1), 0)) for lo, hi in ends]
+        in_specs=[whole, whole, small]
+        + [whole] * len(pres)
         + [pl.BlockSpec(memory_space=pl.ANY)] * (1 + len(deps)),
         out_specs=[pl.BlockSpec((sub, cols), lambda i: (row0 // sub + i, 0)), small],
         input_output_aliases={3 + len(pres): 0},
-        compiler_params=pltpu.CompilerParams(dimension_semantics=("arbitrary",), vmem_limit_bytes=ALL_VMEM),
+        compiler_params=pltpu.CompilerParams(dimension_semantics=("arbitrary",), vmem_limit_bytes=LAST_VMEM),
         name="finish_last",
-    )(ab, at_tgt, ct, *pres, out, *deps)
+    )(held(ab), held(at_tgt), ct, *map(held, pres), out, *deps)
 
 
 def solution(mesh):
@@ -437,14 +441,16 @@
         def close(k):
             nonlocal out, ct, tok
             b, at, _ = units[k]
-            out, ct = finish(pos, pres[k], *stats[k], out, ct, rows_all, b, at, b * blk + at, (tok,))
+            out, ct = finish(pos, pres[k], *stats[k], out, ct, rows_all, b, at, b * blk + at, (tok,),
+                             LAST_VMEM if k == nu - 3 else ALL_VMEM)
             tok = ct
 
         prev = None
         for k, (b, at, rows) in enumerate(units):
             share = k == nu - 1
             pres[k], *small = local_prefix(
-                temp2, tgt2, tri, owns[b], at, recvs[k], rows, b * blk + at, prev, (tok,), share)
+                temp2, tgt2, tri, owns[b], at, recvs[k], rows, b * blk + at, prev, (tok,), share,
+                k >= nu - 2)
             if share:
                 at = units[k - 1][1]
                 out, ct = finish_last(*small, ct, [pres[k - 1], pres[k]], out, b, at, b * blk + at, (tok,))

time: 1420 us -> 1410 us (level)
  no operation moved by 1% of the time
where the time goes in v4:
time: 1410 us
  waiting for transfers between devices  691 us (49%)
  Pallas kernels  621 us (44%)
  blocking collectives  66.4 us (5%)
  starting transfers between devices  23.2 us (2%)
    ppermute x22, waiting for transfers between devices, send(): return [lax.ppermute(a, 'hid', swap) for a in arrays]  691 us
    pallas_call x18, Pallas kernels, partial_products(): pl.pallas_call(functools.partial(mm_kernel, splits=splits, ksteps=ksteps)...  393 us
    pallas_call x11, Pallas kernels, local_prefix(): pl.pallas_call(functools.partial(local_kernel, npieces=len(recvs), has_pr...  148 us
    all_gather x9, blocking collectives, pipeline(): mine = lax.all_gather(st, 'vocab')  66.4 us
    pallas_call x9, Pallas kernels, finish(): pl.pallas_call(functools.partial(final_kernel, blk=blk, at=at, rows=rows)...  58.1 us
  transfers between devices with their start and end apart: 22, of which 8 were waited for; matrix products, arithmetic and copies ran while one was open for 0% of the time, Pallas kernels for 41%

profile of v4, /device:TPU:0, one launch (start us, length us, event | category | flops | bytes accessed | tf_op | source)
XLA Modules:
  0.0 1406.7 jit_solution(10820212755195050554)
XLA Ops:
  13.8 18.7 %shard_map.61.refs_0_ = f32[128,8064]{1,0:T(8,128)} custom-call(s32[1]{0:T(128)} %bitcast.4.sel_ref, bf16[1024,2560]{1,0:T(8,128)(2,1)} %h_ref.35, bf16[2560,25088]{1,0:T(8,128)(2,1)} %w_ref.35, f32[128,3584]{1,0:T(8,128)} %shard_map.60.refs_0_), custom_call_target="tpu_custom_call" | custom-call | flops 5284823040 | bytes 45416448 | tf_op jit(solution)/shard_map/pallas_call | solution.py:39
  37.4 24.1 %shard_map.62.refs_0_ = f32[128,12544]{1,0:T(8,128)} custom-call(s32[1]{0:T(128)} %bitcast.4.sel_ref, bf16[1024,2560]{1,0:T(8,128)(2,1)} %h_ref.35, bf16[2560,25088]{1,0:T(8,128)(2,1)} %w_ref.35, f32[128,8064]{1,0:T(8,128)} %shard_map.61.refs_0_), custom_call_target="tpu_custom_call" | custom-call | flops 8220835840 | bytes 70647808 | tf_op jit(solution)/shard_map/pallas_call | solution.py:39
  62.1 24.1 %shard_map.63.refs_0_ = f32[128,12544]{1,0:T(8,128)} custom-call(s32[1]{0:T(128)} %bitcast.4.sel_ref, bf16[1024,2560]{1,0:T(8,128)(2,1)} %h_ref.35, bf16[2560,25088]{1,0:T(8,128)(2,1)} %w_ref.35, f32[128,12544]{1,0:T(8,128)} %shard_map.62.refs_0_), custom_call_target="tpu_custom_call" | custom-call | flops 8220835840 | bytes 70647808 | tf_op jit(solution)/shard_map/pallas_call | solution.py:39
  90.3 24.1 %shard_map.64.refs_0_.own_ref = f32[128,12544]{1,0:T(8,128)} custom-call(s32[1]{0:T(128)} %bitcast.2.sel_ref, bf16[1024,2560]{1,0:T(8,128)(2,1)} %h_ref.35, bf16[2560,25088]{1,0:T(8,128)(2,1)} %w_ref.35, f32[128,12544]{1,0:T(8,128)} %shard_map.63.refs_0_), custom_call_target="tpu_custom_call" | custom-call | flops 8220835840 | bytes 70647808 | tf_op jit(solution)/shard_map/pallas_call | solution.py:39
  114.4 24.2 %shard_map.65.refs_3_.own_ref = f32[128,12544]{1,0:T(8,128)} custom-call(s32[1]{0:T(128)} %bitcast.2.sel_ref, bf16[1024,2560]{1,0:T(8,128)(2,1)} %h_ref.35, bf16[2560,25088]{1,0:T(8,128)(2,1)} %w_ref.35, f32[128,12544]{1,0:T(8,128)} %shard_map.64.refs_0_.own_ref), custom_call_target="tpu_custom_call" | custom-call | flops 8220835840 | bytes 70647808 | tf_op jit(solution)/shard_map/pallas_call | solution.py:39
  138.5 36.3 %collective-permute-done.2.refs_1_ = f32[128,3584]{1,0:T(8,128)} collective-permute-done((f32[128,3584]{1,0:T(8,128)}, f32[128,3584]{1,0:T(8,128)}, u32[]{:S(2)}, u32[]{:S(2)}) %collective-permute-start.2) | collective-permute-done | bytes 1835040 | tf_op jit(solution)/shard_map/ppermute | solution.py:434
  174.8 18.7 %shard_map.66 = (f32[128,12544]{1,0:T(8,128)}, f32[8,128]{1,0:T(8,128)}) custom-call(f32[1024,1]{1,0:T(8,128)} %copy.35.temp_ref, s32[1024,1]{1,0:T(8,128)} %copy.36.tgt_ref, bf16[256,256]{1,0:T(8,128)(2,1)} %fusion.tri_ref, f32[128,12544]{1,0:T(8,128)} %shard_map.64.refs_0_.own_ref, f32[128,896]{1,0:T(8,128)} %collective-permute-done.1.refs_0_, ...), custom_call_target="tpu_custom_call" | custom-call | flops 2466250752 | bytes 19267584 | tf_op jit(solution)/shard_map/pallas_call | solution.py:157
  205.8 24.1 %shard_map.67.refs_0_ = f32[128,12544]{1,0:T(8,128)} custom-call(s32[1]{0:T(128)} %bitcast.4.sel_ref, bf16[1024,2560]{1,0:T(8,128)(2,1)} %h_ref.35, bf16[2560,25088]{1,0:T(8,128)(2,1)} %w_ref.35, f32[8,128]{1,0:T(8,128)} %group_stats.9.refs_0_), custom_call_target="tpu_custom_call" | custom-call | flops 8220835840 | bytes 70647808 | tf_op jit(solution)/shard_map/pallas_call | solution.py:39
  229.9 24.1 %shard_map.68.refs_1_.own_ref = f32[128,12544]{1,0:T(8,128)} custom-call(s32[1]{0:T(128)} %bitcast.2.sel_ref, bf16[1024,2560]{1,0:T(8,128)(2,1)} %h_ref.35, bf16[2560,25088]{1,0:T(8,128)(2,1)} %w_ref.35, f32[128,12544]{1,0:T(8,128)} %shard_map.67.refs_0_), custom_call_target="tpu_custom_call" | custom-call | flops 8220835840 | bytes 70647808 | tf_op jit(solution)/shard_map/pallas_call | solution.py:39
  254.0 58.5 %collective-permute-done.refs_0_ = f32[128,12544]{1,0:T(8,128)} collective-permute-done((f32[128,12544]{1,0:T(8,128)}, f32[128,12544]{1,0:T(8,128)}, u32[]{:S(2)}, u32[]{:S(2)}) %collective-permute-start) | collective-permute-done | bytes 6422560 | tf_op jit(solution)/shard_map/ppermute | solution.py:434
  341.4 108.8 %collective-permute-done.5.other_ref = f32[8,128]{1,0:T(8,128)} collective-permute-done((f32[8,128]{1,0:T(8,128)}, f32[8,128]{1,0:T(8,128)}, u32[]{:S(2)}, u32[]{:S(2)}) %collective-permute-start.5) | collective-permute-done | bytes 4128 | tf_op jit(solution)/shard_map/ppermute | solution.py:434
  457.9 24.1 %shard_map.71.refs_0_ = f32[128,12544]{1,0:T(8,128)} custom-call(s32[1]{0:T(128)} %bitcast.4.sel_ref, bf16[1024,2560]{1,0:T(8,128)(2,1)} %h_ref.35, bf16[2560,25088]{1,0:T(8,128)(2,1)} %w_ref.35, f32[8,128]{1,0:T(8,128)} %get-tuple-element.73.refs_0_.ctin_ref), custom_call_target="tpu_custom_call" | custom-call | flops 8220835840 | bytes 70647808 | tf_op jit(solution)/shard_map/pallas_call | solution.py:39
  482.0 24.1 %shard_map.72.refs_1_.own_ref = f32[128,12544]{1,0:T(8,128)} custom-call(s32[1]{0:T(128)} %bitcast.2.sel_ref, bf16[1024,2560]{1,0:T(8,128)(2,1)} %h_ref.35, bf16[2560,25088]{1,0:T(8,128)(2,1)} %w_ref.35, f32[128,12544]{1,0:T(8,128)} %shard_map.71.refs_0_), custom_call_target="tpu_custom_call" | custom-call | flops 8220835840 | bytes 70647808 | tf_op jit(solution)/shard_map/pallas_call | solution.py:39
  536.9 187.8 %collective-permute-done.4.other_ref = f32[8,128]{1,0:T(8,128)} collective-permute-done((f32[8,128]{1,0:T(8,128)}, f32[8,128]{1,0:T(8,128)}, u32[]{:S(2)}, u32[]{:S(2)}) %collective-permute-start.4) | collective-permute-done | bytes 4128 | tf_op jit(solution)/shard_map/ppermute | solution.py:434
  731.8 24.1 %shard_map.75.refs_0_ = f32[128,12544]{1,0:T(8,128)} custom-call(s32[1]{0:T(128)} %bitcast.4.sel_ref, bf16[1024,2560]{1,0:T(8,128)(2,1)} %h_ref.35, bf16[2560,25088]{1,0:T(8,128)(2,1)} %w_ref.35, f32[8,128]{1,0:T(8,128)} %get-tuple-element.78.refs_0_.ctin_ref), custom_call_target="tpu_custom_call" | custom-call | flops 8220835840 | bytes 70647808 | tf_op jit(solution)/shard_map/pallas_call | solution.py:39
  755.9 24.1 %shard_map.76.refs_1_.own_ref = f32[128,12544]{1,0:T(8,128)} custom-call(s32[1]{0:T(128)} %bitcast.2.sel_ref, bf16[1024,2560]{1,0:T(8,128)(2,1)} %h_ref.35, bf16[2560,25088]{1,0:T(8,128)(2,1)} %w_ref.35, f32[128,12544]{1,0:T(8,128)} %shard_map.75.refs_0_), custom_call_target="tpu_custom_call" | custom-call | flops 8220835840 | bytes 70647808 | tf_op jit(solution)/shard_map/pallas_call | solution.py:39
  815.6 24.1 %shard_map.79.refs_0_ = f32[128,12544]{1,0:T(8,128)} custom-call(s32[1]{0:T(128)} %bitcast.4.sel_ref, bf16[1024,2560]{1,0:T(8,128)(2,1)} %h_ref.35, bf16[2560,25088]{1,0:T(8,128)(2,1)} %w_ref.35, f32[8,128]{1,0:T(8,128)} %get-tuple-element.85.refs_0_.ctin_ref), custom_call_target="tpu_custom_call" | custom-call | flops 8220835840 | bytes 70647808 | tf_op jit(solution)/shard_map/pallas_call | solution.py:39
  839.7 24.1 %shard_map.80.refs_1_.own_ref = f32[128,12544]{1,0:T(8,128)} custom-call(s32[1]{0:T(128)} %bitcast.2.sel_ref, bf16[1024,2560]{1,0:T(8,128)(2,1)} %h_ref.35, bf16[2560,25088]{1,0:T(8,128)(2,1)} %w_ref.35, f32[128,12544]{1,0:T(8,128)} %shard_map.79.refs_0_), custom_call_target="tpu_custom_call" | custom-call | flops 8220835840 | bytes 70647808 | tf_op jit(solution)/shard_map/pallas_call | solution.py:39
  893.3 192.9 %collective-permute-done.11.other_ref = f32[8,128]{1,0:T(8,128)} collective-permute-done((f32[8,128]{1,0:T(8,128)}, f32[8,128]{1,0:T(8,128)}, u32[]{:S(2)}, u32[]{:S(2)}) %collective-permute-start.11) | collective-permute-done | bytes 4128 | tf_op jit(solution)/shard_map/ppermute | solution.py:434
  1093.2 24.1 %shard_map.83 = (f32[32,12544]{1,0:T(8,128)}, f32[48,12544]{1,0:T(8,128)}, f32[32,12544]{1,0:T(8,128)}, f32[16,12544]{1,0:T(8,128)}) custom-call(s32[1]{0:T(128)} %bitcast.4.sel_ref, bf16[1024,2560]{1,0:T(8,128)(2,1)} %h_ref.35, bf16[2560,25088]{1,0:T(8,128)(2,1)} %w_ref.35, f32[8,128]{1,0:T(8,128)} %get-tuple-element.91.refs_0_.ctin_ref), custom_call_target="tpu_custom_call" | custom-call | flops 8220835840 | bytes 70647808 | tf_op jit(solution)/shard_map/pallas_call | solution.py:39
  1117.3 24.1 %shard_map.84.refs_1_.own_ref = f32[128,12544]{1,0:T(8,128)} custom-call(s32[1]{0:T(128)} %bitcast.2.sel_ref, bf16[1024,2560]{1,0:T(8,128)(2,1)} %h_ref.35, bf16[2560,25088]{1,0:T(8,128)(2,1)} %w_ref.35, f32[32,12544]{1,0:T(8,128)} %get-tuple-element.110.refs_0_), custom_call_target="tpu_custom_call" | custom-call | flops 8220835840 | bytes 70647808 | tf_op jit(solution)/shard_map/pallas_call | solution.py:39
  1175.8 24.1 %shard_map.87.refs_1_.own_ref = f32[128,12544]{1,0:T(8,128)} custom-call(s32[1]{0:T(128)} %bitcast.2.sel_ref, bf16[1024,2560]{1,0:T(8,128)(2,1)} %h_ref.35, bf16[2560,25088]{1,0:T(8,128)(2,1)} %w_ref.35, f32[8,128]{1,0:T(8,128)} %get-tuple-element.97.refs_0_.ctin_ref), custom_call_target="tpu_custom_call" | custom-call | flops 8220835840 | bytes 70647808 | tf_op jit(solution)/shard_map/pallas_call | solution.py:39
  1228.3 52.9 %collective-permute-done.16.other_ref = f32[8,128]{1,0:T(8,128)} collective-permute-done((f32[8,128]{1,0:T(8,128)}, f32[8,128]{1,0:T(8,128)}, u32[]{:S(2)}, u32[]{:S(2)}) %collective-permute-start.16) | collective-permute-done | bytes 4128 | tf_op jit(solution)/shard_map/ppermute | solution.py:434
  1305.8 35.7 %collective-permute-done.15.other_ref = f32[8,128]{1,0:T(8,128)} collective-permute-done((f32[8,128]{1,0:T(8,128)}, f32[8,128]{1,0:T(8,128)}, u32[]{:S(2)}, u32[]{:S(2)}) %collective-permute-start.15) | collective-permute-done | bytes 4128 | tf_op jit(solution)/shard_map/ppermute | solution.py:434
  (83 shorter events, 334.1 us)
Async XLA Ops:
  32.5 142.3 %collective-permute-start.3 = (f32[128,8064]{1,0:T(8,128)}, f32[128,8064]{1,0:T(8,128)}, u32[]{:S(2)}, u32[]{:S(2)}) collective-permute-start(f32[128,8064]{1,0:T(8,128)} %shard_map.61.refs_0_), channel_id=1, source_target_pairs={{0,4},{4,0},{1,5},{5,1},{2,6},{6,2},{3,7},{7,3}} | collective-permute-start | bytes 12386312 | tf_op jit(solution)/shard_map/ppermute | solution.py:434
  35.4 103.2 %collective-permute-start.1 = (f32[128,896]{1,0:T(8,128)}, f32[128,896]{1,0:T(8,128)}, u32[]{:S(2)}, u32[]{:S(2)}) collective-permute-start(f32[128,896]{1,0:T(8,128)} %shard_map.59.refs_0_), channel_id=1, source_target_pairs={{0,4},{4,0},{1,5},{5,1},{2,6},{6,2},{3,7},{7,3}} | collective-permute-start | bytes 1376264 | tf_op jit(solution)/shard_map/ppermute | solution.py:434
  35.4 139.5 %collective-permute-start.2 = (f32[128,3584]{1,0:T(8,128)}, f32[128,3584]{1,0:T(8,128)}, u32[]{:S(2)}, u32[]{:S(2)}) collective-permute-start(f32[128,3584]{1,0:T(8,128)} %shard_map.60.refs_0_), channel_id=1, source_target_pairs={{0,4},{4,0},{1,5},{5,1},{2,6},{6,2},{3,7},{7,3}} | collective-permute-start | bytes 5505032 | tf_op jit(solution)/shard_map/ppermute | solution.py:434
  61.4 251.0 %collective-permute-start = (f32[128,12544]{1,0:T(8,128)}, f32[128,12544]{1,0:T(8,128)}, u32[]{:S(2)}, u32[]{:S(2)}) collective-permute-start(f32[128,12544]{1,0:T(8,128)} %shard_map.62.refs_0_), channel_id=1, source_target_pairs={{0,4},{4,0},{1,5},{5,1},{2,6},{6,2},{3,7},{7,3}} | collective-permute-start | bytes 19267592 | tf_op jit(solution)/shard_map/ppermute | solution.py:434
  203.8 302.3 %collective-permute-start.6 = (f32[128,12544]{1,0:T(8,128)}, f32[128,12544]{1,0:T(8,128)}, u32[]{:S(2)}, u32[]{:S(2)}) collective-permute-start(f32[128,12544]{1,0:T(8,128)} %shard_map.63.refs_0_), channel_id=1, source_target_pairs={{0,4},{4,0},{1,5},{5,1},{2,6},{6,2},{3,7},{7,3}} | collective-permute-start | bytes 19267592 | tf_op jit(solution)/shard_map/ppermute | solution.py:434
  204.8 245.4 %collective-permute-start.5 = (f32[8,128]{1,0:T(8,128)}, f32[8,128]{1,0:T(8,128)}, u32[]{:S(2)}, u32[]{:S(2)}) collective-permute-start(f32[8,128]{1,0:T(8,128)} %group_stats.9.refs_0_), channel_id=1, source_target_pairs={{0,4},{4,0},{1,5},{5,1},{2,6},{6,2},{3,7},{7,3}} | collective-permute-start | bytes 12296 | tf_op jit(solution)/shard_map/ppermute | solution.py:434
  340.4 439.6 %collective-permute-start.9 = (f32[128,12544]{1,0:T(8,128)}, f32[128,12544]{1,0:T(8,128)}, u32[]{:S(2)}, u32[]{:S(2)}) collective-permute-start(f32[128,12544]{1,0:T(8,128)} %shard_map.67.refs_0_), channel_id=1, source_target_pairs={{0,4},{4,0},{1,5},{5,1},{2,6},{6,2},{3,7},{7,3}} | collective-permute-start | bytes 19267592 | tf_op jit(solution)/shard_map/ppermute | solution.py:434
  533.8 330.0 %collective-permute-start.7 = (f32[128,12544]{1,0:T(8,128)}, f32[128,12544]{1,0:T(8,128)}, u32[]{:S(2)}, u32[]{:S(2)}) collective-permute-start(f32[128,12544]{1,0:T(8,128)} %shard_map.71.refs_0_), channel_id=1, source_target_pairs={{0,4},{4,0},{1,5},{5,1},{2,6},{6,2},{3,7},{7,3}} | collective-permute-start | bytes 19267592 | tf_op jit(solution)/shard_map/ppermute | solution.py:434
  534.9 189.9 %collective-permute-start.4 = (f32[8,128]{1,0:T(8,128)}, f32[8,128]{1,0:T(8,128)}, u32[]{:S(2)}, u32[]{:S(2)}) collective-permute-start(f32[8,128]{1,0:T(8,128)} %group_stats.10.refs_0_), channel_id=1, source_target_pairs={{0,4},{4,0},{1,5},{5,1},{2,6},{6,2},{3,7},{7,3}} | collective-permute-start | bytes 12296 | tf_op jit(solution)/shard_map/ppermute | solution.py:434
  535.8 272.6 %collective-permute-start.8 = (f32[8,128]{1,0:T(8,128)}, f32[8,128]{1,0:T(8,128)}, u32[]{:S(2)}, u32[]{:S(2)}) collective-permute-start(f32[8,128]{1,0:T(8,128)} %group_stats.11.refs_1_), channel_id=1, source_target_pairs={{0,4},{4,0},{1,5},{5,1},{2,6},{6,2},{3,7},{7,3}} | collective-permute-start | bytes 12296 | tf_op jit(solution)/shard_map/ppermute | solution.py:434
  807.5 334.0 %collective-permute-start.12 = (f32[128,12544]{1,0:T(8,128)}, f32[128,12544]{1,0:T(8,128)}, u32[]{:S(2)}, u32[]{:S(2)}) collective-permute-start(f32[128,12544]{1,0:T(8,128)} %shard_map.75.refs_0_), channel_id=1, source_target_pairs={{0,4},{4,0},{1,5},{5,1},{2,6},{6,2},{3,7},{7,3}} | collective-permute-start | bytes 19267592 | tf_op jit(solution)/shard_map/ppermute | solution.py:434
  890.2 309.6 %collective-permute-start.13 = (f32[128,12544]{1,0:T(8,128)}, f32[128,12544]{1,0:T(8,128)}, u32[]{:S(2)}, u32[]{:S(2)}) collective-permute-start(f32[128,12544]{1,0:T(8,128)} %shard_map.79.refs_0_), channel_id=1, source_target_pairs={{0,4},{4,0},{1,5},{5,1},{2,6},{6,2},{3,7},{7,3}} | collective-permute-start | bytes 19267592 | tf_op jit(solution)/shard_map/ppermute | solution.py:434
  891.3 194.9 %collective-permute-start.11 = (f32[8,128]{1,0:T(8,128)}, f32[8,128]{1,0:T(8,128)}, u32[]{:S(2)}, u32[]{:S(2)}) collective-permute-start(f32[8,128]{1,0:T(8,128)} %group_stats.12.refs_1_), channel_id=1, source_target_pairs={{0,4},{4,0},{1,5},{5,1},{2,6},{6,2},{3,7},{7,3}} | collective-permute-start | bytes 12296 | tf_op jit(solution)/shard_map/ppermute | solution.py:434
  892.3 276.4 %collective-permute-start.10 = (f32[8,128]{1,0:T(8,128)}, f32[8,128]{1,0:T(8,128)}, u32[]{:S(2)}, u32[]{:S(2)}) collective-permute-start(f32[8,128]{1,0:T(8,128)} %group_stats.13.refs_1_), channel_id=1, source_target_pairs={{0,4},{4,0},{1,5},{5,1},{2,6},{6,2},{3,7},{7,3}} | collective-permute-start | bytes 12296 | tf_op jit(solution)/shard_map/ppermute | solution.py:434
  1167.7 120.7 %collective-permute-start.17 = (f32[32,12544]{1,0:T(8,128)}, f32[32,12544]{1,0:T(8,128)}, u32[]{:S(2)}, u32[]{:S(2)}) collective-permute-start(f32[32,12544]{1,0:T(8,128)} %get-tuple-element.110.refs_0_), channel_id=1, source_target_pairs={{0,4},{4,0},{1,5},{5,1},{2,6},{6,2},{3,7},{7,3}} | collective-permute-start | bytes 4816904 | tf_op jit(solution)/shard_map/ppermute | solution.py:434
  1226.3 122.3 %collective-permute-start.14 = (f32[48,12544]{1,0:T(8,128)}, f32[48,12544]{1,0:T(8,128)}, u32[]{:S(2)}, u32[]{:S(2)}) collective-permute-start(f32[48,12544]{1,0:T(8,128)} %get-tuple-element.102), channel_id=1, source_target_pairs={{0,4},{4,0},{1,5},{5,1},{2,6},{6,2},{3,7},{7,3}} | collective-permute-start | bytes 7225352 | tf_op jit(solution)/shard_map/ppermute | solution.py:434
  1227.3 54.0 %collective-permute-start.16 = (f32[8,128]{1,0:T(8,128)}, f32[8,128]{1,0:T(8,128)}, u32[]{:S(2)}, u32[]{:S(2)}) collective-permute-start(f32[8,128]{1,0:T(8,128)} %group_stats.14.refs_1_), channel_id=1, source_target_pairs={{0,4},{4,0},{1,5},{5,1},{2,6},{6,2},{3,7},{7,3}} | collective-permute-start | bytes 12296 | tf_op jit(solution)/shard_map/ppermute | solution.py:434
  1303.7 84.7 %collective-permute-start.19 = (f32[32,12544]{1,0:T(8,128)}, f32[32,12544]{1,0:T(8,128)}, u32[]{:S(2)}, u32[]{:S(2)}) collective-permute-start(f32[32,12544]{1,0:T(8,128)} %get-tuple-element.116), channel_id=1, source_target_pairs={{0,4},{4,0},{1,5},{5,1},{2,6},{6,2},{3,7},{7,3}} | collective-permute-start | bytes 4816904 | tf_op jit(solution)/shard_map/ppermute | solution.py:434
  1304.8 36.7 %collective-permute-start.15 = (f32[8,128]{1,0:T(8,128)}, f32[8,128]{1,0:T(8,128)}, u32[]{:S(2)}, u32[]{:S(2)}) collective-permute-start(f32[8,128]{1,0:T(8,128)} %group_stats.15.refs_1_), channel_id=1, source_target_pairs={{0,4},{4,0},{1,5},{5,1},{2,6},{6,2},{3,7},{7,3}} | collective-permute-start | bytes 12296 | tf_op jit(solution)/shard_map/ppermute | solution.py:434
  1364.2 33.4 %collective-permute-start.18 = (f32[16,12544]{1,0:T(8,128)}, f32[16,12544]{1,0:T(8,128)}, u32[]{:S(2)}, u32[]{:S(2)}) collective-permute-start(f32[16,12544]{1,0:T(8,128)} %get-tuple-element.115), channel_id=1, source_target_pairs={{0,4},{4,0},{1,5},{5,1},{2,6},{6,2},{3,7},{7,3}} | collective-permute-start | bytes 2408456 | tf_op jit(solution)/shard_map/ppermute | solution.py:434
  1365.2 19.6 %collective-permute-start.20 = (f32[8,128]{1,0:T(8,128)}, f32[8,128]{1,0:T(8,128)}, u32[]{:S(2)}, u32[]{:S(2)}) collective-permute-start(f32[8,128]{1,0:T(8,128)} %group_stats.16.refs_1_), channel_id=1, source_target_pairs={{0,4},{4,0},{1,5},{5,1},{2,6},{6,2},{3,7},{7,3}} | collective-permute-start | bytes 12296 | tf_op jit(solution)/shard_map/ppermute | solution.py:434
  1366.2 26.4 %collective-permute-start.21 = (f32[8,128]{1,0:T(8,128)}, f32[8,128]{1,0:T(8,128)}, u32[]{:S(2)}, u32[]{:S(2)}) collective-permute-start(f32[8,128]{1,0:T(8,128)} %group_stats.17.refs_1_), channel_id=1, source_target_pairs={{0,4},{4,0},{1,5},{5,1},{2,6},{6,2},{3,7},{7,3}} | collective-permute-start | bytes 12296 | tf_op jit(solution)/shard_map/ppermute | solution.py:434

commit v5 on v4

--- a/solution.py
+++ b/solution.py
@@ -310,7 +310,7 @@
     out_ref[...] = pre_ref[...] * ab[:, 0:1] + ab[:, 1:2]
 
 
-def finish(pos, pre, st, mine, other, out, ct, all_rows, blk, at, row0, deps, vmem):
+def finish(pos, pre, st, mine, other, out, ct, all_rows, blk, at, row0, deps, keep):
     rows, cols = pre.shape
     sub = math.gcd(SUB, rows, at)
     tail = ([] if out is None else [out]) + list(deps)
@@ -318,18 +318,20 @@
     wide = pl.BlockSpec(mine.shape, lambda i, s: (0, 0, 0))
     return pl.pallas_call(
         functools.partial(final_kernel, blk=blk, at=at, rows=rows),
-        out_shape=[jax.ShapeDtypeStruct((all_rows, cols), jnp.float32), jax.ShapeDtypeStruct((8, 128), jnp.float32)],
+        out_shape=[jax.ShapeDtypeStruct((all_rows, cols), jnp.float32),
+                   (pltpu.VMEM if keep else jax.ShapeDtypeStruct)((8, 128), jnp.float32)],
         grid_spec=pltpu.PrefetchScalarGridSpec(
             num_scalar_prefetch=1,
             grid=(rows // sub,),
             in_specs=[pl.BlockSpec((sub, cols), lambda i, s: (i, 0)), small, wide, small, small]
             + [pl.BlockSpec(memory_space=pl.ANY)] * len(tail),
-            out_specs=[pl.BlockSpec((sub, cols), lambda i, s: (row0 // sub + i, 0)), small],
+            out_specs=[pl.BlockSpec((sub, cols), lambda i, s: (row0 // sub + i, 0)),
+                       pl.BlockSpec(memory_space=pltpu.VMEM) if keep else small],
             scratch_shapes=[pltpu.VMEM((128, 128), jnp.float32)],
         ),
         input_output_aliases={} if out is None else {6: 0},
         cost_estimate=pl.CostEstimate(flops=64 * rows * cols, bytes_accessed=rows * cols * 8, transcendentals=0),
-        compiler_params=pltpu.CompilerParams(dimension_semantics=("arbitrary",), vmem_limit_bytes=vmem),
+        compiler_params=pltpu.CompilerParams(dimension_semantics=("arbitrary",), vmem_limit_bytes=LAST_VMEM if keep else ALL_VMEM),
     )(pos, pre, st, mine, other, ct, *tail)
 
 
@@ -364,14 +366,14 @@
         functools.partial(last_kernel, blk=blk, at=at, rows=sum(rows), ends=tuple(ends)),
         grid=(lo,),
         out_shape=[jax.ShapeDtypeStruct(out.shape, jnp.float32), jax.ShapeDtypeStruct((8, 128), jnp.float32)],
-        in_specs=[whole, whole, small]
+        in_specs=[whole, whole, whole]
         + [whole] * len(pres)
         + [pl.BlockSpec(memory_space=pl.ANY)] * (1 + len(deps)),
         out_specs=[pl.BlockSpec((sub, cols), lambda i: (row0 // sub + i, 0)), small],
         input_output_aliases={3 + len(pres): 0},
         compiler_params=pltpu.CompilerParams(dimension_semantics=("arbitrary",), vmem_limit_bytes=LAST_VMEM),
         name="finish_last",
-    )(held(ab), held(at_tgt), ct, *map(held, pres), out, *deps)
+    )(held(ab), held(at_tgt), held(ct), *map(held, pres), out, *deps)
 
 
 def solution(mesh):
@@ -442,7 +444,9 @@
             nonlocal out, ct, tok
             b, at, _ = units[k]
             out, ct = finish(pos, pres[k], *stats[k], out, ct, rows_all, b, at, b * blk + at, (tok,),
-                             LAST_VMEM if k == nu - 3 else ALL_VMEM)
+                             k == nu - 3)
+            if k == nu - 3:
+                ct = held(ct)
             tok = ct
 
         prev = None

time: 1410 us -> 1410 us (level)
  no operation moved by 1% of the time
where the time goes in v5:
time: 1410 us
  waiting for transfers between devices  691 us (49%)
  Pallas kernels  620 us (44%)
  blocking collectives  66.4 us (5%)
  starting transfers between devices  23.2 us (2%)
    ppermute x22, waiting for transfers between devices, send(): return [lax.ppermute(a, 'hid', swap) for a in arrays]  691 us
    pallas_call x18, Pallas kernels, partial_products(): pl.pallas_call(functools.partial(mm_kernel, splits=splits, ksteps=ksteps)...  393 us
    pallas_call x11, Pallas kernels, local_prefix(): pl.pallas_call(functools.partial(local_kernel, npieces=len(recvs), has_pr...  148 us
    all_gather x9, blocking collectives, pipeline(): mine = lax.all_gather(st, 'vocab')  66.4 us
    pallas_call x9, Pallas kernels, finish(): pl.pallas_call(functools.partial(final_kernel, blk=blk, at=at, rows=rows)...  58.1 us
  transfers between devices with their start and end apart: 22, of which 8 were waited for; matrix products, arithmetic and copies ran while one was open for 0% of the time, Pallas kernels for 41%

profile of v5, /device:TPU:0, one launch (start us, length us, event | category | flops | bytes accessed | tf_op | source)
XLA Modules:
  0.0 1406.0 jit_solution(761908632486746618)
XLA Ops:
  13.8 18.7 %shard_map.61.refs_0_ = f32[128,8064]{1,0:T(8,128)} custom-call(s32[1]{0:T(128)} %bitcast.4.sel_ref, bf16[1024,2560]{1,0:T(8,128)(2,1)} %h_ref.35, bf16[2560,25088]{1,0:T(8,128)(2,1)} %w_ref.35, f32[128,3584]{1,0:T(8,128)} %shard_map.60.refs_0_), custom_call_target="tpu_custom_call" | custom-call | flops 5284823040 | bytes 45416448 | tf_op jit(solution)/shard_map/pallas_call | solution.py:39
  37.4 24.1 %shard_map.62.refs_0_ = f32[128,12544]{1,0:T(8,128)} custom-call(s32[1]{0:T(128)} %bitcast.4.sel_ref, bf16[1024,2560]{1,0:T(8,128)(2,1)} %h_ref.35, bf16[2560,25088]{1,0:T(8,128)(2,1)} %w_ref.35, f32[128,8064]{1,0:T(8,128)} %shard_map.61.refs_0_), custom_call_target="tpu_custom_call" | custom-call | flops 8220835840 | bytes 70647808 | tf_op jit(solution)/shard_map/pallas_call | solution.py:39
  62.1 24.1 %shard_map.63.refs_0_ = f32[128,12544]{1,0:T(8,128)} custom-call(s32[1]{0:T(128)} %bitcast.4.sel_ref, bf16[1024,2560]{1,0:T(8,128)(2,1)} %h_ref.35, bf16[2560,25088]{1,0:T(8,128)(2,1)} %w_ref.35, f32[128,12544]{1,0:T(8,128)} %shard_map.62.refs_0_), custom_call_target="tpu_custom_call" | custom-call | flops 8220835840 | bytes 70647808 | tf_op jit(solution)/shard_map/pallas_call | solution.py:39
  90.3 24.1 %shard_map.64.refs_0_.own_ref = f32[128,12544]{1,0:T(8,128)} custom-call(s32[1]{0:T(128)} %bitcast.2.sel_ref, bf16[1024,2560]{1,0:T(8,128)(2,1)} %h_ref.35, bf16[2560,25088]{1,0:T(8,128)(2,1)} %w_ref.35, f32[128,12544]{1,0:T(8,128)} %shard_map.63.refs_0_), custom_call_target="tpu_custom_call" | custom-call | flops 8220835840 | bytes 70647808 | tf_op jit(solution)/shard_map/pallas_call | solution.py:39
  114.4 24.2 %shard_map.65.refs_3_.own_ref = f32[128,12544]{1,0:T(8,128)} custom-call(s32[1]{0:T(128)} %bitcast.2.sel_ref, bf16[1024,2560]{1,0:T(8,128)(2,1)} %h_ref.35, bf16[2560,25088]{1,0:T(8,128)(2,1)} %w_ref.35, f32[128,12544]{1,0:T(8,128)} %shard_map.64.refs_0_.own_ref), custom_call_target="tpu_custom_call" | custom-call | flops 8220835840 | bytes 70647808 | tf_op jit(solution)/shard_map/pallas_call | solution.py:39
  138.5 36.3 %collective-permute-done.2.refs_1_ = f32[128,3584]{1,0:T(8,128)} collective-permute-done((f32[128,3584]{1,0:T(8,128)}, f32[128,3584]{1,0:T(8,128)}, u32[]{:S(2)}, u32[]{:S(2)}) %collective-permute-start.2) | collective-permute-done | bytes 1835040 | tf_op jit(solution)/shard_map/ppermute | solution.py:436
  174.8 18.7 %shard_map.66 = (f32[128,12544]{1,0:T(8,128)}, f32[8,128]{1,0:T(8,128)}) custom-call(f32[1024,1]{1,0:T(8,128)} %copy.35.temp_ref, s32[1024,1]{1,0:T(8,128)} %copy.36.tgt_ref, bf16[256,256]{1,0:T(8,128)(2,1)} %fusion.tri_ref, f32[128,12544]{1,0:T(8,128)} %shard_map.64.refs_0_.own_ref, f32[128,896]{1,0:T(8,128)} %collective-permute-done.1.refs_0_, ...), custom_call_target="tpu_custom_call" | custom-call | flops 2466250752 | bytes 19267584 | tf_op jit(solution)/shard_map/pallas_call | solution.py:157
  205.8 24.1 %shard_map.67.refs_0_ = f32[128,12544]{1,0:T(8,128)} custom-call(s32[1]{0:T(128)} %bitcast.4.sel_ref, bf16[1024,2560]{1,0:T(8,128)(2,1)} %h_ref.35, bf16[2560,25088]{1,0:T(8,128)(2,1)} %w_ref.35, f32[8,128]{1,0:T(8,128)} %group_stats.9.refs_0_), custom_call_target="tpu_custom_call" | custom-call | flops 8220835840 | bytes 70647808 | tf_op jit(solution)/shard_map/pallas_call | solution.py:39
  229.9 24.1 %shard_map.68.refs_1_.own_ref = f32[128,12544]{1,0:T(8,128)} custom-call(s32[1]{0:T(128)} %bitcast.2.sel_ref, bf16[1024,2560]{1,0:T(8,128)(2,1)} %h_ref.35, bf16[2560,25088]{1,0:T(8,128)(2,1)} %w_ref.35, f32[128,12544]{1,0:T(8,128)} %shard_map.67.refs_0_), custom_call_target="tpu_custom_call" | custom-call | flops 8220835840 | bytes 70647808 | tf_op jit(solution)/shard_map/pallas_call | solution.py:39
  254.0 58.5 %collective-permute-done.refs_0_ = f32[128,12544]{1,0:T(8,128)} collective-permute-done((f32[128,12544]{1,0:T(8,128)}, f32[128,12544]{1,0:T(8,128)}, u32[]{:S(2)}, u32[]{:S(2)}) %collective-permute-start) | collective-permute-done | bytes 6422560 | tf_op jit(solution)/shard_map/ppermute | solution.py:436
  341.4 108.8 %collective-permute-done.5.other_ref = f32[8,128]{1,0:T(8,128)} collective-permute-done((f32[8,128]{1,0:T(8,128)}, f32[8,128]{1,0:T(8,128)}, u32[]{:S(2)}, u32[]{:S(2)}) %collective-permute-start.5) | collective-permute-done | bytes 4128 | tf_op jit(solution)/shard_map/ppermute | solution.py:436
  457.9 24.1 %shard_map.71.refs_0_ = f32[128,12544]{1,0:T(8,128)} custom-call(s32[1]{0:T(128)} %bitcast.4.sel_ref, bf16[1024,2560]{1,0:T(8,128)(2,1)} %h_ref.35, bf16[2560,25088]{1,0:T(8,128)(2,1)} %w_ref.35, f32[8,128]{1,0:T(8,128)} %get-tuple-element.73.refs_0_.ctin_ref), custom_call_target="tpu_custom_call" | custom-call | flops 8220835840 | bytes 70647808 | tf_op jit(solution)/shard_map/pallas_call | solution.py:39
  482.0 24.1 %shard_map.72.refs_1_.own_ref = f32[128,12544]{1,0:T(8,128)} custom-call(s32[1]{0:T(128)} %bitcast.2.sel_ref, bf16[1024,2560]{1,0:T(8,128)(2,1)} %h_ref.35, bf16[2560,25088]{1,0:T(8,128)(2,1)} %w_ref.35, f32[128,12544]{1,0:T(8,128)} %shard_map.71.refs_0_), custom_call_target="tpu_custom_call" | custom-call | flops 8220835840 | bytes 70647808 | tf_op jit(solution)/shard_map/pallas_call | solution.py:39
  536.9 187.8 %collective-permute-done.4.other_ref = f32[8,128]{1,0:T(8,128)} collective-permute-done((f32[8,128]{1,0:T(8,128)}, f32[8,128]{1,0:T(8,128)}, u32[]{:S(2)}, u32[]{:S(2)}) %collective-permute-start.4) | collective-permute-done | bytes 4128 | tf_op jit(solution)/shard_map/ppermute | solution.py:436
  731.8 24.1 %shard_map.75.refs_0_ = f32[128,12544]{1,0:T(8,128)} custom-call(s32[1]{0:T(128)} %bitcast.4.sel_ref, bf16[1024,2560]{1,0:T(8,128)(2,1)} %h_ref.35, bf16[2560,25088]{1,0:T(8,128)(2,1)} %w_ref.35, f32[8,128]{1,0:T(8,128)} %get-tuple-element.78.refs_0_.ctin_ref), custom_call_target="tpu_custom_call" | custom-call | flops 8220835840 | bytes 70647808 | tf_op jit(solution)/shard_map/pallas_call | solution.py:39
  755.9 24.1 %shard_map.76.refs_1_.own_ref = f32[128,12544]{1,0:T(8,128)} custom-call(s32[1]{0:T(128)} %bitcast.2.sel_ref, bf16[1024,2560]{1,0:T(8,128)(2,1)} %h_ref.35, bf16[2560,25088]{1,0:T(8,128)(2,1)} %w_ref.35, f32[128,12544]{1,0:T(8,128)} %shard_map.75.refs_0_), custom_call_target="tpu_custom_call" | custom-call | flops 8220835840 | bytes 70647808 | tf_op jit(solution)/shard_map/pallas_call | solution.py:39
  815.6 24.1 %shard_map.79.refs_0_ = f32[128,12544]{1,0:T(8,128)} custom-call(s32[1]{0:T(128)} %bitcast.4.sel_ref, bf16[1024,2560]{1,0:T(8,128)(2,1)} %h_ref.35, bf16[2560,25088]{1,0:T(8,128)(2,1)} %w_ref.35, f32[8,128]{1,0:T(8,128)} %get-tuple-element.85.refs_0_.ctin_ref), custom_call_target="tpu_custom_call" | custom-call | flops 8220835840 | bytes 70647808 | tf_op jit(solution)/shard_map/pallas_call | solution.py:39
  839.7 24.1 %shard_map.80.refs_1_.own_ref = f32[128,12544]{1,0:T(8,128)} custom-call(s32[1]{0:T(128)} %bitcast.2.sel_ref, bf16[1024,2560]{1,0:T(8,128)(2,1)} %h_ref.35, bf16[2560,25088]{1,0:T(8,128)(2,1)} %w_ref.35, f32[128,12544]{1,0:T(8,128)} %shard_map.79.refs_0_), custom_call_target="tpu_custom_call" | custom-call | flops 8220835840 | bytes 70647808 | tf_op jit(solution)/shard_map/pallas_call | solution.py:39
  893.3 192.9 %collective-permute-done.11.other_ref = f32[8,128]{1,0:T(8,128)} collective-permute-done((f32[8,128]{1,0:T(8,128)}, f32[8,128]{1,0:T(8,128)}, u32[]{:S(2)}, u32[]{:S(2)}) %collective-permute-start.11) | collective-permute-done | bytes 4128 | tf_op jit(solution)/shard_map/ppermute | solution.py:436
  1093.2 24.1 %shard_map.83 = (f32[32,12544]{1,0:T(8,128)}, f32[48,12544]{1,0:T(8,128)}, f32[32,12544]{1,0:T(8,128)}, f32[16,12544]{1,0:T(8,128)}) custom-call(s32[1]{0:T(128)} %bitcast.4.sel_ref, bf16[1024,2560]{1,0:T(8,128)(2,1)} %h_ref.35, bf16[2560,25088]{1,0:T(8,128)(2,1)} %w_ref.35, f32[8,128]{1,0:T(8,128)} %get-tuple-element.91.refs_0_.ctin_ref), custom_call_target="tpu_custom_call" | custom-call | flops 8220835840 | bytes 70647808 | tf_op jit(solution)/shard_map/pallas_call | solution.py:39
  1117.3 24.1 %shard_map.84.refs_1_.own_ref = f32[128,12544]{1,0:T(8,128)} custom-call(s32[1]{0:T(128)} %bitcast.2.sel_ref, bf16[1024,2560]{1,0:T(8,128)(2,1)} %h_ref.35, bf16[2560,25088]{1,0:T(8,128)(2,1)} %w_ref.35, f32[32,12544]{1,0:T(8,128)} %get-tuple-element.110.refs_0_), custom_call_target="tpu_custom_call" | custom-call | flops 8220835840 | bytes 70647808 | tf_op jit(solution)/shard_map/pallas_call | solution.py:39
  1175.8 24.1 %shard_map.87.refs_1_.own_ref = f32[128,12544]{1,0:T(8,128)} custom-call(s32[1]{0:T(128)} %bitcast.2.sel_ref, bf16[1024,2560]{1,0:T(8,128)(2,1)} %h_ref.35, bf16[2560,25088]{1,0:T(8,128)(2,1)} %w_ref.35, f32[8,128]{1,0:T(8,128)} %get-tuple-element.97.refs_0_.ctin_ref), custom_call_target="tpu_custom_call" | custom-call | flops 8220835840 | bytes 70647808 | tf_op jit(solution)/shard_map/pallas_call | solution.py:39
  1228.3 52.9 %collective-permute-done.16.other_ref = f32[8,128]{1,0:T(8,128)} collective-permute-done((f32[8,128]{1,0:T(8,128)}, f32[8,128]{1,0:T(8,128)}, u32[]{:S(2)}, u32[]{:S(2)}) %collective-permute-start.16) | collective-permute-done | bytes 4128 | tf_op jit(solution)/shard_map/ppermute | solution.py:436
  1305.8 35.7 %collective-permute-done.15.other_ref = f32[8,128]{1,0:T(8,128)} collective-permute-done((f32[8,128]{1,0:T(8,128)}, f32[8,128]{1,0:T(8,128)}, u32[]{:S(2)}, u32[]{:S(2)}) %collective-permute-start.15) | collective-permute-done | bytes 4128 | tf_op jit(solution)/shard_map/ppermute | solution.py:436
  (83 shorter events, 333.4 us)
Async XLA Ops:
  32.5 142.3 %collective-permute-start.3 = (f32[128,8064]{1,0:T(8,128)}, f32[128,8064]{1,0:T(8,128)}, u32[]{:S(2)}, u32[]{:S(2)}) collective-permute-start(f32[128,8064]{1,0:T(8,128)} %shard_map.61.refs_0_), channel_id=1, source_target_pairs={{0,4},{4,0},{1,5},{5,1},{2,6},{6,2},{3,7},{7,3}} | collective-permute-start | bytes 12386312 | tf_op jit(solution)/shard_map/ppermute | solution.py:436
  35.4 103.2 %collective-permute-start.1 = (f32[128,896]{1,0:T(8,128)}, f32[128,896]{1,0:T(8,128)}, u32[]{:S(2)}, u32[]{:S(2)}) collective-permute-start(f32[128,896]{1,0:T(8,128)} %shard_map.59.refs_0_), channel_id=1, source_target_pairs={{0,4},{4,0},{1,5},{5,1},{2,6},{6,2},{3,7},{7,3}} | collective-permute-start | bytes 1376264 | tf_op jit(solution)/shard_map/ppermute | solution.py:436
  35.4 139.5 %collective-permute-start.2 = (f32[128,3584]{1,0:T(8,128)}, f32[128,3584]{1,0:T(8,128)}, u32[]{:S(2)}, u32[]{:S(2)}) collective-permute-start(f32[128,3584]{1,0:T(8,128)} %shard_map.60.refs_0_), channel_id=1, source_target_pairs={{0,4},{4,0},{1,5},{5,1},{2,6},{6,2},{3,7},{7,3}} | collective-permute-start | bytes 5505032 | tf_op jit(solution)/shard_map/ppermute | solution.py:436
  61.4 251.0 %collective-permute-start = (f32[128,12544]{1,0:T(8,128)}, f32[128,12544]{1,0:T(8,128)}, u32[]{:S(2)}, u32[]{:S(2)}) collective-permute-start(f32[128,12544]{1,0:T(8,128)} %shard_map.62.refs_0_), channel_id=1, source_target_pairs={{0,4},{4,0},{1,5},{5,1},{2,6},{6,2},{3,7},{7,3}} | collective-permute-start | bytes 19267592 | tf_op jit(solution)/shard_map/ppermute | solution.py:436
  203.8 302.3 %collective-permute-start.6 = (f32[128,12544]{1,0:T(8,128)}, f32[128,12544]{1,0:T(8,128)}, u32[]{:S(2)}, u32[]{:S(2)}) collective-permute-start(f32[128,12544]{1,0:T(8,128)} %shard_map.63.refs_0_), channel_id=1, source_target_pairs={{0,4},{4,0},{1,5},{5,1},{2,6},{6,2},{3,7},{7,3}} | collective-permute-start | bytes 19267592 | tf_op jit(solution)/shard_map/ppermute | solution.py:436
  204.8 245.4 %collective-permute-start.5 = (f32[8,128]{1,0:T(8,128)}, f32[8,128]{1,0:T(8,128)}, u32[]{:S(2)}, u32[]{:S(2)}) collective-permute-start(f32[8,128]{1,0:T(8,128)} %group_stats.9.refs_0_), channel_id=1, source_target_pairs={{0,4},{4,0},{1,5},{5,1},{2,6},{6,2},{3,7},{7,3}} | collective-permute-start | bytes 12296 | tf_op jit(solution)/shard_map/ppermute | solution.py:436
  340.4 439.6 %collective-permute-start.9 = (f32[128,12544]{1,0:T(8,128)}, f32[128,12544]{1,0:T(8,128)}, u32[]{:S(2)}, u32[]{:S(2)}) collective-permute-start(f32[128,12544]{1,0:T(8,128)} %shard_map.67.refs_0_), channel_id=1, source_target_pairs={{0,4},{4,0},{1,5},{5,1},{2,6},{6,2},{3,7},{7,3}} | collective-permute-start | bytes 19267592 | tf_op jit(solution)/shard_map/ppermute | solution.py:436
  533.8 330.0 %collective-permute-start.7 = (f32[128,12544]{1,0:T(8,128)}, f32[128,12544]{1,0:T(8,128)}, u32[]{:S(2)}, u32[]{:S(2)}) collective-permute-start(f32[128,12544]{1,0:T(8,128)} %shard_map.71.refs_0_), channel_id=1, source_target_pairs={{0,4},{4,0},{1,5},{5,1},{2,6},{6,2},{3,7},{7,3}} | collective-permute-start | bytes 19267592 | tf_op jit(solution)/shard_map/ppermute | solution.py:436
  534.9 189.9 %collective-permute-start.4 = (f32[8,128]{1,0:T(8,128)}, f32[8,128]{1,0:T(8,128)}, u32[]{:S(2)}, u32[]{:S(2)}) collective-permute-start(f32[8,128]{1,0:T(8,128)} %group_stats.10.refs_0_), channel_id=1, source_target_pairs={{0,4},{4,0},{1,5},{5,1},{2,6},{6,2},{3,7},{7,3}} | collective-permute-start | bytes 12296 | tf_op jit(solution)/shard_map/ppermute | solution.py:436
  535.8 272.6 %collective-permute-start.8 = (f32[8,128]{1,0:T(8,128)}, f32[8,128]{1,0:T(8,128)}, u32[]{:S(2)}, u32[]{:S(2)}) collective-permute-start(f32[8,128]{1,0:T(8,128)} %group_stats.11.refs_1_), channel_id=1, source_target_pairs={{0,4},{4,0},{1,5},{5,1},{2,6},{6,2},{3,7},{7,3}} | collective-permute-start | bytes 12296 | tf_op jit(solution)/shard_map/ppermute | solution.py:436
  807.5 334.0 %collective-permute-start.12 = (f32[128,12544]{1,0:T(8,128)}, f32[128,12544]{1,0:T(8,128)}, u32[]{:S(2)}, u32[]{:S(2)}) collective-permute-start(f32[128,12544]{1,0:T(8,128)} %shard_map.75.refs_0_), channel_id=1, source_target_pairs={{0,4},{4,0},{1,5},{5,1},{2,6},{6,2},{3,7},{7,3}} | collective-permute-start | bytes 19267592 | tf_op jit(solution)/shard_map/ppermute | solution.py:436
  890.2 309.6 %collective-permute-start.13 = (f32[128,12544]{1,0:T(8,128)}, f32[128,12544]{1,0:T(8,128)}, u32[]{:S(2)}, u32[]{:S(2)}) collective-permute-start(f32[128,12544]{1,0:T(8,128)} %shard_map.79.refs_0_), channel_id=1, source_target_pairs={{0,4},{4,0},{1,5},{5,1},{2,6},{6,2},{3,7},{7,3}} | collective-permute-start | bytes 19267592 | tf_op jit(solution)/shard_map/ppermute | solution.py:436
  891.3 194.9 %collective-permute-start.11 = (f32[8,128]{1,0:T(8,128)}, f32[8,128]{1,0:T(8,128)}, u32[]{:S(2)}, u32[]{:S(2)}) collective-permute-start(f32[8,128]{1,0:T(8,128)} %group_stats.12.refs_1_), channel_id=1, source_target_pairs={{0,4},{4,0},{1,5},{5,1},{2,6},{6,2},{3,7},{7,3}} | collective-permute-start | bytes 12296 | tf_op jit(solution)/shard_map/ppermute | solution.py:436
  892.3 276.4 %collective-permute-start.10 = (f32[8,128]{1,0:T(8,128)}, f32[8,128]{1,0:T(8,128)}, u32[]{:S(2)}, u32[]{:S(2)}) collective-permute-start(f32[8,128]{1,0:T(8,128)} %group_stats.13.refs_1_), channel_id=1, source_target_pairs={{0,4},{4,0},{1,5},{5,1},{2,6},{6,2},{3,7},{7,3}} | collective-permute-start | bytes 12296 | tf_op jit(solution)/shard_map/ppermute | solution.py:436
  1167.7 120.7 %collective-permute-start.17 = (f32[32,12544]{1,0:T(8,128)}, f32[32,12544]{1,0:T(8,128)}, u32[]{:S(2)}, u32[]{:S(2)}) collective-permute-start(f32[32,12544]{1,0:T(8,128)} %get-tuple-element.110.refs_0_), channel_id=1, source_target_pairs={{0,4},{4,0},{1,5},{5,1},{2,6},{6,2},{3,7},{7,3}} | collective-permute-start | bytes 4816904 | tf_op jit(solution)/shard_map/ppermute | solution.py:436
  1226.3 122.3 %collective-permute-start.14 = (f32[48,12544]{1,0:T(8,128)}, f32[48,12544]{1,0:T(8,128)}, u32[]{:S(2)}, u32[]{:S(2)}) collective-permute-start(f32[48,12544]{1,0:T(8,128)} %get-tuple-element.102), channel_id=1, source_target_pairs={{0,4},{4,0},{1,5},{5,1},{2,6},{6,2},{3,7},{7,3}} | collective-permute-start | bytes 7225352 | tf_op jit(solution)/shard_map/ppermute | solution.py:436
  1227.3 54.0 %collective-permute-start.16 = (f32[8,128]{1,0:T(8,128)}, f32[8,128]{1,0:T(8,128)}, u32[]{:S(2)}, u32[]{:S(2)}) collective-permute-start(f32[8,128]{1,0:T(8,128)} %group_stats.14.refs_1_), channel_id=1, source_target_pairs={{0,4},{4,0},{1,5},{5,1},{2,6},{6,2},{3,7},{7,3}} | collective-permute-start | bytes 12296 | tf_op jit(solution)/shard_map/ppermute | solution.py:436
  1303.7 84.7 %collective-permute-start.19 = (f32[32,12544]{1,0:T(8,128)}, f32[32,12544]{1,0:T(8,128)}, u32[]{:S(2)}, u32[]{:S(2)}) collective-permute-start(f32[32,12544]{1,0:T(8,128)} %get-tuple-element.116), channel_id=1, source_target_pairs={{0,4},{4,0},{1,5},{5,1},{2,6},{6,2},{3,7},{7,3}} | collective-permute-start | bytes 4816904 | tf_op jit(solution)/shard_map/ppermute | solution.py:436
  1304.8 36.7 %collective-permute-start.15 = (f32[8,128]{1,0:T(8,128)}, f32[8,128]{1,0:T(8,128)}, u32[]{:S(2)}, u32[]{:S(2)}) collective-permute-start(f32[8,128]{1,0:T(8,128)} %group_stats.15.refs_1_), channel_id=1, source_target_pairs={{0,4},{4,0},{1,5},{5,1},{2,6},{6,2},{3,7},{7,3}} | collective-permute-start | bytes 12296 | tf_op jit(solution)/shard_map/ppermute | solution.py:436
  1364.2 33.4 %collective-permute-start.18 = (f32[16,12544]{1,0:T(8,128)}, f32[16,12544]{1,0:T(8,128)}, u32[]{:S(2)}, u32[]{:S(2)}) collective-permute-start(f32[16,12544]{1,0:T(8,128)} %get-tuple-element.115), channel_id=1, source_target_pairs={{0,4},{4,0},{1,5},{5,1},{2,6},{6,2},{3,7},{7,3}} | collective-permute-start | bytes 2408456 | tf_op jit(solution)/shard_map/ppermute | solution.py:436
  1365.2 19.6 %collective-permute-start.20 = (f32[8,128]{1,0:T(8,128)}, f32[8,128]{1,0:T(8,128)}, u32[]{:S(2)}, u32[]{:S(2)}) collective-permute-start(f32[8,128]{1,0:T(8,128)} %group_stats.16.refs_1_), channel_id=1, source_target_pairs={{0,4},{4,0},{1,5},{5,1},{2,6},{6,2},{3,7},{7,3}} | collective-permute-start | bytes 12296 | tf_op jit(solution)/shard_map/ppermute | solution.py:436
  1366.2 26.4 %collective-permute-start.21 = (f32[8,128]{1,0:T(8,128)}, f32[8,128]{1,0:T(8,128)}, u32[]{:S(2)}, u32[]{:S(2)}) collective-permute-start(f32[8,128]{1,0:T(8,128)} %group_stats.17.refs_1_), channel_id=1, source_target_pairs={{0,4},{4,0},{1,5},{5,1},{2,6},{6,2},{3,7},{7,3}} | collective-permute-start | bytes 12296 | tf_op jit(solution)/shard_map/ppermute | solution.py:436
